TPU v7x, 8 devices: a whole 2x2x1 slice. The times are simulated.
8 devices in a mesh: dp: 1 (over z), yz: 2 (over y), x: 4 (over x, core).
Axes of the slice: x: 2, y: 2, z: 1, core: 2. Of those that a mesh axis runs over, the one named last changes fastest.
Arguments:
- x_in: bfloat16 [128, 4096], P('dp', ('x', 'yz'))
- ln_gain: bfloat16 [4096], P(('x', 'yz'))
- w_qkv: bfloat16 [4096, 4608], P('x', 'yz')
- w_gate: bfloat16 [4096, 16384], P('x', 'yz')
- w_up: bfloat16 [4096, 16384], P('x', 'yz')
- w_attn_out: bfloat16 [4096, 4096], P('yz', 'x')
- w_mlp_out: bfloat16 [16384, 4096], P('yz', 'x')
- k_cache: bfloat16 [128, 4096, 256], P(('dp', 'x', 'yz'))
- v_cache: bfloat16 [128, 4096, 256], P(('dp', 'x', 'yz'))
- ctx_len: int32 [128], P(('dp', 'x', 'yz'))
Outputs:
- output 1: bfloat16 [128, 4096], P('dp', ('x', 'yz'))
- output 2: bfloat16 [128, 4096, 256], P(('dp', 'x', 'yz'))
- output 3: bfloat16 [128, 4096, 256], P(('dp', 'x', 'yz'))
All inputs are finite; a program needn't handle non-finite values.
Results may differ from a plain program's by a relative error of at most 0.00714708.
Values are sent between devices in bfloat16 or wider.
A program may use at most 1 GiB of HBM per device.

v0:
```python
import jax
import jax.numpy as jnp
from jax import lax
from jax.sharding import PartitionSpec as P


def apply_rope(vecs, positions):
    half_dim = vecs.shape[-1] // 2
    inv_freq = 10000.0 ** (-jnp.arange(half_dim, dtype=jnp.float32) / half_dim)
    angles = positions.astype(jnp.float32)[..., None] * inv_freq
    cos_t = jnp.cos(angles)
    sin_t = jnp.sin(angles)
    first_half = vecs[..., :half_dim]
    second_half = vecs[..., half_dim:]
    return jnp.concatenate([first_half * cos_t - second_half * sin_t, second_half * cos_t + first_half * sin_t], axis=-1)


def attend_local(q_rot, k_all, v_all, ctx_len):
    head_dim = q_rot.shape[-1]
    positions = jnp.arange(k_all.shape[1])
    scores = jnp.einsum("bhd,btd->bht", q_rot, k_all, preferred_element_type=jnp.float32) * head_dim ** -0.5
    visible = (positions[None, :] <= ctx_len[:, None])[:, None, :]
    scores = jnp.where(visible, scores, -1e30)
    attn_probs = jax.nn.softmax(scores, axis=-1).astype(jnp.bfloat16)
    return jnp.einsum("bht,btd->bhd", attn_probs, v_all, preferred_element_type=jnp.float32).astype(jnp.bfloat16)


def solution(mesh):
    x_size = mesh.shape["x"]
    yz_size = mesh.shape["yz"]
    both_axes = ("x", "yz")
    row_spec = P("dp", both_axes)
    in_w_spec = P("x", "yz")
    out_w_spec = P("yz", "x")
    cache_spec = P(("dp", "x", "yz"), None, None)
    len_spec = P(("dp", "x", "yz"))

    def local_layer(x_loc, gain_loc, wqkv_loc, wgate_loc, wup_loc, wao_loc, wmo_loc, kc_loc, vc_loc, len_loc):
        d_model = x_loc.shape[1] * x_size * yz_size
        head_dim = kc_loc.shape[2]
        dev_rows = kc_loc.shape[0]
        attn_cols = wao_loc.shape[0] * yz_size
        num_heads = attn_cols // head_dim
        x_f32 = x_loc.astype(jnp.float32)
        row_stats = jnp.stack([jnp.sum(x_f32, axis=1), jnp.sum(x_f32 * x_f32, axis=1)], axis=1)
        row_stats = lax.psum(row_stats, both_axes)
        row_mean = row_stats[:, 0:1] / d_model
        row_var = row_stats[:, 1:2] / d_model - row_mean * row_mean
        normed = ((x_f32 - row_mean) * lax.rsqrt(row_var + 1e-6) * gain_loc.astype(jnp.float32)).astype(jnp.bfloat16)
        normed_rows = lax.all_gather(normed, "yz", axis=1, tiled=True)
        qkv_part = jnp.dot(normed_rows, wqkv_loc, preferred_element_type=jnp.float32)
        gate_part = jnp.dot(normed_rows, wgate_loc, preferred_element_type=jnp.float32)
        up_part = jnp.dot(normed_rows, wup_loc, preferred_element_type=jnp.float32)
        qkv_rows = lax.psum_scatter(qkv_part, "x", scatter_dimension=0, tiled=True).astype(jnp.bfloat16)
        gate_rows = lax.psum_scatter(gate_part, "x", scatter_dimension=0, tiled=True).astype(jnp.bfloat16)
        up_rows = lax.psum_scatter(up_part, "x", scatter_dimension=0, tiled=True).astype(jnp.bfloat16)
        mlp_rows = (jax.nn.silu(gate_rows.astype(jnp.float32)) * up_rows.astype(jnp.float32)).astype(jnp.bfloat16)
        qkv_dev = lax.all_to_all(qkv_rows, "yz", 0, 1, tiled=True)
        q_heads = qkv_dev[:, :attn_cols].reshape(dev_rows, num_heads, head_dim)
        k_new = qkv_dev[:, attn_cols:attn_cols + head_dim]
        v_new = qkv_dev[:, attn_cols + head_dim:]
        q_rot = apply_rope(q_heads.astype(jnp.float32), len_loc[:, None]).astype(jnp.bfloat16)
        k_rot = apply_rope(k_new.astype(jnp.float32), len_loc).astype(jnp.bfloat16)
        new_slot = (jnp.arange(kc_loc.shape[1])[None, :] == len_loc[:, None])[:, :, None]
        k_all = jnp.where(new_slot, k_rot[:, None, :], kc_loc)
        v_all = jnp.where(new_slot, v_new[:, None, :], vc_loc)
        attn_dev = attend_local(q_rot, k_all, v_all, len_loc).reshape(dev_rows, attn_cols)
        attn_rows = lax.all_to_all(attn_dev, "yz", 1, 0, tiled=True)
        attn_full = lax.all_gather(attn_rows, "x", axis=0, tiled=True)
        mlp_full = lax.all_gather(mlp_rows, "x", axis=0, tiled=True)
        z_part = jnp.dot(attn_full, wao_loc, preferred_element_type=jnp.float32) + jnp.dot(mlp_full, wmo_loc, preferred_element_type=jnp.float32)
        z_loc = lax.psum_scatter(z_part, "yz", scatter_dimension=1, tiled=True)
        y_loc = (x_f32 + z_loc).astype(jnp.bfloat16)
        return y_loc, k_all, v_all

    in_specs = (row_spec, P(both_axes), in_w_spec, in_w_spec, in_w_spec, out_w_spec, out_w_spec, cache_spec, cache_spec, len_spec)
    out_specs = (row_spec, cache_spec, cache_spec)
    return jax.shard_map(local_layer, mesh=mesh, in_specs=in_specs, out_specs=out_specs, check_vma=False)
```

profile of v0, /device:TPU:0, one launch (start us, length us, event | category | flops | bytes accessed | tf_op | source)
XLA Modules:
  0.0 229.8 jit_solution(18002998257350613124)
XLA Ops:
  7.2 1.0 convert_reduce_fusion
  8.2 25.1 %psum.7 = f32[128,2]{0,1:T(2,128)S(1)} all-reduce(f32[128,2]{0,1:T(2,128)S(1)} %pad_maximum_fusion.1), channel_id=1, replica_groups=mesh['dp'=1,'yz'=2,'x'=4] {'x','yz'}, use_global_device_ids=true, to_apply=%region_2.0 | all-reduce | flops 256 | bytes 2048 | tf_op jit(solution)/shard_map/psum | solution.py:46
  33.3 0.7 convert_element_type.57
  34.0 1.0 fusion.15
  35.0 5.9 %all_gather.9 = bf16[128,1024]{1,0:T(8,128)(2,1)S(1)} all-gather(bf16[128,512]{1,0:T(8,128)(2,1)S(1)} %fusion.15), channel_id=1, replica_groups=mesh['dp'=1,'yz'=2,'x'=4] {'yz'}, dimensions={1}, use_global_device_ids=true | all-gather | bytes 393216 | tf_op jit(solution)/shard_map/all_gather | solution.py:50
  40.9 4.1 %fusion.24 = f32[128,2304]{1,0:T(8,128)} fusion(bf16[128,1024]{1,0:T(8,128)(2,1)S(1)} %all_gather.9, bf16[1024,2304]{1,0:T(8,128)(2,1)} %param.12), kind=kOutput, calls=%fused_computation.50 | convolution fusion | flops 603979776 | bytes 6160384 | tf_op jit(solution)/shard_map/dot_general | solution.py:51
  45.1 0.0 reduce-scatter.9.cloned.1.call-start
  45.1 10.1 %fusion.26 = f32[128,8192]{1,0:T(8,128)} fusion(bf16[128,1024]{1,0:T(8,128)(2,1)S(1)} %all_gather.9, bf16[1024,8192]{1,0:T(8,128)(2,1)} %param.14), kind=kOutput, calls=%fused_computation.52 | convolution fusion | flops 2147483648 | bytes 21233664 | tf_op jit(solution)/shard_map/dot_general | solution.py:53
  55.2 0.0 reduce-scatter.7.cloned.1.call-start
  55.3 10.1 %fusion.25 = f32[128,8192]{1,0:T(8,128)} fusion(bf16[128,1024]{1,0:T(8,128)(2,1)S(1)} %all_gather.9, bf16[1024,8192]{1,0:T(8,128)(2,1)} %param.13), kind=kOutput, calls=%fused_computation.51 | convolution fusion | flops 2147483648 | bytes 21233664 | tf_op jit(solution)/shard_map/dot_general | solution.py:52
  65.4 0.6 copy-done.3
  66.0 0.1 iota_compare_fusion.1
  66.2 1.6 convert_element_type.59
  67.8 3.4 %all-to-all-start = ((bf16[2,16,2304]{2,1,0:T(8,128)(2,1)}), bf16[2,16,2304]{2,1,0:T(8,128)(2,1)S(1)}, u32[]{:S(2)}, u32[]{:S(2)}) async-start(bf16[2,16,2304]{2,1,0:T(8,128)(2,1)} %bitcast.4), calls=%async_computation.1 | async-start | bytes 294912 | tf_op jit(solution)/shard_map/all_to_all | solution.py:58
  71.3 0.0 all-gather.2.cloned.1.call-start
  71.3 4.3 %all-to-all-done = bf16[2,16,2304]{2,1,0:T(8,128)(2,1)S(1)} async-done(((bf16[2,16,2304]{2,1,0:T(8,128)(2,1)}), bf16[2,16,2304]{2,1,0:T(8,128)(2,1)S(1)}, u32[]{:S(2)}, u32[]{:S(2)}) %all-to-all-start) | async-done | bytes 147488 | tf_op jit(solution)/shard_map/all_to_all | solution.py:58
  75.6 0.1 copy.18
  75.7 0.1 multiply_cosine_fusion
  75.9 44.8 %broadcast_select_fusion.1 = (bf16[16,4096,256]{2,1,0:T(8,128)(2,1)}, bf16[16,4096,256]{2,1,0:T(8,128)(2,1)}) fusion(bf16[16,4096,256]{2,1,0:T(8,128)(2,1)} %param.17, pred[16,4096]{1,0:T(8,128)(4,1)S(1)} %get-tuple-element.20, bf16[16,256]{1,0:T(8,128)(2,1)S(1)} %pad_maximum_fusion, bf16[16,4096,256]{2,1,0:T(8,128)(2,1)} %param.18, ...), kind=kLoop, calls=%fused_computation.2 | loop fusion | flops 33554432 | bytes 134299648 | tf_op jit(solution)/shard_map/jit(_where)/select_n | solution.py:65
  120.7 26.7 %reduce-scatter.7.cloned.1.call-done = f32[32,8192]{1,0:T(8,128)} async-done(((f32[128,8192]{1,0:T(8,128)}), f32[32,8192]{1,0:T(8,128)}) %reduce-scatter.7.cloned.1.call-update) | async-done | bytes 1048592 | tf_op jit(solution)/shard_map/reduce_scatter | solution.py:55
  147.4 2.6 %fusion.11 = bf16[32,8192]{1,0:T(8,128)(2,1)} fusion(f32[32,8192]{1,0:T(8,128)} %reduce-scatter.9.cloned.1.call-done, f32[32,8192]{1,0:T(8,128)} %reduce-scatter.7.cloned.1.call-done), kind=kLoop, calls=%fused_computation.18 | loop fusion | flops 2621440 | bytes 2621440 | tf_op jit(solution)/shard_map/convert_element_type | solution.py:57
  150.1 0.2 reduce-scatter.11.cloned.1.call-start
  150.3 14.5 %fusion.3 = f32[16,16,4096]{2,1,0:T(8,128)S(1)} fusion(bf16[16,4096,256]{2,1,0:T(8,128)(2,1)} %get-tuple-element.9, pred[16,4096]{1,0:T(8,128)(4,1)S(1)} %get-tuple-element.19, bf16[16,16,128]{2,1,0:T(8,128)(2,1)S(1)} %get-tuple-element.6, bf16[16,16,128]{2,1,0:T(8,128)(2,1)S(1)} %get-tuple-element.5), kind=kOutput, calls=%fused_computation.6 | convolution fusion | flops 539230208 | bytes 37945344 | tf_op jit(solution)/shard_map/bhd,btd->bht/dot_general | solution.py:21
  164.9 1.9 copy-done
  166.8 0.8 fusion.23
  167.6 15.5 %fusion.6 = bf16[16,16,256]{2,1,0:T(8,128)(2,1)S(1)} fusion(bf16[16,4096,256]{2,1,0:T(8,128)(2,1)} %get-tuple-element.10, f32[16,16]{1,0:T(8,128)S(1)} %fusion.23, f32[16,16,4096]{2,1,0:T(8,128)} %copy-done), kind=kOutput, calls=%fused_computation.13 | convolution fusion | flops 540086528 | bytes 37880832 | tf_op jit(solution)/shard_map/bht,btd->bhd/dot_general | solution.py:25
  183.1 7.0 %all_to_all.38 = bf16[16,2,2048]{2,0,1:T(8,128)(2,1)S(1)} all-to-all(bf16[16,2,2048]{2,0,1:T(8,128)(2,1)S(1)} %copy.16), channel_id=1, replica_groups=mesh['dp'=1,'yz'=2,'x'=4] {'yz'}, dimensions={1} | all-to-all | bytes 262144 | tf_op jit(solution)/shard_map/all_to_all | solution.py:68
  190.2 9.1 %all_gather.10 = bf16[128,2048]{1,0:T(8,128)(2,1)S(1)} all-gather(bf16[32,2048]{1,0:T(8,128)(2,1)S(1)} %bitcast.34), channel_id=1, replica_groups=mesh['dp'=1,'yz'=2,'x'=4] {'x'}, dimensions={0}, use_global_device_ids=true | all-gather | bytes 655360 | tf_op jit(solution)/shard_map/all_gather | solution.py:69
  199.2 8.9 %fusion.27 = f32[128,1024]{1,0:T(8,128)S(1)} fusion(bf16[128,8192]{1,0:T(8,128)(2,1)} %all-gather.2.cloned.1.call-done, bf16[8192,1024]{1,0:T(8,128)(2,1)} %param.16), kind=kOutput, calls=%fused_computation.53 | convolution fusion | flops 2147483648 | bytes 19398656 | tf_op jit(solution)/shard_map/dot_general | solution.py:71
  208.2 1.5 convolution_add_fusion
  209.7 11.9 %reduce-scatter.11.cloned.1.call-done = f32[128,512]{1,0:T(8,128)} async-done(((f32[128,1024]{1,0:T(8,128)}), f32[128,512]{1,0:T(8,128)}) %reduce-scatter.11.cloned.1.call-update) | async-done | bytes 262160 | tf_op jit(solution)/shard_map/reduce_scatter | solution.py:72
  221.6 1.6 fusion.16
  (26 shorter events, 0.4 us)
Async XLA Ops:
  7.2 59.0 %reduce-scatter.5.cloned.1.call-start = ((), (), s32[]{:S(2)}) async-start(), calls=%async_computation.6 | async-start | bytes 1474560 | tf_op jit(solution)/shard_map/reduce_scatter | solution.py:54
  45.1 75.6 %reduce-scatter.9.cloned.1.call-start = ((), (), s32[]{:S(2)}) async-start(), calls=%async_computation.8 | async-start | bytes 5242880 | tf_op jit(solution)/shard_map/reduce_scatter | solution.py:56
  55.2 92.2 %reduce-scatter.7.cloned.1.call-start = ((), (), s32[]{:S(2)}) async-start(), calls=%async_computation.7 | async-start | bytes 5242880 | tf_op jit(solution)/shard_map/reduce_scatter | solution.py:55
  65.4 0.7 copy-start.3
  67.8 7.8 %all-to-all-start = ((bf16[2,16,2304]{2,1,0:T(8,128)(2,1)}), bf16[2,16,2304]{2,1,0:T(8,128)(2,1)S(1)}, u32[]{:S(2)}, u32[]{:S(2)}) async-start(bf16[2,16,2304]{2,1,0:T(8,128)(2,1)} %bitcast.4), calls=%async_computation.1 | async-start | bytes 294912 | tf_op jit(solution)/shard_map/all_to_all | solution.py:58
  71.3 128.0 %all-gather.2.cloned.1.call-start = ((), (), s32[]{:S(2)}) async-start(), calls=%async_computation.9 | async-start | bytes 2621440 | tf_op jit(solution)/shard_map/all_gather | solution.py:70
  150.1 71.5 %reduce-scatter.11.cloned.1.call-start = ((), (), s32[]{:S(2)}) async-start(), calls=%async_computation.10 | async-start | bytes 786432 | tf_op jit(solution)/shard_map/reduce_scatter | solution.py:72
  164.9 1.9 copy-start
  199.2 8.9 %copy-start.1 = (bf16[2048,1024]{1,0:T(8,128)(2,1)S(1)}, bf16[2048,1024]{1,0:T(8,128)(2,1)}, u32[]{:S(2)}) copy-start(bf16[2048,1024]{1,0:T(8,128)(2,1)} %param.15) | copy-start | bytes 12582916
  208.1 13.5 %copy-start.2 = (bf16[128,512]{1,0:T(8,128)(2,1)S(1)}, bf16[128,512]{1,0:T(8,128)(2,1)}, u32[]{:S(2)}) copy-start(bf16[128,512]{1,0:T(8,128)(2,1)} %param.10) | copy-start | bytes 393220
Sparse Core Ops, SparseCore 0:
  45.2 20.5 reduce-scatter.4
  68.3 38.2 reduce-scatter.8
  109.1 38.2 reduce-scatter.6
  150.2 19.5 all-gather.1
  209.8 11.7 reduce-scatter.10
where the time goes:
time: 230 us
  matrix products  64.7 us (28%)
  other arithmetic  54.5 us (24%)
  blocking collectives  47.1 us (20%)
  waiting for transfers between devices  43 us (19%)
  between operations  13.9 us (6%)
  starting transfers between devices  3.81 us (2%)
  local copies, waits for them, and re-layouts  2.76 us (1%)
    select_n x1, other arithmetic, local_layer(): k_all = jnp.where(new_slot, k_rot[:, None, :], kc_loc)  44.8 us
    reduce_scatter x1, waiting for transfers between devices, local_layer(): lax.psum_scatter(gate_part, 'x', scatter_dimension=0, tiled=True)  26.7 us
    psum x1, blocking collectives, local_layer(): row_stats = lax.psum(row_stats, both_axes)  25.1 us
    dot_general x1, matrix products, attend_local(): jnp.einsum('bht,btd->bhd', attn_probs, v_all, preferred_element_type=jnp....  15.5 us
    dot_general x1, matrix products, attend_local(): jnp.einsum('bhd,btd->bht', q_rot, k_all, preferred_element_type=jnp.float32)  14.5 us
    reduce_scatter x1, waiting for transfers between devices, local_layer(): z_loc = lax.psum_scatter(z_part, 'yz', scatter_dimension=1, tiled=True)  11.9 us
    dot_general x1, matrix products, local_layer(): jnp.dot(normed_rows, wgate_loc, preferred_element_type=jnp.float32)  10.1 us
    dot_general x1, matrix products, local_layer(): up_part = jnp.dot(normed_rows, wup_loc, preferred_element_type=jnp.float32)  10.1 us
  transfers between devices with their start and end apart: 6, of which 3 were waited for; matrix products, arithmetic and copies ran while one was open for 43% of the time, Pallas kernels for 0%

commit v1 on v0

v1 whole, which is shorter than its diff:
```python
import functools

import jax
import jax.numpy as jnp
from jax import lax
from jax.experimental import pallas as pl
from jax.experimental.pallas import tpu as pltpu
from jax.sharding import PartitionSpec as P

MESH = pl.DeviceIdType.MESH
VMEM_LIMIT = 67043328
TILE = 512
NT = 8
QC = 768
NQ = 3

f32 = jnp.float32
bf16 = jnp.bfloat16


def local_copy(src, dst, sem):
    return pltpu.make_async_copy(src, dst, sem)


def remote_copy(src, dst, ssem, rsem, dev):
    return pltpu.make_async_remote_copy(src, dst, ssem, rsem, device_id=dev, device_id_type=MESH)


def in_proj_kernel(x_ref, g_ref, wq_ref, wg_ref, wu_ref, qkv_ref, s_ref, d_ref,
                   wqv, wv, xr, gr, st, stx, h, qp, qr, qxs, qxr, qf, qyr, sbuf, rbuf, obuf,
                   wqsem, wsem, xs_sem, xr_sem, gs_sem, gr_sem, sts_sem, str_sem,
                   qds_sem, qdr_sem, qxs_sem, qxr_sem, qys_sem, qyr_sem, ds_sem, dr_sem, out_sem):
    d_model = 4096
    x = lax.axis_index("x")
    yz = lax.axis_index("yz")
    core = lax.rem(x, 2)
    x_core = x + 1 - 2 * core
    x_chip = lax.rem(x + 2, 4)
    x_diag = x_chip + 1 - 2 * core
    me = 2 * x + yz
    partner = {"x": x_core}
    xpeer = {"x": x_chip}
    ypeer = {"yz": 1 - yz}

    def wq_copy(j):
        return local_copy(wq_ref.at[:, pl.ds(QC * j, QC)], wqv.at[j], wqsem.at[j])

    quarters = (x_diag, x_chip, x_core, x)

    def w_copy(w_hbm, quarter, t, slot):
        cols = pl.multiple_of(quarter * 2048 + t * TILE, TILE)
        return local_copy(w_hbm.at[:, pl.ds(cols, TILE)], wv.at[slot], wsem.at[slot])

    for j in range(NQ):
        wq_copy(j).start()
    for ph in range(4):
        for t in range(4):
            w_copy(wg_ref, quarters[ph], t, ph * NT + 2 * t).start()
            w_copy(wu_ref, quarters[ph], t, ph * NT + 2 * t + 1).start()

    def w_wait(slot):
        local_copy(wg_ref.at[:, pl.ds(0, TILE)], wv.at[slot], wsem.at[slot]).wait()

    xf = x_ref[...].astype(f32)
    s1 = jnp.sum(xf, axis=1, keepdims=True)
    s2 = jnp.sum(xf * xf, axis=1, keepdims=True)
    lane = lax.broadcasted_iota(jnp.int32, (128, 128), 1)
    stat = jnp.where(lane == 0, s1, s2).T
    st[me] = stat[0:8]

    barrier = pltpu.get_barrier_semaphore()
    others = []
    for dx in range(4):
        for dy in range(2):
            if dx or dy:
                others.append((lax.rem(x + dx, 4), lax.rem(yz + dy, 2)))
    for ox, oy in others:
        pl.semaphore_signal(barrier, inc=1, device_id={"x": ox, "yz": oy}, device_id_type=MESH)
    pl.semaphore_wait(barrier, 7)

    for n, (ox, oy) in enumerate(others):
        remote_copy(st.at[me], stx.at[me], sts_sem.at[n], str_sem.at[me], {"x": ox, "yz": oy}).start()
    x_send = remote_copy(x_ref, xr, xs_sem, xr_sem, ypeer)
    g_send = remote_copy(g_ref, gr, gs_sem, gr_sem, ypeer)
    x_send.start()
    g_send.start()
    stx[me] = st[me]
    for n, (ox, oy) in enumerate(others):
        src = 2 * ox + oy
        remote_copy(st.at[me], stx.at[src], sts_sem.at[n], str_sem.at[src], {"x": ox, "yz": oy}).wait()
    tot = jnp.sum(stx[...], axis=0)
    tot = jnp.concatenate([tot, jnp.zeros((120, 128), f32)], axis=0).T
    mean = tot[:, 0:1] / d_model
    var = tot[:, 1:2] / d_model - mean * mean
    rstd = lax.rsqrt(var + 1e-6)
    own_cols = pl.multiple_of(yz * 512, 512)
    peer_cols = pl.multiple_of((1 - yz) * 512, 512)
    h[:, pl.ds(own_cols, 512)] = ((xf - mean) * rstd * g_ref[0:1, :]).astype(bf16)
    x_send.wait()
    g_send.wait()
    h[:, pl.ds(peer_cols, 512)] = ((xr[...].astype(f32) - mean) * rstd * gr[0:1, :]).astype(bf16)

    def q_compute(j):
        wq_copy(j).wait()
        part = jnp.dot(h[...], wqv[j], preferred_element_type=f32)
        qp[j] = part.reshape(4, 32, QC)

    def q_pair(j, k):
        block = (x_diag, x_core)[k]
        return remote_copy(qp.at[j, block], qr.at[j, k], qds_sem.at[j, k], qdr_sem.at[j, k], partner)

    def q_pair_start(j):
        q_pair(j, 0).start()
        q_pair(j, 1).start()

    def q_chip(j):
        return remote_copy(qxs.at[j], qxr.at[j], qxs_sem.at[j], qxr_sem.at[j], xpeer)

    def q_sum(j):
        q_pair(j, 0).wait()
        qxs[j] = qp[j, x_chip] + qr[j, 0]

    def tile(slot):
        w_wait(slot)
        return jnp.dot(h[...], wv[slot], preferred_element_type=f32)

    def d_copy(i):
        return remote_copy(sbuf.at[i], rbuf.at[i], ds_sem.at[i], dr_sem.at[i], partner)

    def s_out(i):
        return local_copy(obuf.at[i], s_ref.at[i], out_sem.at[i])

    def d_out(i):
        return local_copy(obuf.at[NT + i], d_ref.at[i], out_sem.at[NT + i])

    q_compute(0)
    q_compute(1)
    q_pair_start(0)
    q_compute(2)
    q_pair_start(1)

    after = {
        0: lambda: q_pair_start(2),
        1: lambda: q_sum(0),
        2: lambda: (q_chip(0).start(), q_sum(1)),
        3: lambda: (q_chip(1).start(), q_sum(2)),
        4: lambda: q_chip(2).start(),
    }
    for i in range(NT):
        sbuf[i] = tile(i)
        if i:
            d_copy(i - 1).start()
        if i in after:
            after[i]()

    for i in range(NT):
        part = tile(NT + i)
        if i == 0:
            d_copy(NT - 1).start()
        d_copy(i).wait()
        obuf[i] = part + rbuf[i]
        if i:
            s_out(i - 1).start()

    def send_body(i, _):
        sbuf[NT + i] = tile(2 * NT + i)

        @pl.when(i == 0)
        def _():
            s_out(NT - 1).start()

        @pl.when(i > 0)
        def _():
            d_copy(NT + i - 1).start()
        return 0

    lax.fori_loop(0, NT, send_body, 0)

    def keep_body(i, _):
        part = tile(3 * NT + i)

        @pl.when(i == 0)
        def _():
            d_copy(2 * NT - 1).start()
        d_copy(NT + i).wait()
        obuf[NT + i] = part + rbuf[NT + i]

        @pl.when(i > 0)
        def _():
            d_out(i - 1).start()
        return 0

    lax.fori_loop(0, NT, keep_body, 0)

    own_rows = pl.multiple_of(yz * 16, 16)
    peer_rows = pl.multiple_of((1 - yz) * 16, 16)

    def q_y(j):
        return remote_copy(qf.at[j, pl.ds(peer_rows, 16)], qyr.at[j], qys_sem.at[j], qyr_sem.at[j], ypeer)

    for j in range(NQ):
        q_pair(j, 1).wait()
        if j == 0:
            d_out(NT - 1).start()
        q_chip(j).wait()
        qf[j] = (qp[j, x] + qr[j, 1] + qxr[j]).astype(bf16)
        if j:
            q_y(j - 1).start()
    for j in range(NQ):
        qkv_ref[yz, :, pl.ds(QC * j, QC)] = qf[j, pl.ds(own_rows, 16)]
    q_y(NQ - 1).start()
    for j in range(NQ):
        q_y(j).wait()
        qkv_ref[1 - yz, :, pl.ds(QC * j, QC)] = qyr[j]
    for i in range(NT):
        s_out(i).wait()
        d_out(i).wait()


def in_proj(x_loc, gain, wq, wg, wu):
    anyspec = pl.BlockSpec(memory_space=pltpu.HBM)
    vspec = pl.BlockSpec(memory_space=pltpu.VMEM)
    dma = pltpu.SemaphoreType.DMA
    return pl.pallas_call(
        in_proj_kernel,
        out_shape=[
            jax.ShapeDtypeStruct((2, 16, NQ * QC), bf16),
            jax.ShapeDtypeStruct((NT, 128, TILE), f32),
            jax.ShapeDtypeStruct((NT, 128, TILE), f32),
        ],
        in_specs=[vspec, vspec, anyspec, anyspec, anyspec],
        out_specs=[vspec, anyspec, anyspec],
        scratch_shapes=[
            pltpu.VMEM((NQ, 1024, QC), bf16),
            pltpu.VMEM((4 * NT, 1024, TILE), bf16),
            pltpu.VMEM((128, 512), bf16),
            pltpu.VMEM((8, 512), f32),
            pltpu.VMEM((8, 8, 128), f32),
            pltpu.VMEM((8, 8, 128), f32),
            pltpu.VMEM((128, 1024), bf16),
            pltpu.VMEM((NQ, 4, 32, QC), f32),
            pltpu.VMEM((NQ, 2, 32, QC), f32),
            pltpu.VMEM((NQ, 32, QC), f32),
            pltpu.VMEM((NQ, 32, QC), f32),
            pltpu.VMEM((NQ, 32, QC), bf16),
            pltpu.VMEM((NQ, 16, QC), bf16),
            pltpu.VMEM((2 * NT, 128, TILE), f32),
            pltpu.VMEM((2 * NT, 128, TILE), f32),
            pltpu.VMEM((2 * NT, 128, TILE), f32),
            dma((NQ,)), dma((4 * NT,)), dma, dma, dma, dma, dma((7,)), dma((8,)),
            dma((NQ, 2)), dma((NQ, 2)), dma((NQ,)), dma((NQ,)), dma((NQ,)), dma((NQ,)),
            dma((2 * NT,)), dma((2 * NT,)), dma((2 * NT,)),
        ],
        compiler_params=pltpu.CompilerParams(
            collective_id=0, has_side_effects=True, vmem_limit_bytes=VMEM_LIMIT),
        cost_estimate=pl.CostEstimate(flops=5_000_000_000, bytes_accessed=45_000_000, transcendentals=0),
        name="in_proj",
    )(x_loc, gain, wq, wg, wu)


SLOTS = 5


def attend_kernel(len_ref, qkv_ref, cos_ref, sin_ref, k_ref, v_ref, ko_ref, vo_ref, o_ref,
                  kb, vb, qs, kns, vns, osc, ksem, vsem, kosem, vosem):
    n = k_ref.shape[0]
    t_len = k_ref.shape[1]

    def k_in(r, s):
        return local_copy(k_ref.at[r], kb.at[s], ksem.at[s])

    def v_in(r, s):
        return local_copy(v_ref.at[r], vb.at[s], vsem.at[s])

    def k_out(r, s):
        return local_copy(kb.at[s], ko_ref.at[r], kosem.at[s])

    def v_out(r, s):
        return local_copy(vb.at[s], vo_ref.at[r], vosem.at[s])

    AHEAD = 3
    for r in range(AHEAD):
        k_in(r, r).start()
        v_in(r, r).start()

    cos_t = cos_ref[...]
    sin_t = sin_ref[...]
    for g in range(17):
        part, base = (0, g * 256) if g < 9 else (1, (g - 9) * 256)
        a = qkv_ref[part, :, base:base + 128].astype(f32)
        b = qkv_ref[part, :, base + 128:base + 256].astype(f32)
        lo = (a * cos_t - b * sin_t).astype(bf16).astype(f32)
        hi = (b * cos_t + a * sin_t).astype(bf16).astype(f32)
        if g < 16:
            qs[:, g, 0:128] = lo
            qs[:, g, 128:256] = hi
        else:
            kns[:, 0:128] = lo
            kns[:, 128:256] = hi
    vns[...] = qkv_ref[1, :, 2048:2304].astype(f32)

    row16 = lax.broadcasted_iota(jnp.int32, (16, 256), 0)
    pos = lax.broadcasted_iota(jnp.int32, (16, t_len), 1)

    def body(r, _):
        s = lax.rem(r, SLOTS)
        nxt = r + AHEAD

        @pl.when(nxt < n)
        def _():
            s2 = lax.rem(nxt, SLOTS)

            @pl.when(nxt >= SLOTS)
            def _():
                k_out(nxt - SLOTS, s2).wait()
                v_out(nxt - SLOTS, s2).wait()
            k_in(nxt, s2).start()
            v_in(nxt, s2).start()

        p = len_ref[r]
        base = pl.multiple_of((p // 16) * 16, 16)
        hit = row16 == p - base
        k_in(r, s).wait()
        krow = kb[s, pl.ds(base, 16), :]
        kb[s, pl.ds(base, 16), :] = jnp.where(hit, kns[pl.ds(r, 1), :].astype(bf16), krow)
        q = qs[r].astype(bf16)
        sc = lax.dot_general(q, kb[s], (((1,), (1,)), ((), ())), preferred_element_type=f32) * (256 ** -0.5)
        k_out(r, s).start()
        v_in(r, s).wait()
        vrow = vb[s, pl.ds(base, 16), :]
        vb[s, pl.ds(base, 16), :] = jnp.where(hit, vns[pl.ds(r, 1), :].astype(bf16), vrow)
        sc = jnp.where(pos <= p, sc, -1e30)
        m = jnp.max(sc, axis=1, keepdims=True)
        e = jnp.exp(sc - m)
        den = jnp.sum(e, axis=1, keepdims=True)
        pr = (e / den).astype(bf16)
        osc[r] = jnp.dot(pr, vb[s], preferred_element_type=f32).astype(bf16).astype(f32)
        v_out(r, s).start()
        return 0

    lax.fori_loop(0, n, body, 0)
    for g in range(16):
        o_ref[:, 256 * g:256 * (g + 1)] = osc[:, g, :].astype(bf16)
    for r in range(n - SLOTS, n):
        k_out(r, r % SLOTS).wait()
        v_out(r, r % SLOTS).wait()


def attend(lens, qkv, cos_t, sin_t, kc, vc):
    anyspec = pl.BlockSpec(memory_space=pltpu.HBM)
    vspec = pl.BlockSpec(memory_space=pltpu.VMEM)
    dma = pltpu.SemaphoreType.DMA
    n, t_len, hd = kc.shape
    return pl.pallas_call(
        attend_kernel,
        out_shape=[
            jax.ShapeDtypeStruct(kc.shape, bf16),
            jax.ShapeDtypeStruct(vc.shape, bf16),
            jax.ShapeDtypeStruct((n, 4096), bf16),
        ],
        in_specs=[pl.BlockSpec(memory_space=pltpu.SMEM), vspec, vspec, vspec, anyspec, anyspec],
        out_specs=[anyspec, anyspec, vspec],
        scratch_shapes=[
            pltpu.VMEM((SLOTS, t_len, hd), bf16),
            pltpu.VMEM((SLOTS, t_len, hd), bf16),
            pltpu.VMEM((n, 16, hd), f32),
            pltpu.VMEM((n, hd), f32),
            pltpu.VMEM((n, hd), f32),
            pltpu.VMEM((n, 16, hd), f32),
            dma((SLOTS,)), dma((SLOTS,)), dma((SLOTS,)), dma((SLOTS,)),
        ],
        compiler_params=pltpu.CompilerParams(vmem_limit_bytes=40 * 2 ** 20),
        cost_estimate=pl.CostEstimate(flops=40_000_000_000, bytes_accessed=134_000_000, transcendentals=1_000_000),
        name="attend",
    )(lens, qkv, cos_t, sin_t, kc, vc)


def out_proj_kernel(o_ref, x_ref, d_ref, r_ref, wao_ref, wmo_ref, y_ref,
                    db, rb, wao, wmo, ab, ob, zs, zk, zr,
                    dsem, rsem, waosem, wmosem, a1s, a1r, a2s, a2r, a3s, a3r,
                    o0s, o0r, o1s, o1r, o2s, o2r, o3s, o3r, zss, zrs):
    x = lax.axis_index("x")
    yz = lax.axis_index("yz")
    core = lax.rem(x, 2)
    x_core = x + 1 - 2 * core
    x_chip = lax.rem(x + 2, 4)
    x_diag = x_chip + 1 - 2 * core
    partner = {"x": x_core}
    xpeer = {"x": x_chip}
    ypeer = {"yz": 1 - yz}

    def d_in(i):
        return local_copy(d_ref.at[i], db.at[i], dsem.at[i])

    def r_in(i):
        return local_copy(r_ref.at[i], rb.at[i], rsem.at[i])

    for i in range(NT):
        d_in(i).start()
        r_in(i).start()
    order = (x, x_core, x_chip, x_diag)

    def wmo_in(n, t):
        rows = pl.multiple_of(order[n] * 2048 + t * TILE, TILE)
        return local_copy(wmo_ref.at[pl.ds(rows, TILE), :], wmo.at[n * 4 + t], wmosem.at[n * 4 + t])

    wao_in = local_copy(wao_ref, wao, waosem)
    for n in range(4):
        for t in range(4):
            wmo_in(n, t).start()
        if n == 1:
            wao_in.start()

    barrier = pltpu.get_barrier_semaphore()
    for dev in (partner, xpeer, ypeer):
        pl.semaphore_signal(barrier, inc=1, device_id=dev, device_id_type=MESH)
    pl.semaphore_wait(barrier, 3)

    own_half = pl.multiple_of(yz * 2048, 2048)
    peer_half = pl.multiple_of((1 - yz) * 2048, 2048)
    mine = 2 * x + yz
    o_y = remote_copy(o_ref.at[:, pl.ds(peer_half, 2048)], ob.at[mine], o0s, o0r, ypeer)
    o_y.start()
    ob[mine] = o_ref[:, pl.ds(own_half, 2048)]

    def a_part(t):
        return remote_copy(ab.at[x, t], ab.at[x, t], a1s.at[t], a1r.at[t], partner)

    def a_chip(t):
        return remote_copy(ab.at[x, t], ab.at[x, t], a2s.at[t], a2r.at[t], xpeer)

    def a_fwd(t):
        return remote_copy(ab.at[x_chip, t], ab.at[x_chip, t], a3s.at[t], a3r.at[t], partner)

    def o_block(b):
        return ob.at[pl.ds(2 * b, 2)]

    o_part = remote_copy(o_block(x), o_block(x), o1s, o1r, partner)
    o_chip = remote_copy(o_block(x), o_block(x), o2s, o2r, xpeer)
    o_fwd = remote_copy(o_block(x_chip), o_block(x_chip), o3s, o3r, partner)

    for t in range(4):
        for i in (2 * t, 2 * t + 1):
            d_in(i).wait()
            r_in(i).wait()
        gate = (db[2 * t] + rb[2 * t]).astype(bf16).astype(f32)
        up = (db[2 * t + 1] + rb[2 * t + 1]).astype(bf16).astype(f32)
        ab[x, t] = (jax.nn.silu(gate) * up).astype(bf16)
        if t:
            a_chip(t - 1).start()
            a_part(t - 1).start()
        if t == 2:
            o_y.wait()
            o_chip.start()
            o_part.start()

    mc = pl.multiple_of((1 - yz) * 512, 512)
    kc = pl.multiple_of(yz * 512, 512)

    def mlp(n, t, first=False):
        wmo_in(n, t).wait()
        a = ab[order[n], t]
        w = wmo.at[n * 4 + t]
        ps = jnp.dot(a, w[:, pl.ds(mc, 512)], preferred_element_type=f32)
        pk = jnp.dot(a, w[:, pl.ds(kc, 512)], preferred_element_type=f32)
        if first:
            zs[...] = ps
            zk[...] = pk
        else:
            zs[...] += ps
            zk[...] += pk

    mlp(0, 0, first=True)
    a_chip(3).start()
    a_part(3).start()
    for t in range(1, 4):
        mlp(0, t)
    o_part.wait()
    for t in range(4):
        a_part(t).wait()
        mlp(1, t)
    for t in range(4):
        a_chip(t).wait()
        a_fwd(t).start()
        if t == 1:
            o_chip.wait()
            o_fwd.start()
        mlp(2, t)
        if t == 2:
            o_fwd.wait()
            wao_in.wait()
            attn = ob[...].reshape(128, 2048)
            zs[...] += jnp.dot(attn, wao[:, pl.ds(mc, 512)], preferred_element_type=f32)
            zk[...] += jnp.dot(attn, wao[:, pl.ds(kc, 512)], preferred_element_type=f32)
        if t:
            a_fwd(t - 1).wait()
            mlp(3, t - 1)
    a_fwd(3).wait()
    mlp(3, 3)
    z_y = remote_copy(zs, zr, zss, zrs, ypeer)
    z_y.start()
    z_y.wait()
    y_ref[...] = (x_ref[...].astype(f32) + (zk[...] + zr[...])).astype(bf16)


def out_proj(o, x_loc, d, r, wao, wmo):
    anyspec = pl.BlockSpec(memory_space=pltpu.HBM)
    vspec = pl.BlockSpec(memory_space=pltpu.VMEM)
    dma = pltpu.SemaphoreType.DMA
    return pl.pallas_call(
        out_proj_kernel,
        out_shape=jax.ShapeDtypeStruct((128, 512), bf16),
        in_specs=[vspec, vspec, anyspec, anyspec, anyspec, anyspec],
        out_specs=vspec,
        scratch_shapes=[
            pltpu.VMEM((NT, 128, TILE), f32),
            pltpu.VMEM((NT, 128, TILE), f32),
            pltpu.VMEM((2048, 1024), bf16),
            pltpu.VMEM((16, TILE, 1024), bf16),
            pltpu.VMEM((4, 4, 128, TILE), bf16),
            pltpu.VMEM((8, 16, 2048), bf16),
            pltpu.VMEM((128, 512), f32),
            pltpu.VMEM((128, 512), f32),
            pltpu.VMEM((128, 512), f32),
            dma((NT,)), dma((NT,)), dma, dma((16,)),
            dma((4,)), dma((4,)), dma((4,)), dma((4,)), dma((4,)), dma((4,)),
            dma, dma, dma, dma, dma, dma, dma, dma, dma, dma,
        ],
        compiler_params=pltpu.CompilerParams(
            collective_id=1, has_side_effects=True, vmem_limit_bytes=48 * 2 ** 20),
        cost_estimate=pl.CostEstimate(flops=3_000_000_000, bytes_accessed=26_000_000, transcendentals=0),
        name="out_proj",
    )(o, x_loc, d, r, wao, wmo)


def solution(mesh):
    both_axes = ("x", "yz")
    row_spec = P("dp", both_axes)
    in_w_spec = P("x", "yz")
    out_w_spec = P("yz", "x")
    cache_spec = P(("dp", "x", "yz"), None, None)
    len_spec = P(("dp", "x", "yz"))
    swap = [(0, 2), (2, 0), (1, 3), (3, 1)]

    def local_layer(x_loc, gain_loc, wqkv_loc, wgate_loc, wup_loc, wao_loc, wmo_loc, kc_loc, vc_loc, len_loc):
        gain = jnp.broadcast_to(gain_loc.astype(f32)[None, :], (8, 512))
        inv_freq = 10000.0 ** (-jnp.arange(128, dtype=f32) / 128)
        angles = len_loc.astype(f32)[:, None] * inv_freq
        cos_t = jnp.cos(angles)
        sin_t = jnp.sin(angles)
        qkv, s, d = in_proj(x_loc, gain, wqkv_loc, wgate_loc, wup_loc)
        r = lax.ppermute(s, "x", swap)
        k_all, v_all, o = attend(len_loc, qkv, cos_t, sin_t, kc_loc, vc_loc)
        y_loc = out_proj(o, x_loc, d, r, wao_loc, wmo_loc)
        return y_loc, k_all, v_all

    in_specs = (row_spec, P(both_axes), in_w_spec, in_w_spec, in_w_spec, out_w_spec, out_w_spec, cache_spec, cache_spec, len_spec)
    out_specs = (row_spec, cache_spec, cache_spec)
    return jax.shard_map(local_layer, mesh=mesh, in_specs=in_specs, out_specs=out_specs, check_vma=False)
```

time: 230 us -> 110 us (0.48)
  Pallas kernels: 0 us -> 104 us
  matrix products: 64.7 us -> 0 us
  other arithmetic: 54.5 us -> 0.79 us
  blocking collectives: 47.1 us -> 0 us
  waiting for transfers between devices: 43 us -> 0.01 us
  between operations: 13.9 us -> 0.69 us
    pallas_call x0 -> x3, Pallas kernels: none -> 104 us  [the longest x1 45 us: attend(): pl.pallas_call(attend_kernel, out_shape=[jax.ShapeDtypeStruct(kc.shape, b...]
    dot_general x7 -> x0, matrix products: 64.7 us -> none  [the longest x1 15.5 us: attend_local(): jnp.einsum('bht,btd->bhd', attn_probs, v_all, preferred_element_type=jnp....]
    select_n x1 -> x0, other arithmetic: 44.8 us -> none  [local_layer(): k_all = jnp.where(new_slot, k_rot[:, None, :], kc_loc)]
    reduce_scatter x4 -> x0, waiting for transfers between devices: 38.6 us -> none  [the longest x1 26.7 us: local_layer(): lax.psum_scatter(gate_part, 'x', scatter_dimension=0, tiled=True)]
    psum x1 -> x0, blocking collectives: 25.1 us -> none  [local_layer(): row_stats = lax.psum(row_stats, both_axes)]
    all_gather x2 -> x0, blocking collectives: 15 us -> none  [the longest x1 9.09 us: local_layer(): attn_full = lax.all_gather(attn_rows, 'x', axis=0, tiled=True)]
    all_to_all x1 -> x0, blocking collectives: 7.01 us -> none  [local_layer(): attn_rows = lax.all_to_all(attn_dev, 'yz', 1, 0, tiled=True)]
    convert_element_type x8 -> x1, other arithmetic: 7.63 us -> 0.66 us  [local_layer(): angles = len_loc.astype(f32)[:, None] * inv_freq]
  transfers between devices with their start and end apart: 6 -> 1, of which waited for: 3 -> 0; matrix products, arithmetic and copies ran while one was open for 43% -> 1% of each run, Pallas kernels for 0% -> 41%
where the time goes in v1:
time: 110 us
  Pallas kernels  104 us (95%)
  local copies, waits for them, and re-layouts  3.51 us (3%)
  starting transfers between devices  1.51 us (1%)
    pallas_call x1, Pallas kernels, attend(): pl.pallas_call(attend_kernel, out_shape=[jax.ShapeDtypeStruct(kc.shape, b...  45 us
    pallas_call x1, Pallas kernels, in_proj(): pl.pallas_call(in_proj_kernel, out_shape=[jax.ShapeDtypeStruct((2, 16, NQ...  32.8 us
    pallas_call x1, Pallas kernels, out_proj(): pl.pallas_call(out_proj_kernel, out_shape=jax.ShapeDtypeStruct((128, 512)...  25.8 us
    unnamed x9, local copies, waits for them, and re-layouts  2.22 us
  transfers between devices with their start and end apart: 1, of which 0 were waited for; matrix products, arithmetic and copies ran while one was open for 1% of the time, Pallas kernels for 41%

profile of v1, /device:TPU:0, one launch (start us, length us, event | category | flops | bytes accessed | tf_op | source)
XLA Modules:
  0.0 110.2 jit_solution(7915613694214829583)
XLA Ops:
  0.6 1.3 %broadcast_in_dim.2.g_ref = f32[8,512]{1,0:T(8,128)} broadcast(bf16[512]{0:T(512)(128)(2,1)} %param.11), dimensions={1} | broadcast | bytes 17408 | tf_op jit(solution)/shard_map/broadcast_in_dim | solution.py:546
  1.9 32.8 %in_proj.1 = (bf16[2,16,2304]{2,1,0:T(8,128)(2,1)}, f32[8,128,512]{2,1,0:T(8,128)}, f32[8,128,512]{2,1,0:T(8,128)}) custom-call(bf16[128,512]{1,0:T(8,128)(2,1)} %x_ref.3, f32[8,512]{1,0:T(8,128)} %broadcast_in_dim.2.g_ref, bf16[1024,2304]{1,0:T(8,128)(2,1)} %wq_ref.1, bf16[1024,8192]{1,0:T(8,128)(2,1)} %wg_ref.1, bf16[1024,8192]{1,0:T(8,128)(2,1)} %wu_ref.1), custom_call_target="tpu_custom_call" | custom-call | flops 5000000000 | bytes 45000000 | tf_op jit(solution)/shard_map/in_proj/pallas_call | solution.py:224
  34.7 1.5 %collective-permute-start = (f32[8,128,512]{2,1,0:T(8,128)}, f32[8,128,512]{2,1,0:T(8,128)S(1)}, u32[]{:S(2)}, u32[]{:S(2)}) collective-permute-start(f32[8,128,512]{2,1,0:T(8,128)} %get-tuple-element.12), channel_id=1, source_target_pairs={{0,2},{2,0},{1,3},{3,1},{4,6},{6,4},{5,7},{7,5}} | collective-permute-start | bytes 6291464 | tf_op jit(solution)/shard_map/ppermute | solution.py:552
  36.2 0.7 convert_element_type.7
  36.9 0.1 multiply_sine_fusion
  37.0 0.0 copy-start.2
  37.0 0.9 copy-done.2
  37.9 0.0 copy-start.3
  37.9 0.7 copy-done.3
  38.6 0.0 copy-start
  38.6 0.0 copy-start.1
  38.6 45.0 %attend.1 = (bf16[16,4096,256]{2,1,0:T(8,128)(2,1)}, bf16[16,4096,256]{2,1,0:T(8,128)(2,1)}, bf16[16,4096]{1,0:T(8,128)(2,1)S(1)}) custom-call(s32[16]{0:T(128)S(1)} %copy-done.3, bf16[2,16,2304]{2,1,0:T(8,128)(2,1)S(1)} %copy-done.2, f32[16,128]{1,0:T(8,128)S(1)} %get-tuple-element.16.cos_ref, f32[16,128]{1,0:T(8,128)S(1)} %get-tuple-element.15.sin_ref, ...), custom_call_target="tpu_custom_call" | custom-call | flops 40000000000 | bytes 134000000 | tf_op jit(solution)/shard_map/attend/pallas_call | solution.py:354
  83.6 0.0 collective-permute-done.r_ref
  83.6 0.0 copy-done
  83.6 0.0 copy-done.1
  83.6 25.8 %out_proj.1 = bf16[128,512]{1,0:T(8,128)(2,1)S(1)} custom-call(bf16[16,4096]{1,0:T(8,128)(2,1)S(1)} %get-tuple-element.10.o_ref, bf16[128,512]{1,0:T(8,128)(2,1)S(1)} %copy-done.1, f32[8,128,512]{2,1,0:T(8,128)S(1)} %copy-done, f32[8,128,512]{2,1,0:T(8,128)S(1)} %collective-permute-done.r_ref, bf16[2048,1024]{1,0:T(8,128)(2,1)} %wao_ref.1, ...), custom_call_target="tpu_custom_call" | custom-call | flops 3000000000 | bytes 26000000 | tf_op jit(solution)/shard_map/out_proj/pallas_call | solution.py:510
  109.5 0.7 copy.14
  (1 shorter events, 0.0 us)
Async XLA Ops:
  34.7 48.9 %collective-permute-start = (f32[8,128,512]{2,1,0:T(8,128)}, f32[8,128,512]{2,1,0:T(8,128)S(1)}, u32[]{:S(2)}, u32[]{:S(2)}) collective-permute-start(f32[8,128,512]{2,1,0:T(8,128)} %get-tuple-element.12), channel_id=1, source_target_pairs={{0,2},{2,0},{1,3},{3,1},{4,6},{6,4},{5,7},{7,5}} | collective-permute-start | bytes 6291464 | tf_op jit(solution)/shard_map/ppermute | solution.py:552
  37.0 0.9 copy-start.2
  37.9 0.7 copy-start.3
  38.6 45.1 %copy-start = (f32[8,128,512]{2,1,0:T(8,128)S(1)}, f32[8,128,512]{2,1,0:T(8,128)}, u32[]{:S(2)}) copy-start(f32[8,128,512]{2,1,0:T(8,128)} %get-tuple-element.11.d_ref) | copy-start | bytes 6291460
  38.6 45.1 %copy-start.1 = (bf16[128,512]{1,0:T(8,128)(2,1)S(1)}, bf16[128,512]{1,0:T(8,128)(2,1)}, u32[]{:S(2)}) copy-start(bf16[128,512]{1,0:T(8,128)(2,1)} %x_ref.3) | copy-start | bytes 393220

commit v2 on v1

v2 whole, which is shorter than its diff:
```python
import functools

import jax
import jax.numpy as jnp
from jax import lax
from jax.experimental import pallas as pl
from jax.experimental.pallas import tpu as pltpu
from jax.sharding import PartitionSpec as P

MESH = pl.DeviceIdType.MESH
VMEM_LIMIT = 67043328
TILE = 512
NT = 8
QC = 768
NQ = 3
W_FIRST = 8
W_AHEAD = 12

f32 = jnp.float32
bf16 = jnp.bfloat16


def local_copy(src, dst, sem):
    return pltpu.make_async_copy(src, dst, sem)


def remote_copy(src, dst, ssem, rsem, dev):
    return pltpu.make_async_remote_copy(src, dst, ssem, rsem, device_id=dev, device_id_type=MESH)


def in_proj_kernel(x_hbm, g_hbm, wq_ref, wg_ref, wu_ref, qkv_ref, s_ref, d_ref,
                   wqv, wv, x_ref, g_ref, xr, gr, qout, st, stx, h, qp, qr, qxs, qxr, qf, qyr, sbuf, rbuf, obuf,
                   wqsem, wsem, xs_sem, xr_sem, gs_sem, gr_sem, sts_sem, str_sem,
                   qds_sem, qdr_sem, qxs_sem, qxr_sem, qys_sem, qyr_sem, ds_sem, dr_sem, out_sem, xin_sem, gin_sem, qo_sem):
    d_model = 4096
    x = lax.axis_index("x")
    yz = lax.axis_index("yz")
    core = lax.rem(x, 2)
    x_core = x + 1 - 2 * core
    x_chip = lax.rem(x + 2, 4)
    x_diag = x_chip + 1 - 2 * core
    me = 2 * x + yz
    partner = {"x": x_core}
    xpeer = {"x": x_chip}
    ypeer = {"yz": 1 - yz}

    barrier = pltpu.get_barrier_semaphore()
    others = []
    for dx in range(4):
        for dy in range(2):
            if dx or dy:
                others.append((lax.rem(x + dx, 4), lax.rem(yz + dy, 2)))
    for ox, oy in others:
        pl.semaphore_signal(barrier, inc=1, device_id={"x": ox, "yz": oy}, device_id_type=MESH)
    x_in = local_copy(x_hbm, x_ref, xin_sem)
    g_in = local_copy(g_hbm, g_ref, gin_sem)
    x_in.start()
    g_in.start()

    def wq_copy(j):
        return local_copy(wq_ref.at[:, pl.ds(QC * j, QC)], wqv.at[j], wqsem.at[j])

    quarters = (x_diag, x_chip, x_core, x)

    def w_start(slot):
        phase = slot // NT
        q = quarters[0]
        for n in range(1, 4):
            q = jnp.where(phase == n, quarters[n], q)
        cols = pl.multiple_of(q * 2048 + (slot % NT) // 2 * TILE, TILE)

        def start(w_hbm):
            local_copy(w_hbm.at[:, pl.ds(cols, TILE)], wv.at[slot], wsem.at[slot]).start()

        if isinstance(slot, int):
            start(wg_ref if slot % 2 == 0 else wu_ref)
        else:
            pl.when(slot % 2 == 0)(lambda: start(wg_ref))
            pl.when(slot % 2 == 1)(lambda: start(wu_ref))

    def w_wait(slot):
        local_copy(wg_ref.at[:, pl.ds(0, TILE)], wv.at[slot], wsem.at[slot]).wait()

    x_in.wait()
    for j in range(NQ):
        wq_copy(j).start()
    for slot in range(W_FIRST):
        w_start(slot)
    g_in.wait()
    xf = x_ref[...].astype(f32)
    s1 = jnp.sum(xf, axis=1, keepdims=True)
    s2 = jnp.sum(xf * xf, axis=1, keepdims=True)
    lane = lax.broadcasted_iota(jnp.int32, (128, 128), 1)
    stat = jnp.where(lane == 0, s1, s2).T
    st[me] = stat[0:8]

    pl.semaphore_wait(barrier, 7)

    x_send = remote_copy(x_ref, xr, xs_sem, xr_sem, ypeer)
    g_send = remote_copy(g_ref, gr, gs_sem, gr_sem, ypeer)
    for n, (ox, oy) in enumerate(others):
        remote_copy(st.at[me], stx.at[me], sts_sem.at[n], str_sem.at[me], {"x": ox, "yz": oy}).start()
    g_send.start()
    x_send.start()
    stx[me] = st[me]
    for n, (ox, oy) in enumerate(others):
        src = 2 * ox + oy
        remote_copy(st.at[me], stx.at[src], sts_sem.at[n], str_sem.at[src], {"x": ox, "yz": oy}).wait()
    tot = jnp.sum(stx[...], axis=0)
    tot = jnp.concatenate([tot, jnp.zeros((120, 128), f32)], axis=0).T
    mean = tot[:, 0:1] / d_model
    var = tot[:, 1:2] / d_model - mean * mean
    rstd = lax.rsqrt(var + 1e-6)
    own_cols = pl.multiple_of(yz * 512, 512)
    peer_cols = pl.multiple_of((1 - yz) * 512, 512)
    h[:, pl.ds(own_cols, 512)] = ((xf - mean) * rstd * g_ref[...].astype(f32).reshape(1, 512)).astype(bf16)
    x_send.wait()
    g_send.wait()
    h[:, pl.ds(peer_cols, 512)] = ((xr[...].astype(f32) - mean) * rstd * gr[...].astype(f32).reshape(1, 512)).astype(bf16)

    for slot in range(W_FIRST, W_AHEAD):
        w_start(slot)

    def q_compute(j):
        wq_copy(j).wait()
        part = jnp.dot(h[...], wqv[j], preferred_element_type=f32)
        qp[j] = part.reshape(4, 32, QC)

    def q_pair(j, k):
        block = (x_diag, x_core)[k]
        return remote_copy(qp.at[j, block], qr.at[j, k], qds_sem.at[j, k], qdr_sem.at[j, k], partner)

    def q_pair_start(j):
        q_pair(j, 0).start()
        q_pair(j, 1).start()

    def q_chip(j):
        return remote_copy(qxs.at[j], qxr.at[j], qxs_sem.at[j], qxr_sem.at[j], xpeer)

    def q_sum(j):
        q_pair(j, 0).wait()
        qxs[j] = qp[j, x_chip] + qr[j, 0]

    def tile(slot):
        w_wait(slot)
        if isinstance(slot, int):
            if slot + W_AHEAD < 4 * NT:
                w_start(slot + W_AHEAD)
        else:
            @pl.when(slot + W_AHEAD < 4 * NT)
            def _():
                w_start(slot + W_AHEAD)
        return jnp.dot(h[...], wv[slot], preferred_element_type=f32)

    def d_copy(i):
        return remote_copy(sbuf.at[i], rbuf.at[i], ds_sem.at[i], dr_sem.at[i], partner)

    def s_out(i):
        return local_copy(obuf.at[i], s_ref.at[i], out_sem.at[i])

    def d_out(i):
        return local_copy(obuf.at[NT + i], d_ref.at[i], out_sem.at[NT + i])

    q_compute(0)
    q_compute(1)
    q_pair_start(0)
    q_compute(2)
    q_pair_start(1)

    after = {
        0: lambda: q_pair_start(2),
        1: lambda: q_sum(0),
        2: lambda: (q_chip(0).start(), q_sum(1)),
        3: lambda: (q_chip(1).start(), q_sum(2)),
        4: lambda: q_chip(2).start(),
    }
    for i in range(NT):
        sbuf[i] = tile(i)
        if i:
            d_copy(i - 1).start()
        if i in after:
            after[i]()

    for i in range(NT):
        part = tile(NT + i)
        if i == 0:
            d_copy(NT - 1).start()
        d_copy(i).wait()
        obuf[i] = part + rbuf[i]
        if i:
            s_out(i - 1).start()

    own_rows = pl.multiple_of(yz * 16, 16)
    peer_rows = pl.multiple_of((1 - yz) * 16, 16)

    def q_y(j):
        return remote_copy(qf.at[j, pl.ds(peer_rows, 16)], qyr.at[j], qys_sem.at[j], qyr_sem.at[j], ypeer)

    def q_final(j):
        q_pair(j, 1).wait()
        q_chip(j).wait()
        qf[j] = (qp[j, x] + qr[j, 1] + qxr[j]).astype(bf16)
        qout[yz, :, pl.ds(QC * j, QC)] = qf[j, pl.ds(own_rows, 16)]

    def send_tiles(lo, hi):
        def body(i, _):
            sbuf[NT + i] = tile(2 * NT + i)

            @pl.when(i == 0)
            def _():
                s_out(NT - 1).start()

            @pl.when(i > 0)
            def _():
                d_copy(NT + i - 1).start()
            return 0

        lax.fori_loop(lo, hi, body, 0)

    def keep_tiles(lo, hi):
        def body(i, _):
            part = tile(3 * NT + i)

            @pl.when(i == 0)
            def _():
                d_copy(2 * NT - 1).start()
            d_copy(NT + i).wait()
            obuf[NT + i] = part + rbuf[NT + i]

            @pl.when(i > 0)
            def _():
                d_out(i - 1).start()
            return 0

        lax.fori_loop(lo, hi, body, 0)

    send_tiles(0, 3)
    q_final(0)
    send_tiles(3, 4)
    q_y(0).start()
    send_tiles(4, 8)
    keep_tiles(0, 2)
    q_final(1)
    keep_tiles(2, 3)
    q_y(1).start()
    keep_tiles(3, 7)
    q_final(2)
    keep_tiles(7, 8)
    q_y(2).start()
    d_out(NT - 1).start()
    for j in range(NQ):
        q_y(j).wait()
        qout[1 - yz, :, pl.ds(QC * j, QC)] = qyr[j]
    for i in range(NT):
        s_out(i).wait()
        d_out(i).wait()
    q_out = local_copy(qout, qkv_ref, qo_sem)
    q_out.start()
    q_out.wait()


def in_proj(x_loc, gain, wq, wg, wu):
    anyspec = pl.BlockSpec(memory_space=pltpu.HBM)
    dma = pltpu.SemaphoreType.DMA
    return pl.pallas_call(
        in_proj_kernel,
        out_shape=[
            jax.ShapeDtypeStruct((2, 16, NQ * QC), bf16),
            jax.ShapeDtypeStruct((NT, 128, TILE), f32),
            jax.ShapeDtypeStruct((NT, 128, TILE), f32),
        ],
        in_specs=[anyspec] * 5,
        out_specs=[anyspec] * 3,
        scratch_shapes=[
            pltpu.VMEM((NQ, 1024, QC), bf16),
            pltpu.VMEM((4 * NT, 1024, TILE), bf16),
            pltpu.VMEM((128, 512), bf16),
            pltpu.VMEM((512,), bf16),
            pltpu.VMEM((128, 512), bf16),
            pltpu.VMEM((512,), bf16),
            pltpu.VMEM((2, 16, NQ * QC), bf16),
            pltpu.VMEM((8, 8, 128), f32),
            pltpu.VMEM((8, 8, 128), f32),
            pltpu.VMEM((128, 1024), bf16),
            pltpu.VMEM((NQ, 4, 32, QC), f32),
            pltpu.VMEM((NQ, 2, 32, QC), f32),
            pltpu.VMEM((NQ, 32, QC), f32),
            pltpu.VMEM((NQ, 32, QC), f32),
            pltpu.VMEM((NQ, 32, QC), bf16),
            pltpu.VMEM((NQ, 16, QC), bf16),
            pltpu.VMEM((2 * NT, 128, TILE), f32),
            pltpu.VMEM((2 * NT, 128, TILE), f32),
            pltpu.VMEM((2 * NT, 128, TILE), f32),
            dma((NQ,)), dma((4 * NT,)), dma, dma, dma, dma, dma((7,)), dma((8,)),
            dma((NQ, 2)), dma((NQ, 2)), dma((NQ,)), dma((NQ,)), dma((NQ,)), dma((NQ,)),
            dma((2 * NT,)), dma((2 * NT,)), dma((2 * NT,)), dma, dma, dma,
        ],
        compiler_params=pltpu.CompilerParams(
            collective_id=0, has_side_effects=True, vmem_limit_bytes=VMEM_LIMIT),
        cost_estimate=pl.CostEstimate(flops=5_000_000_000, bytes_accessed=45_000_000, transcendentals=0),
        name="in_proj",
    )(x_loc, gain, wq, wg, wu)


SLOTS = 6


def attend_kernel(len_hbm, qkv_hbm, k_ref, v_ref, ko_ref, vo_ref, o_ref,
                  kb, vb, len_ref, qkv_ref, qs, kns, vns, osc, ksem, vsem, kosem, vosem, isem):
    n = k_ref.shape[0]
    t_len = k_ref.shape[1]

    def k_in(r, s):
        return local_copy(k_ref.at[r], kb.at[s], ksem.at[s])

    def v_in(r, s):
        return local_copy(v_ref.at[r], vb.at[s], vsem.at[s])

    def k_out(r, s):
        return local_copy(kb.at[s], ko_ref.at[r], kosem.at[s])

    def v_out(r, s):
        return local_copy(vb.at[s], vo_ref.at[r], vosem.at[s])

    AHEAD = 4
    len_in = local_copy(len_hbm, len_ref, isem.at[0])
    qkv_in = local_copy(qkv_hbm, qkv_ref, isem.at[1])
    len_in.start()
    qkv_in.start()
    k_in(0, 0).start()
    v_in(0, 0).start()
    len_in.wait()
    qkv_in.wait()
    for r in range(1, AHEAD):
        k_in(r, r).start()
        v_in(r, r).start()
    row = lax.broadcasted_iota(jnp.int32, (16, 128), 0)
    lens = jnp.zeros((16, 128), jnp.int32)
    for r in range(16):
        lens = jnp.where(row == r, len_ref[r], lens)
    half = lax.broadcasted_iota(jnp.int32, (16, 128), 1).astype(f32)
    angles = lens.astype(f32) * 10000.0 ** (-half / 128)
    cos_t = jnp.cos(angles)
    sin_t = jnp.sin(angles)
    for g in range(17):
        part, base = (0, g * 256) if g < 9 else (1, (g - 9) * 256)
        a = qkv_ref[part, :, base:base + 128].astype(f32)
        b = qkv_ref[part, :, base + 128:base + 256].astype(f32)
        lo = (a * cos_t - b * sin_t).astype(bf16).astype(f32)
        hi = (b * cos_t + a * sin_t).astype(bf16).astype(f32)
        if g < 16:
            qs[:, g, 0:128] = lo
            qs[:, g, 128:256] = hi
        else:
            kns[:, 0:128] = lo
            kns[:, 128:256] = hi
    vns[...] = qkv_ref[1, :, 2048:2304].astype(f32)

    row16 = lax.broadcasted_iota(jnp.int32, (16, 256), 0)
    pos = lax.broadcasted_iota(jnp.int32, (16, t_len), 1)

    def body(r, _):
        s = lax.rem(r, SLOTS)
        nxt = r + AHEAD

        @pl.when(nxt < n)
        def _():
            s2 = lax.rem(nxt, SLOTS)

            @pl.when(nxt >= SLOTS)
            def _():
                k_out(nxt - SLOTS, s2).wait()
                v_out(nxt - SLOTS, s2).wait()
            k_in(nxt, s2).start()
            v_in(nxt, s2).start()

        p = len_ref[r]
        base = pl.multiple_of((p // 16) * 16, 16)
        hit = row16 == p - base
        k_in(r, s).wait()
        krow = kb[s, pl.ds(base, 16), :]
        kb[s, pl.ds(base, 16), :] = jnp.where(hit, kns[pl.ds(r, 1), :].astype(bf16), krow)
        q = qs[r].astype(bf16)
        sc = lax.dot_general(q, kb[s], (((1,), (1,)), ((), ())), preferred_element_type=f32) * (256 ** -0.5)
        k_out(r, s).start()
        v_in(r, s).wait()
        vrow = vb[s, pl.ds(base, 16), :]
        vb[s, pl.ds(base, 16), :] = jnp.where(hit, vns[pl.ds(r, 1), :].astype(bf16), vrow)
        sc = jnp.where(pos <= p, sc, -1e30)
        m = jnp.max(sc, axis=1, keepdims=True)
        e = jnp.exp(sc - m)
        den = jnp.sum(e, axis=1, keepdims=True)
        pr = (e / den).astype(bf16)
        v_out(r, s).start()
        osc[r] = jnp.dot(pr, vb[s], preferred_element_type=f32).astype(bf16).astype(f32)
        return 0

    lax.fori_loop(0, n, body, 0)
    for g in range(16):
        o_ref[:, 256 * g:256 * (g + 1)] = osc[:, g, :].astype(bf16)
    for r in range(n - SLOTS, n):
        k_out(r, r % SLOTS).wait()
        v_out(r, r % SLOTS).wait()


def attend(lens, qkv, kc, vc):
    anyspec = pl.BlockSpec(memory_space=pltpu.HBM)
    vspec = pl.BlockSpec(memory_space=pltpu.VMEM)
    dma = pltpu.SemaphoreType.DMA
    n, t_len, hd = kc.shape
    return pl.pallas_call(
        attend_kernel,
        out_shape=[
            jax.ShapeDtypeStruct(kc.shape, bf16),
            jax.ShapeDtypeStruct(vc.shape, bf16),
            jax.ShapeDtypeStruct((n, 4096), bf16),
        ],
        in_specs=[anyspec] * 4,
        out_specs=[anyspec, anyspec, vspec],
        scratch_shapes=[
            pltpu.VMEM((SLOTS, t_len, hd), bf16),
            pltpu.VMEM((SLOTS, t_len, hd), bf16),
            pltpu.SMEM((n,), jnp.int32),
            pltpu.VMEM((2, 16, NQ * QC), bf16),
            pltpu.VMEM((n, 16, hd), f32),
            pltpu.VMEM((n, hd), f32),
            pltpu.VMEM((n, hd), f32),
            pltpu.VMEM((n, 16, hd), f32),
            dma((SLOTS,)), dma((SLOTS,)), dma((SLOTS,)), dma((SLOTS,)), dma((2,)),
        ],
        compiler_params=pltpu.CompilerParams(vmem_limit_bytes=VMEM_LIMIT),
        cost_estimate=pl.CostEstimate(flops=40_000_000_000, bytes_accessed=134_000_000, transcendentals=1_000_000),
        name="attend",
    )(lens, qkv, kc, vc)


UNITS = ((0, 0, 128), (1, 0, 128), (2, 0, 64), (3, 0, 64), (2, 64, 64), (3, 64, 64))
NU = len(UNITS)


def out_proj_kernel(o_ref, x_hbm, d_ref, r_ref, wao_ref, wmo_ref, y_ref,
                    x_ref, db, rb, wao, wmo, ab, ob, zs, zk, zr,
                    xsem, dsem, rsem, waosem, wmosem, a1s, a1r, a2s, a2r, a3s, a3r,
                    o0s, o0r, o1s, o1r, o2s, o2r, o3s, o3r, zss, zrs):
    x = lax.axis_index("x")
    yz = lax.axis_index("yz")
    core = lax.rem(x, 2)
    x_core = x + 1 - 2 * core
    x_chip = lax.rem(x + 2, 4)
    x_diag = x_chip + 1 - 2 * core
    partner = {"x": x_core}
    xpeer = {"x": x_chip}
    ypeer = {"yz": 1 - yz}

    barrier = pltpu.get_barrier_semaphore()
    for dev in (partner, xpeer, ypeer):
        pl.semaphore_signal(barrier, inc=1, device_id=dev, device_id_type=MESH)

    def d_in(i):
        return local_copy(d_ref.at[i], db.at[i], dsem.at[i])

    def r_in(i):
        return local_copy(r_ref.at[i], rb.at[i], rsem.at[i])

    for i in range(NT):
        d_in(i).start()
        r_in(i).start()
    x_in = local_copy(x_hbm, x_ref, xsem)
    x_in.start()
    order = (x, x_core, x_chip, x_diag)

    def wmo_in(n, t):
        rows = pl.multiple_of(order[n] * 2048 + t * TILE, TILE)
        return local_copy(wmo_ref.at[pl.ds(rows, TILE), :], wmo.at[4 * n + t], wmosem.at[4 * n + t])

    wao_in = local_copy(wao_ref, wao, waosem)

    def wmo_start(n):
        for t in range(4):
            wmo_in(n, t).start()

    def a_tile(t):
        for i in (2 * t, 2 * t + 1):
            d_in(i).wait()
            r_in(i).wait()
        gate = (db[2 * t] + rb[2 * t]).astype(bf16).astype(f32)
        up = (db[2 * t + 1] + rb[2 * t + 1]).astype(bf16).astype(f32)
        ab[x, t] = (jax.nn.silu(gate) * up).astype(bf16)

    def unit(owner, u):
        t, r0, n = UNITS[u]
        return ab.at[owner, t, pl.ds(r0, n)]

    def a_part(u):
        return remote_copy(unit(x, u), unit(x, u), a1s.at[u], a1r.at[u], partner)

    def a_chip(u):
        return remote_copy(unit(x, u), unit(x, u), a2s.at[u], a2r.at[u], xpeer)

    def a_fwd(u):
        return remote_copy(unit(x_chip, u), unit(x_chip, u), a3s.at[u], a3r.at[u], partner)

    def a_send(u):
        a_chip(u).start()
        a_part(u).start()

    def o_block(b):
        return ob.at[pl.ds(2 * b, 2)]

    own_half = pl.multiple_of(yz * 2048, 2048)
    peer_half = pl.multiple_of((1 - yz) * 2048, 2048)
    mine = 2 * x + yz
    o_y = remote_copy(o_ref.at[:, pl.ds(peer_half, 2048)], ob.at[mine], o0s, o0r, ypeer)
    o_part = remote_copy(o_block(x), o_block(x), o1s, o1r, partner)
    o_chip = remote_copy(o_block(x), o_block(x), o2s, o2r, xpeer)
    o_fwd = remote_copy(o_block(x_chip), o_block(x_chip), o3s, o3r, partner)

    mc = pl.multiple_of((1 - yz) * 512, 512)
    kc = pl.multiple_of(yz * 512, 512)

    def mlp(n, u, wait=True, first=False):
        t, r0, m = UNITS[u]
        rows = pl.ds(r0, m)
        if wait:
            wmo_in(n, t).wait()
        a = ab[order[n], t, rows]
        w = wmo.at[4 * n + t]
        ps = jnp.dot(a, w[:, pl.ds(mc, 512)], preferred_element_type=f32)
        zs[rows] = ps if first else zs[rows] + ps
        pk = jnp.dot(a, w[:, pl.ds(kc, 512)], preferred_element_type=f32)
        zk[rows] = pk if first else zk[rows] + pk

    def mlp_tile(n, t, first=False):
        wmo_in(n, t).wait()
        a = ab[order[n], t]
        w = wmo.at[4 * n + t]
        ps = jnp.dot(a, w[:, pl.ds(mc, 512)], preferred_element_type=f32)
        zs[...] = ps if first else zs[...] + ps
        pk = jnp.dot(a, w[:, pl.ds(kc, 512)], preferred_element_type=f32)
        zk[...] = pk if first else zk[...] + pk

    a_tile(0)
    ob[mine] = o_ref[:, pl.ds(own_half, 2048)]
    pl.semaphore_wait(barrier, 3)
    o_y.start()
    a_send(0)
    a_tile(1)
    wmo_start(0)
    a_tile(2)
    a_send(1)
    a_tile(3)
    wmo_start(1)
    mlp_tile(0, 0, first=True)
    mlp_tile(0, 1)
    o_y.wait()
    o_chip.start()
    o_part.start()
    for u in range(2, NU):
        a_send(u)
    wmo_start(2)
    wao_in.start()
    mlp_tile(0, 2)
    mlp_tile(0, 3)
    a_part(0).wait()
    mlp_tile(1, 0)
    a_part(1).wait()
    mlp_tile(1, 1)
    a_chip(0).wait()
    a_fwd(0).start()
    wmo_start(3)
    mlp(2, 0)
    for u in range(2, NU):
        a_part(u).wait()
    mlp_tile(1, 2)
    mlp_tile(1, 3)
    a_chip(1).wait()
    a_fwd(1).start()
    mlp(2, 1)
    a_fwd(0).wait()
    mlp(3, 0)
    o_part.wait()
    o_chip.wait()
    o_fwd.start()
    a_fwd(1).wait()
    mlp(3, 1)
    wao_in.wait()
    a_chip(2).wait()
    a_fwd(2).start()
    mlp(2, 2)
    o_fwd.wait()
    attn = ob[...].reshape(128, 2048)
    zs[...] += jnp.dot(attn, wao[:, pl.ds(mc, 512)], preferred_element_type=f32)
    zk[...] += jnp.dot(attn, wao[:, pl.ds(kc, 512)], preferred_element_type=f32)

    def z_y(c):
        rows = pl.ds(64 * c, 64)
        return remote_copy(zs.at[rows], zr.at[rows], zss.at[c], zrs.at[c], ypeer)

    a_chip(3).wait()
    a_fwd(3).start()
    mlp(2, 3)
    a_fwd(2).wait()
    mlp(3, 2)
    a_fwd(3).wait()
    mlp(3, 3)
    z_y(0).start()
    a_chip(4).wait()
    a_fwd(4).start()
    mlp(2, 4, wait=False)
    a_chip(5).wait()
    a_fwd(5).start()
    mlp(2, 5, wait=False)
    a_fwd(4).wait()
    mlp(3, 4, wait=False)
    a_fwd(5).wait()
    mlp(3, 5, wait=False)
    z_y(1).start()
    x_in.wait()
    for c in range(2):
        z_y(c).wait()
        rows = pl.ds(64 * c, 64)
        y_ref[rows, :] = (x_ref[rows, :].astype(f32) + (zk[rows, :] + zr[rows, :])).astype(bf16)


def out_proj(o, x_loc, d, r, wao, wmo):
    anyspec = pl.BlockSpec(memory_space=pltpu.HBM)
    vspec = pl.BlockSpec(memory_space=pltpu.VMEM)
    dma = pltpu.SemaphoreType.DMA
    return pl.pallas_call(
        out_proj_kernel,
        out_shape=jax.ShapeDtypeStruct((128, 512), bf16),
        in_specs=[vspec, anyspec, anyspec, anyspec, anyspec, anyspec],
        out_specs=vspec,
        scratch_shapes=[
            pltpu.VMEM((128, 512), bf16),
            pltpu.VMEM((NT, 128, TILE), f32),
            pltpu.VMEM((NT, 128, TILE), f32),
            pltpu.VMEM((2048, 1024), bf16),
            pltpu.VMEM((16, TILE, 1024), bf16),
            pltpu.VMEM((4, 4, 128, TILE), bf16),
            pltpu.VMEM((8, 16, 2048), bf16),
            pltpu.VMEM((128, 512), f32),
            pltpu.VMEM((128, 512), f32),
            pltpu.VMEM((128, 512), f32),
            dma, dma((NT,)), dma((NT,)), dma, dma((16,)),
            dma((NU,)), dma((NU,)), dma((NU,)), dma((NU,)), dma((NU,)), dma((NU,)),
            dma, dma, dma, dma, dma, dma, dma, dma, dma((2,)), dma((2,)),
        ],
        compiler_params=pltpu.CompilerParams(
            collective_id=1, has_side_effects=True, vmem_limit_bytes=48 * 2 ** 20),
        cost_estimate=pl.CostEstimate(flops=3_000_000_000, bytes_accessed=26_000_000, transcendentals=0),
        name="out_proj",
    )(o, x_loc, d, r, wao, wmo)


def solution(mesh):
    both_axes = ("x", "yz")
    row_spec = P("dp", both_axes)
    in_w_spec = P("x", "yz")
    out_w_spec = P("yz", "x")
    cache_spec = P(("dp", "x", "yz"), None, None)
    len_spec = P(("dp", "x", "yz"))
    swap = [(0, 2), (2, 0), (1, 3), (3, 1)]

    def local_layer(x_loc, gain_loc, wqkv_loc, wgate_loc, wup_loc, wao_loc, wmo_loc, kc_loc, vc_loc, len_loc):
        qkv, s, d = in_proj(x_loc, gain_loc, wqkv_loc, wgate_loc, wup_loc)
        r = lax.ppermute(s, "x", swap)
        k_all, v_all, o = attend(len_loc, qkv, kc_loc, vc_loc)
        y_loc = out_proj(o, x_loc, d, r, wao_loc, wmo_loc)
        return y_loc, k_all, v_all

    in_specs = (row_spec, P(both_axes), in_w_spec, in_w_spec, in_w_spec, out_w_spec, out_w_spec, cache_spec, cache_spec, len_spec)
    out_specs = (row_spec, cache_spec, cache_spec)
    return jax.shard_map(local_layer, mesh=mesh, in_specs=in_specs, out_specs=out_specs, check_vma=False)
```

time: 110 us -> 103 us (0.936)
  Pallas kernels: 104 us -> 96.3 us
  waiting for transfers between devices: 0.01 us -> 1.28 us
    pallas_call x1, Pallas kernels: 32.8 us -> 27.1 us  [in_proj(): pl.pallas_call(in_proj_kernel, out_shape=[jax.ShapeDtypeStruct((2, 16, NQ...]
    unnamed x9 -> x7, local copies, waits for them, and re-layouts: 2.22 us -> 4.06 us
    pallas_call x1, Pallas kernels: 25.8 us -> 24 us  [out_proj(): pl.pallas_call(out_proj_kernel, out_shape=jax.ShapeDtypeStruct((128, 512)...]
    broadcast_in_dim x1 -> x0, local copies, waits for them, and re-layouts: 1.29 us -> none  [local_layer(): gain = jnp.broadcast_to(gain_loc.astype(f32)[None, :], (8, 512))]
    ppermute x1, waiting for transfers between devices: 0.01 us -> 1.28 us  [local_layer(): r = lax.ppermute(s, 'x', swap)]
  transfers between devices with their start and end apart: 1 -> 1, of which waited for: 0 -> 1; matrix products, arithmetic and copies ran while one was open for 1% -> 0% of each run, Pallas kernels for 41% -> 44%
where the time goes in v2:
time: 103 us
  Pallas kernels  96.3 us (93%)
  local copies, waits for them, and re-layouts  4.06 us (4%)
  waiting for transfers between devices  1.28 us (1%)
    pallas_call x1, Pallas kernels, attend(): pl.pallas_call(attend_kernel, out_shape=[jax.ShapeDtypeStruct(kc.shape, b...  45.2 us
    pallas_call x1, Pallas kernels, in_proj(): pl.pallas_call(in_proj_kernel, out_shape=[jax.ShapeDtypeStruct((2, 16, NQ...  27.1 us
    pallas_call x1, Pallas kernels, out_proj(): pl.pallas_call(out_proj_kernel, out_shape=jax.ShapeDtypeStruct((128, 512)...  24 us
    unnamed x7, local copies, waits for them, and re-layouts  4.06 us
  transfers between devices with their start and end apart: 1, of which 1 were waited for; matrix products, arithmetic and copies ran while one was open for 0% of the time, Pallas kernels for 44%

profile of v2, /device:TPU:0, one launch (start us, length us, event | category | flops | bytes accessed | tf_op | source)
XLA Modules:
  0.0 102.9 jit_solution(1766193763665004285)
XLA Ops:
  0.6 27.1 %in_proj.1 = (bf16[2,16,2304]{2,1,0:T(8,128)(2,1)}, f32[8,128,512]{2,1,0:T(8,128)}, f32[8,128,512]{2,1,0:T(8,128)}) custom-call(bf16[128,512]{1,0:T(8,128)(2,1)} %x_hbm.3, bf16[512]{0:T(512)(128)(2,1)} %g_hbm.1, bf16[1024,2304]{1,0:T(8,128)(2,1)} %wq_ref.1, bf16[1024,8192]{1,0:T(8,128)(2,1)} %wg_ref.1, bf16[1024,8192]{1,0:T(8,128)(2,1)} %wu_ref.1), custom_call_target="tpu_custom_call" | custom-call | flops 5000000000 | bytes 45000000 | tf_op jit(solution)/shard_map/in_proj/pallas_call | solution.py:265
  27.8 0.6 collective-permute-start
  28.4 45.2 %attend.1 = (bf16[16,4096,256]{2,1,0:T(8,128)(2,1)}, bf16[16,4096,256]{2,1,0:T(8,128)(2,1)}, bf16[16,4096]{1,0:T(8,128)(2,1)}) custom-call(s32[16]{0:T(128)} %len_hbm.1, bf16[2,16,2304]{2,1,0:T(8,128)(2,1)} %get-tuple-element.9.qkv_hbm, bf16[16,4096,256]{2,1,0:T(8,128)(2,1)} %k_ref.1, bf16[16,4096,256]{2,1,0:T(8,128)(2,1)} %v_ref.1), custom_call_target="tpu_custom_call" | custom-call | flops 40000000000 | bytes 134000000 | tf_op jit(solution)/shard_map/attend/pallas_call | solution.py:411
  73.5 1.3 %collective-permute-done.r_ref = f32[8,128,512]{2,1,0:T(8,128)} collective-permute-done((f32[8,128,512]{2,1,0:T(8,128)}, f32[8,128,512]{2,1,0:T(8,128)}, u32[]{:S(2)}, u32[]{:S(2)}) %collective-permute-start) | collective-permute-done | bytes 2097184 | tf_op jit(solution)/shard_map/ppermute | solution.py:667
  74.8 0.0 copy-start
  74.8 1.6 %copy-done = f32[8,128,512]{2,1,0:T(8,128)S(1)} copy-done((f32[8,128,512]{2,1,0:T(8,128)S(1)}, f32[8,128,512]{2,1,0:T(8,128)}, u32[]{:S(2)}) %copy-start) | copy-done | bytes 2097176
  76.4 0.0 copy-start.1
  76.4 0.9 copy-done.1
  77.3 0.0 copy-start.2
  77.3 0.9 copy-done.2
  78.2 24.0 %out_proj.1 = bf16[128,512]{1,0:T(8,128)(2,1)S(1)} custom-call(bf16[16,4096]{1,0:T(8,128)(2,1)S(1)} %copy-done.2, bf16[128,512]{1,0:T(8,128)(2,1)S(1)} %copy-done.1, f32[8,128,512]{2,1,0:T(8,128)S(1)} %copy-done, f32[8,128,512]{2,1,0:T(8,128)} %collective-permute-done.r_ref, bf16[2048,1024]{1,0:T(8,128)(2,1)} %wao_ref.1, bf16[8192,1024]{1,0:T(8,128)(2,1)} %wmo_ref.1), custom_call_target="tpu_custom_call" | custom-call | flops 3000000000 | bytes 26000000 | tf_op jit(solution)/shard_map/out_proj/pallas_call | solution.py:629
  102.2 0.7 copy.14
Async XLA Ops:
  27.8 47.0 %collective-permute-start = (f32[8,128,512]{2,1,0:T(8,128)}, f32[8,128,512]{2,1,0:T(8,128)}, u32[]{:S(2)}, u32[]{:S(2)}) collective-permute-start(f32[8,128,512]{2,1,0:T(8,128)} %get-tuple-element.12), channel_id=1, source_target_pairs={{0,2},{2,0},{1,3},{3,1},{4,6},{6,4},{5,7},{7,5}} | collective-permute-start | bytes 6291464 | tf_op jit(solution)/shard_map/ppermute | solution.py:667
  74.8 1.6 %copy-start = (f32[8,128,512]{2,1,0:T(8,128)S(1)}, f32[8,128,512]{2,1,0:T(8,128)}, u32[]{:S(2)}) copy-start(f32[8,128,512]{2,1,0:T(8,128)} %get-tuple-element.11.d_ref) | copy-start | bytes 6291460
  76.4 0.9 copy-start.1
  77.3 0.9 copy-start.2

commit v3 on v2

--- a/solution.py
+++ b/solution.py
@@ -9,7 +9,10 @@
 
 MESH = pl.DeviceIdType.MESH
 VMEM_LIMIT = 67043328
+OUT_ROOM = 8000000
 TILE = 512
+SA = 5
+SPLIT = 10
 NT = 8
 QC = 768
 NQ = 3
@@ -28,10 +31,10 @@
     return pltpu.make_async_remote_copy(src, dst, ssem, rsem, device_id=dev, device_id_type=MESH)
 
 
-def in_proj_kernel(x_hbm, g_hbm, wq_ref, wg_ref, wu_ref, qkv_ref, s_ref, d_ref,
+def in_proj_kernel(x_hbm, g_hbm, wq_ref, wg_ref, wu_ref, qkv_ref, sa_ref, sb_ref, r0_ref, d_ref,
                    wqv, wv, x_ref, g_ref, xr, gr, qout, st, stx, h, qp, qr, qxs, qxr, qf, qyr, sbuf, rbuf, obuf,
                    wqsem, wsem, xs_sem, xr_sem, gs_sem, gr_sem, sts_sem, str_sem,
-                   qds_sem, qdr_sem, qxs_sem, qxr_sem, qys_sem, qyr_sem, ds_sem, dr_sem, out_sem, xin_sem, gin_sem, qo_sem):
+                   qds_sem, qdr_sem, qxs_sem, qxr_sem, qys_sem, qyr_sem, ds_sem, dr_sem, out_sem, xin_sem, gin_sem, qo_sem, es_sem, er_sem):
     d_model = 4096
     x = lax.axis_index("x")
     yz = lax.axis_index("yz")
@@ -156,10 +159,13 @@
         return remote_copy(sbuf.at[i], rbuf.at[i], ds_sem.at[i], dr_sem.at[i], partner)
 
     def s_out(i):
-        return local_copy(obuf.at[i], s_ref.at[i], out_sem.at[i])
+        dst = sa_ref.at[i - 1] if i <= SA else sb_ref.at[i - 1 - SA]
+        return local_copy(obuf.at[i], dst, out_sem.at[i])
 
     def d_out(i):
         return local_copy(obuf.at[NT + i], d_ref.at[i], out_sem.at[NT + i])
+
+    early = remote_copy(obuf.at[0], r0_ref.at[0], es_sem, er_sem, xpeer)
 
     q_compute(0)
     q_compute(1)
@@ -187,7 +193,9 @@
             d_copy(NT - 1).start()
         d_copy(i).wait()
         obuf[i] = part + rbuf[i]
-        if i:
+        if i == 1:
+            early.start()
+        elif i:
             s_out(i - 1).start()
 
     own_rows = pl.multiple_of(yz * 16, 16)
@@ -251,12 +259,14 @@
     for j in range(NQ):
         q_y(j).wait()
         qout[1 - yz, :, pl.ds(QC * j, QC)] = qyr[j]
-    for i in range(NT):
-        s_out(i).wait()
-        d_out(i).wait()
     q_out = local_copy(qout, qkv_ref, qo_sem)
     q_out.start()
+    for i in range(NT):
+        if i:
+            s_out(i).wait()
+        d_out(i).wait()
     q_out.wait()
+    early.wait()
 
 
 def in_proj(x_loc, gain, wq, wg, wu):
@@ -266,11 +276,13 @@
         in_proj_kernel,
         out_shape=[
             jax.ShapeDtypeStruct((2, 16, NQ * QC), bf16),
-            jax.ShapeDtypeStruct((NT, 128, TILE), f32),
+            jax.ShapeDtypeStruct((SA, 128, TILE), f32),
+            jax.ShapeDtypeStruct((NT - 1 - SA, 128, TILE), f32),
+            jax.ShapeDtypeStruct((1, 128, TILE), f32),
             jax.ShapeDtypeStruct((NT, 128, TILE), f32),
         ],
         in_specs=[anyspec] * 5,
-        out_specs=[anyspec] * 3,
+        out_specs=[anyspec] * 5,
         scratch_shapes=[
             pltpu.VMEM((NQ, 1024, QC), bf16),
             pltpu.VMEM((4 * NT, 1024, TILE), bf16),
@@ -293,7 +305,7 @@
             pltpu.VMEM((2 * NT, 128, TILE), f32),
             dma((NQ,)), dma((4 * NT,)), dma, dma, dma, dma, dma((7,)), dma((8,)),
             dma((NQ, 2)), dma((NQ, 2)), dma((NQ,)), dma((NQ,)), dma((NQ,)), dma((NQ,)),
-            dma((2 * NT,)), dma((2 * NT,)), dma((2 * NT,)), dma, dma, dma,
+            dma((2 * NT,)), dma((2 * NT,)), dma((2 * NT,)), dma, dma, dma, dma, dma,
         ],
         compiler_params=pltpu.CompilerParams(
             collective_id=0, has_side_effects=True, vmem_limit_bytes=VMEM_LIMIT),
@@ -305,9 +317,11 @@
 SLOTS = 6
 
 
-def attend_kernel(len_hbm, qkv_hbm, k_ref, v_ref, ko_ref, vo_ref, o_ref,
-                  kb, vb, len_ref, qkv_ref, qs, kns, vns, osc, ksem, vsem, kosem, vosem, isem):
-    n = k_ref.shape[0]
+def attend_kernel(lo, hi, len_hbm, qkv_hbm, k_ref, v_ref, *refs):
+    if lo:
+        refs = refs[2:]
+    (ko_ref, vo_ref, o_hbm, o_ref, kb, vb, len_ref, qkv_ref, qs, kns, vns, osc,
+     ksem, vsem, kosem, vosem, isem, osem) = refs
     t_len = k_ref.shape[1]
 
     def k_in(r, s):
@@ -327,13 +341,14 @@
     qkv_in = local_copy(qkv_hbm, qkv_ref, isem.at[1])
     len_in.start()
     qkv_in.start()
-    k_in(0, 0).start()
-    v_in(0, 0).start()
+    for r in range(lo, lo + 2):
+        k_in(r, r % SLOTS).start()
+        v_in(r, r % SLOTS).start()
     len_in.wait()
     qkv_in.wait()
-    for r in range(1, AHEAD):
-        k_in(r, r).start()
-        v_in(r, r).start()
+    for r in range(lo + 2, lo + AHEAD):
+        k_in(r, r % SLOTS).start()
+        v_in(r, r % SLOTS).start()
     row = lax.broadcasted_iota(jnp.int32, (16, 128), 0)
     lens = jnp.zeros((16, 128), jnp.int32)
     for r in range(16):
@@ -346,14 +361,14 @@
         part, base = (0, g * 256) if g < 9 else (1, (g - 9) * 256)
         a = qkv_ref[part, :, base:base + 128].astype(f32)
         b = qkv_ref[part, :, base + 128:base + 256].astype(f32)
-        lo = (a * cos_t - b * sin_t).astype(bf16).astype(f32)
-        hi = (b * cos_t + a * sin_t).astype(bf16).astype(f32)
+        lower = (a * cos_t - b * sin_t).astype(bf16).astype(f32)
+        upper = (b * cos_t + a * sin_t).astype(bf16).astype(f32)
         if g < 16:
-            qs[:, g, 0:128] = lo
-            qs[:, g, 128:256] = hi
+            qs[:, g, 0:128] = lower
+            qs[:, g, 128:256] = upper
         else:
-            kns[:, 0:128] = lo
-            kns[:, 128:256] = hi
+            kns[:, 0:128] = lower
+            kns[:, 128:256] = upper
     vns[...] = qkv_ref[1, :, 2048:2304].astype(f32)
 
     row16 = lax.broadcasted_iota(jnp.int32, (16, 256), 0)
@@ -363,11 +378,11 @@
         s = lax.rem(r, SLOTS)
         nxt = r + AHEAD
 
-        @pl.when(nxt < n)
+        @pl.when(nxt < hi)
         def _():
             s2 = lax.rem(nxt, SLOTS)
 
-            @pl.when(nxt >= SLOTS)
+            @pl.when(nxt - SLOTS >= lo)
             def _():
                 k_out(nxt - SLOTS, s2).wait()
                 v_out(nxt - SLOTS, s2).wait()
@@ -395,29 +410,33 @@
         osc[r] = jnp.dot(pr, vb[s], preferred_element_type=f32).astype(bf16).astype(f32)
         return 0
 
-    lax.fori_loop(0, n, body, 0)
+    lax.fori_loop(lo, hi, body, 0)
     for g in range(16):
         o_ref[:, 256 * g:256 * (g + 1)] = osc[:, g, :].astype(bf16)
-    for r in range(n - SLOTS, n):
+    o_out = local_copy(o_ref, o_hbm, osem)
+    o_out.start()
+    for r in range(max(lo, hi - SLOTS), hi):
         k_out(r, r % SLOTS).wait()
         v_out(r, r % SLOTS).wait()
-
-
-def attend(lens, qkv, kc, vc):
+    o_out.wait()
+
+
+def attend(lo, hi, lens, qkv, kc, vc, *prev):
     anyspec = pl.BlockSpec(memory_space=pltpu.HBM)
-    vspec = pl.BlockSpec(memory_space=pltpu.VMEM)
     dma = pltpu.SemaphoreType.DMA
     n, t_len, hd = kc.shape
     return pl.pallas_call(
-        attend_kernel,
+        functools.partial(attend_kernel, lo, hi),
         out_shape=[
             jax.ShapeDtypeStruct(kc.shape, bf16),
             jax.ShapeDtypeStruct(vc.shape, bf16),
             jax.ShapeDtypeStruct((n, 4096), bf16),
         ],
-        in_specs=[anyspec] * 4,
-        out_specs=[anyspec, anyspec, vspec],
+        in_specs=[anyspec] * (4 + len(prev)),
+        out_specs=[anyspec] * 3,
+        input_output_aliases={4: 0, 5: 1} if prev else {},
         scratch_shapes=[
+            pltpu.VMEM((n, 4096), bf16),
             pltpu.VMEM((SLOTS, t_len, hd), bf16),
             pltpu.VMEM((SLOTS, t_len, hd), bf16),
             pltpu.SMEM((n,), jnp.int32),
@@ -426,21 +445,68 @@
             pltpu.VMEM((n, hd), f32),
             pltpu.VMEM((n, hd), f32),
             pltpu.VMEM((n, 16, hd), f32),
-            dma((SLOTS,)), dma((SLOTS,)), dma((SLOTS,)), dma((SLOTS,)), dma((2,)),
+            dma((SLOTS,)), dma((SLOTS,)), dma((SLOTS,)), dma((SLOTS,)), dma((2,)), dma,
         ],
         compiler_params=pltpu.CompilerParams(vmem_limit_bytes=VMEM_LIMIT),
-        cost_estimate=pl.CostEstimate(flops=40_000_000_000, bytes_accessed=134_000_000, transcendentals=1_000_000),
-        name="attend",
-    )(lens, qkv, kc, vc)
-
-
-UNITS = ((0, 0, 128), (1, 0, 128), (2, 0, 64), (3, 0, 64), (2, 64, 64), (3, 64, 64))
-NU = len(UNITS)
-
-
-def out_proj_kernel(o_ref, x_hbm, d_ref, r_ref, wao_ref, wmo_ref, y_ref,
-                    x_ref, db, rb, wao, wmo, ab, ob, zs, zk, zr,
-                    xsem, dsem, rsem, waosem, wmosem, a1s, a1r, a2s, a2r, a3s, a3r,
+        cost_estimate=pl.CostEstimate(flops=2_500_000_000 * (hi - lo), bytes_accessed=8_400_000 * (hi - lo), transcendentals=1_000_000),
+        name=f"attend{lo}",
+    )(lens, qkv, kc, vc, *prev)
+
+
+NA = 3
+
+
+def act_kernel(d_ref, r0_ref, r_ref, a_hbm, db, rb, a_ref, dsem, rsem, asem):
+    def d_in(i):
+        return local_copy(d_ref.at[i], db.at[i], dsem.at[i])
+
+    def r_in(i):
+        return local_copy(r_ref.at[i - 1] if i else r0_ref.at[0], rb.at[i], rsem.at[i])
+
+    def a_out(t):
+        return local_copy(a_ref.at[t], a_hbm.at[t], asem.at[t])
+
+    for i in range(2 * NA):
+        d_in(i).start()
+        r_in(i).start()
+
+    def total(i):
+        d_in(i).wait()
+        r_in(i).wait()
+        return (db[i] + rb[i]).astype(bf16).astype(f32)
+
+    for t in range(NA):
+        a_ref[t] = (jax.nn.silu(total(2 * t)) * total(2 * t + 1)).astype(bf16)
+        if t:
+            a_out(t - 1).start()
+    a_out(NA - 1).start()
+    for t in range(NA):
+        a_out(t).wait()
+
+
+def act(d, r0, r):
+    anyspec = pl.BlockSpec(memory_space=pltpu.HBM)
+    dma = pltpu.SemaphoreType.DMA
+    return pl.pallas_call(
+        act_kernel,
+        out_shape=jax.ShapeDtypeStruct((NA, 128, TILE), bf16),
+        in_specs=[anyspec] * 3,
+        out_specs=anyspec,
+        scratch_shapes=[
+            pltpu.VMEM((2 * NA, 128, TILE), f32),
+            pltpu.VMEM((2 * NA, 128, TILE), f32),
+            pltpu.VMEM((NA, 128, TILE), bf16),
+            dma((2 * NA,)), dma((2 * NA,)), dma((NA,)),
+        ],
+        compiler_params=pltpu.CompilerParams(vmem_limit_bytes=VMEM_LIMIT),
+        cost_estimate=pl.CostEstimate(flops=5_000_000, bytes_accessed=4_000_000, transcendentals=200_000),
+        name="act",
+    )(d, r0, r)
+
+
+def out_proj_kernel(o1_hbm, o2_hbm, x_hbm, d_ref, r_ref, ao_ref, ax_ref, wao_ref, wmo_ref, y_ref,
+                    o1_ref, o2_ref, o_ref, x_ref, db, rb, wao, wmo, ab, ob, zs, zk, zr,
+                    osem, xsem, dsem, rsem, asem, waosem, wmosem, pss, psr, fss, fsr, e_s, e_r,
                     o0s, o0r, o1s, o1r, o2s, o2r, o3s, o3r, zss, zrs):
     x = lax.axis_index("x")
     yz = lax.axis_index("yz")
@@ -456,18 +522,23 @@
     for dev in (partner, xpeer, ypeer):
         pl.semaphore_signal(barrier, inc=1, device_id=dev, device_id_type=MESH)
 
-    def d_in(i):
-        return local_copy(d_ref.at[i], db.at[i], dsem.at[i])
-
-    def r_in(i):
-        return local_copy(r_ref.at[i], rb.at[i], rsem.at[i])
-
-    for i in range(NT):
-        d_in(i).start()
-        r_in(i).start()
+    o_in = [local_copy(o1_hbm, o1_ref, osem.at[0]), local_copy(o2_hbm, o2_ref, osem.at[1])]
+    for c in o_in:
+        c.start()
+    first = pl.ds(0, NA)
+    own_in = local_copy(ao_ref, ab.at[x, first], asem.at[0])
+    chip_in = local_copy(ax_ref, ab.at[x_chip, first], asem.at[1])
+    own_in.start()
+    chip_in.start()
+    loads = [local_copy(d_ref.at[pl.ds(2 * NA, 2)], db, dsem), local_copy(r_ref, rb, rsem)]
+    for c in loads:
+        c.start()
+    for c in o_in:
+        c.wait()
     x_in = local_copy(x_hbm, x_ref, xsem)
     x_in.start()
-    order = (x, x_core, x_chip, x_diag)
+
+    order = (x, x_chip, x_core, x_diag)
 
     def wmo_in(n, t):
         rows = pl.multiple_of(order[n] * 2048 + t * TILE, TILE)
@@ -479,162 +550,148 @@
         for t in range(4):
             wmo_in(n, t).start()
 
-    def a_tile(t):
-        for i in (2 * t, 2 * t + 1):
-            d_in(i).wait()
-            r_in(i).wait()
-        gate = (db[2 * t] + rb[2 * t]).astype(bf16).astype(f32)
-        up = (db[2 * t + 1] + rb[2 * t + 1]).astype(bf16).astype(f32)
-        ab[x, t] = (jax.nn.silu(gate) * up).astype(bf16)
-
-    def unit(owner, u):
-        t, r0, n = UNITS[u]
-        return ab.at[owner, t, pl.ds(r0, n)]
-
-    def a_part(u):
-        return remote_copy(unit(x, u), unit(x, u), a1s.at[u], a1r.at[u], partner)
-
-    def a_chip(u):
-        return remote_copy(unit(x, u), unit(x, u), a2s.at[u], a2r.at[u], xpeer)
-
-    def a_fwd(u):
-        return remote_copy(unit(x_chip, u), unit(x_chip, u), a3s.at[u], a3r.at[u], partner)
-
-    def a_send(u):
-        a_chip(u).start()
-        a_part(u).start()
-
-    def o_block(b):
-        return ob.at[pl.ds(2 * b, 2)]
-
+    wmo_start(0)
+    row = lax.broadcasted_iota(jnp.int32, (16, 4096), 0)
+    o_ref[...] = jnp.where(row < SPLIT, o1_ref[...].astype(f32), o2_ref[...].astype(f32)).astype(bf16)
     own_half = pl.multiple_of(yz * 2048, 2048)
     peer_half = pl.multiple_of((1 - yz) * 2048, 2048)
     mine = 2 * x + yz
+    theirs = 2 * x + 1 - yz
+    ob[mine] = o_ref[:, pl.ds(own_half, 2048)]
+
+    for c in loads:
+        c.wait()
+    gate = (db[0] + rb[0]).astype(bf16).astype(f32)
+    up = (db[1] + rb[1]).astype(bf16).astype(f32)
+    ab[x, NA] = (jax.nn.silu(gate) * up).astype(bf16)
+    pl.semaphore_wait(barrier, 3)
+
     o_y = remote_copy(o_ref.at[:, pl.ds(peer_half, 2048)], ob.at[mine], o0s, o0r, ypeer)
-    o_part = remote_copy(o_block(x), o_block(x), o1s, o1r, partner)
-    o_chip = remote_copy(o_block(x), o_block(x), o2s, o2r, xpeer)
-    o_fwd = remote_copy(o_block(x_chip), o_block(x_chip), o3s, o3r, partner)
+
+    def o_hop(k, ss, rs, dev, owner):
+        block = ob.at[2 * owner + (yz if k == 0 else 1 - yz)]
+        return remote_copy(block, block, ss.at[k], rs.at[k], dev)
+
+    o_part = [o_hop(k, o1s, o1r, partner, x) for k in range(2)]
+    o_chip = [o_hop(k, o2s, o2r, xpeer, x) for k in range(2)]
+    o_fwd = [o_hop(k, o3s, o3r, partner, x_chip) for k in range(2)]
+
+    def a_hop(owner, tiles, ss, rs, k, dev):
+        block = ab.at[owner, tiles]
+        return remote_copy(block, block, ss.at[k], rs.at[k], dev)
+
+    last = pl.ds(NA, 1)
+    a_part = [a_hop(x, first, pss, psr, 0, partner), a_hop(x, last, pss, psr, 1, partner)]
+    a_fwd = [a_hop(x_chip, first, fss, fsr, 0, partner), a_hop(x_chip, last, fss, fsr, 1, partner)]
+    a_chip = remote_copy(ab.at[x, last], ab.at[x, last], e_s, e_r, xpeer)
+
+    o_y.start()
+    o_chip[0].start()
+    a_chip.start()
+    o_part[0].start()
+    a_part[1].start()
+    own_in.wait()
+    a_part[0].start()
+    chip_in.wait()
+    a_fwd[0].start()
+    wmo_start(1)
+    wmo_start(2)
 
     mc = pl.multiple_of((1 - yz) * 512, 512)
     kc = pl.multiple_of(yz * 512, 512)
 
-    def mlp(n, u, wait=True, first=False):
-        t, r0, m = UNITS[u]
-        rows = pl.ds(r0, m)
-        if wait:
-            wmo_in(n, t).wait()
-        a = ab[order[n], t, rows]
-        w = wmo.at[4 * n + t]
-        ps = jnp.dot(a, w[:, pl.ds(mc, 512)], preferred_element_type=f32)
-        zs[rows] = ps if first else zs[rows] + ps
-        pk = jnp.dot(a, w[:, pl.ds(kc, 512)], preferred_element_type=f32)
-        zk[rows] = pk if first else zk[rows] + pk
-
-    def mlp_tile(n, t, first=False):
+    def mlp(n, t, init=False):
         wmo_in(n, t).wait()
         a = ab[order[n], t]
         w = wmo.at[4 * n + t]
         ps = jnp.dot(a, w[:, pl.ds(mc, 512)], preferred_element_type=f32)
-        zs[...] = ps if first else zs[...] + ps
+        zs[...] = ps if init else zs[...] + ps
         pk = jnp.dot(a, w[:, pl.ds(kc, 512)], preferred_element_type=f32)
-        zk[...] = pk if first else zk[...] + pk
-
-    a_tile(0)
-    ob[mine] = o_ref[:, pl.ds(own_half, 2048)]
-    pl.semaphore_wait(barrier, 3)
-    o_y.start()
-    a_send(0)
-    a_tile(1)
-    wmo_start(0)
-    a_tile(2)
-    a_send(1)
-    a_tile(3)
-    wmo_start(1)
-    mlp_tile(0, 0, first=True)
-    mlp_tile(0, 1)
+        zk[...] = pk if init else zk[...] + pk
+
+    mlp(0, 0, init=True)
+    mlp(0, 1)
+    mlp(0, 2)
+    mlp(0, 3)
     o_y.wait()
-    o_chip.start()
-    o_part.start()
-    for u in range(2, NU):
-        a_send(u)
-    wmo_start(2)
+    o_chip[1].start()
+    o_part[1].start()
+    wmo_start(3)
     wao_in.start()
-    mlp_tile(0, 2)
-    mlp_tile(0, 3)
-    a_part(0).wait()
-    mlp_tile(1, 0)
-    a_part(1).wait()
-    mlp_tile(1, 1)
-    a_chip(0).wait()
-    a_fwd(0).start()
-    wmo_start(3)
+    mlp(1, 0)
+    mlp(1, 1)
+    o_chip[0].wait()
+    o_fwd[0].start()
+    mlp(1, 2)
+    a_part[0].wait()
     mlp(2, 0)
-    for u in range(2, NU):
-        a_part(u).wait()
-    mlp_tile(1, 2)
-    mlp_tile(1, 3)
-    a_chip(1).wait()
-    a_fwd(1).start()
     mlp(2, 1)
-    a_fwd(0).wait()
+    a_chip.wait()
+    a_fwd[1].start()
+    mlp(1, 3)
+    mlp(2, 2)
+    a_part[1].wait()
+    mlp(2, 3)
+    a_fwd[0].wait()
     mlp(3, 0)
-    o_part.wait()
-    o_chip.wait()
-    o_fwd.start()
-    a_fwd(1).wait()
     mlp(3, 1)
+    mlp(3, 2)
+    a_fwd[1].wait()
+    mlp(3, 3)
+
+    chip = x // 2
+    own_rows = pl.multiple_of(64 * chip, 64)
+    chip_rows = pl.multiple_of(32 * x_chip, 32)
+    diag_rows = pl.multiple_of(32 * x_diag, 32)
+
+    def z_y(c, base, m):
+        rows = pl.ds(base, m)
+        return remote_copy(zs.at[rows], zr.at[rows], zss.at[c], zrs.at[c], ypeer)
+
+    def attn_rows(base, m):
+        rows = pl.ds(base, m)
+        attn = ob[pl.ds(base // 16, m // 16)].reshape(m, 2048)
+        zs[rows] += jnp.dot(attn, wao[:, pl.ds(mc, 512)], preferred_element_type=f32)
+        zk[rows] += jnp.dot(attn, wao[:, pl.ds(kc, 512)], preferred_element_type=f32)
+
+    blocks = ((own_rows, 64), (chip_rows, 32), (diag_rows, 32))
     wao_in.wait()
-    a_chip(2).wait()
-    a_fwd(2).start()
-    mlp(2, 2)
-    o_fwd.wait()
-    attn = ob[...].reshape(128, 2048)
-    zs[...] += jnp.dot(attn, wao[:, pl.ds(mc, 512)], preferred_element_type=f32)
-    zk[...] += jnp.dot(attn, wao[:, pl.ds(kc, 512)], preferred_element_type=f32)
-
-    def z_y(c):
-        rows = pl.ds(64 * c, 64)
-        return remote_copy(zs.at[rows], zr.at[rows], zss.at[c], zrs.at[c], ypeer)
-
-    a_chip(3).wait()
-    a_fwd(3).start()
-    mlp(2, 3)
-    a_fwd(2).wait()
-    mlp(3, 2)
-    a_fwd(3).wait()
-    mlp(3, 3)
-    z_y(0).start()
-    a_chip(4).wait()
-    a_fwd(4).start()
-    mlp(2, 4, wait=False)
-    a_chip(5).wait()
-    a_fwd(5).start()
-    mlp(2, 5, wait=False)
-    a_fwd(4).wait()
-    mlp(3, 4, wait=False)
-    a_fwd(5).wait()
-    mlp(3, 5, wait=False)
-    z_y(1).start()
+    for k in range(2):
+        o_part[k].wait()
+    attn_rows(*blocks[0])
+    z_y(0, *blocks[0]).start()
+    o_chip[1].wait()
+    o_fwd[1].start()
+    attn_rows(*blocks[1])
+    z_y(1, *blocks[1]).start()
+    for k in range(2):
+        o_fwd[k].wait()
+    attn_rows(*blocks[2])
+    z_y(2, *blocks[2]).start()
     x_in.wait()
-    for c in range(2):
-        z_y(c).wait()
-        rows = pl.ds(64 * c, 64)
+    for c, (base, m) in enumerate(blocks):
+        z_y(c, base, m).wait()
+        rows = pl.ds(base, m)
         y_ref[rows, :] = (x_ref[rows, :].astype(f32) + (zk[rows, :] + zr[rows, :])).astype(bf16)
 
 
-def out_proj(o, x_loc, d, r, wao, wmo):
+def out_proj(o1, o2, x_loc, d, r, a_own, a_chip, wao, wmo):
     anyspec = pl.BlockSpec(memory_space=pltpu.HBM)
     vspec = pl.BlockSpec(memory_space=pltpu.VMEM)
     dma = pltpu.SemaphoreType.DMA
+    two = dma((2,))
     return pl.pallas_call(
         out_proj_kernel,
         out_shape=jax.ShapeDtypeStruct((128, 512), bf16),
-        in_specs=[vspec, anyspec, anyspec, anyspec, anyspec, anyspec],
+        in_specs=[anyspec] * 9,
         out_specs=vspec,
         scratch_shapes=[
+            pltpu.VMEM((16, 4096), bf16),
+            pltpu.VMEM((16, 4096), bf16),
+            pltpu.VMEM((16, 4096), bf16),
             pltpu.VMEM((128, 512), bf16),
-            pltpu.VMEM((NT, 128, TILE), f32),
-            pltpu.VMEM((NT, 128, TILE), f32),
+            pltpu.VMEM((2, 128, TILE), f32),
+            pltpu.VMEM((2, 128, TILE), f32),
             pltpu.VMEM((2048, 1024), bf16),
             pltpu.VMEM((16, TILE, 1024), bf16),
             pltpu.VMEM((4, 4, 128, TILE), bf16),
@@ -642,15 +699,15 @@
             pltpu.VMEM((128, 512), f32),
             pltpu.VMEM((128, 512), f32),
             pltpu.VMEM((128, 512), f32),
-            dma, dma((NT,)), dma((NT,)), dma, dma((16,)),
-            dma((NU,)), dma((NU,)), dma((NU,)), dma((NU,)), dma((NU,)), dma((NU,)),
-            dma, dma, dma, dma, dma, dma, dma, dma, dma((2,)), dma((2,)),
+            two, dma, dma, dma, two, dma, dma((16,)),
+            two, two, two, two, dma, dma,
+            dma, dma, two, two, two, two, two, two, dma((3,)), dma((3,)),
         ],
         compiler_params=pltpu.CompilerParams(
-            collective_id=1, has_side_effects=True, vmem_limit_bytes=48 * 2 ** 20),
+            collective_id=1, has_side_effects=True, vmem_limit_bytes=VMEM_LIMIT - OUT_ROOM),
         cost_estimate=pl.CostEstimate(flops=3_000_000_000, bytes_accessed=26_000_000, transcendentals=0),
         name="out_proj",
-    )(o, x_loc, d, r, wao, wmo)
+    )(o1, o2, x_loc, d, r, a_own, a_chip, wao, wmo)
 
 
 def solution(mesh):
@@ -663,10 +720,15 @@
     swap = [(0, 2), (2, 0), (1, 3), (3, 1)]
 
     def local_layer(x_loc, gain_loc, wqkv_loc, wgate_loc, wup_loc, wao_loc, wmo_loc, kc_loc, vc_loc, len_loc):
-        qkv, s, d = in_proj(x_loc, gain_loc, wqkv_loc, wgate_loc, wup_loc)
-        r = lax.ppermute(s, "x", swap)
-        k_all, v_all, o = attend(len_loc, qkv, kc_loc, vc_loc)
-        y_loc = out_proj(o, x_loc, d, r, wao_loc, wmo_loc)
+        qkv, sa, sb, r0, d = in_proj(x_loc, gain_loc, wqkv_loc, wgate_loc, wup_loc)
+        ra = lax.ppermute(sa, "x", swap)
+        k_all, v_all, o1 = attend(0, SPLIT, len_loc, qkv, kc_loc, vc_loc)
+        sb, o1 = lax.optimization_barrier((sb, o1))
+        rb = lax.ppermute(sb, "x", swap)
+        a_own = act(d, r0, ra)
+        a_chip = lax.ppermute(a_own, "x", swap)
+        k_all, v_all, o2 = attend(SPLIT, 16, len_loc, qkv, kc_loc, vc_loc, k_all, v_all)
+        y_loc = out_proj(o1, o2, x_loc, d, rb, a_own, a_chip, wao_loc, wmo_loc)
         return y_loc, k_all, v_all
 
     in_specs = (row_spec, P(both_axes), in_w_spec, in_w_spec, in_w_spec, out_w_spec, out_w_spec, cache_spec, cache_spec, len_spec)

time: 103 us -> 101 us (0.981)
  local copies, waits for them, and re-layouts: 4.06 us -> 1.57 us
  starting transfers between devices: 0.58 us -> 2.65 us
  waiting for transfers between devices: 1.28 us -> 0.01 us
    pallas_call x1, Pallas kernels: 24 us -> 18.7 us  [out_proj(): pl.pallas_call(out_proj_kernel, out_shape=jax.ShapeDtypeStruct((128, 512)...]
    pallas_call x1 -> x3, Pallas kernels: 45.2 us -> 49.5 us  [the longest x2 46.8 us: attend(): pl.pallas_call(functools.partial(attend_kernel, lo, hi), out_shape=[jax.S...]
    unnamed x7 -> x1, local copies, waits for them, and re-layouts: 4.06 us -> 1.57 us
    ppermute x1 -> x3, starting transfers between devices: 0.58 us -> 2.65 us  [the longest x1 1.47 us: local_layer(): rb = lax.ppermute(sb, 'x', swap)]
    ppermute x1 -> x3, waiting for transfers between devices: 1.28 us -> 0.01 us  [the longest x1 0.01 us: local_layer(): ra = lax.ppermute(sa, 'x', swap)]
  transfers between devices with their start and end apart: 1 -> 3, of which waited for: 1 -> 0; matrix products, arithmetic and copies ran while one was open for 0% -> 0% of each run, Pallas kernels for 44% -> 49%
where the time goes in v3:
time: 101 us; the launch traced here: 100 us
  Pallas kernels  95.5 us (95%)
  starting transfers between devices  2.65 us (3%)
  local copies, waits for them, and re-layouts  1.57 us (2%)
    pallas_call x2, Pallas kernels, attend(): pl.pallas_call(functools.partial(attend_kernel, lo, hi), out_shape=[jax.S...  46.8 us
    pallas_call x1, Pallas kernels, in_proj(): pl.pallas_call(in_proj_kernel, out_shape=[jax.ShapeDtypeStruct((2, 16, NQ...  27.3 us
    pallas_call x1, Pallas kernels, out_proj(): pl.pallas_call(out_proj_kernel, out_shape=jax.ShapeDtypeStruct((128, 512)...  18.7 us
    pallas_call x1, Pallas kernels, act(): pl.pallas_call(act_kernel, out_shape=jax.ShapeDtypeStruct((NA, 128, TILE)...  2.68 us
  transfers between devices with their start and end apart: 3, of which 0 were waited for; matrix products, arithmetic and copies ran while one was open for 0% of the time, Pallas kernels for 49%

profile of v3, /device:TPU:0, one launch (start us, length us, event | category | flops | bytes accessed | tf_op | source)
XLA Modules:
  0.0 100.4 jit_solution(3050808188286043427)
XLA Ops:
  0.6 27.3 %in_proj.1 = (bf16[2,16,2304]{2,1,0:T(8,128)(2,1)}, f32[5,128,512]{2,1,0:T(8,128)}, f32[2,128,512]{2,1,0:T(8,128)}, f32[1,128,512]{2,1,0:T(8,128)}, f32[8,128,512]{2,1,0:T(8,128)}) custom-call(bf16[128,512]{1,0:T(8,128)(2,1)} %x_hbm.3, bf16[512]{0:T(512)(128)(2,1)} %g_hbm.1, bf16[1024,2304]{1,0:T(8,128)(2,1)} %wq_ref.1, bf16[1024,8192]{1,0:T(8,128)(2,1)} %wg_ref.1, ...), custom_call_target="tpu_custom_call" | custom-call | flops 5000000000 | bytes 45000000 | tf_op jit(solution)/shard_map/in_proj/pallas_call | solution.py:275
  28.0 0.6 collective-permute-start.1
  28.5 28.8 %attend0.1 = (bf16[16,4096,256]{2,1,0:T(8,128)(2,1)}, bf16[16,4096,256]{2,1,0:T(8,128)(2,1)}, bf16[16,4096]{1,0:T(8,128)(2,1)}) custom-call(s32[16]{0:T(128)} %len_hbm.3, bf16[2,16,2304]{2,1,0:T(8,128)(2,1)} %get-tuple-element.17.qkv_hbm, bf16[16,4096,256]{2,1,0:T(8,128)(2,1)} %k_ref.3, bf16[16,4096,256]{2,1,0:T(8,128)(2,1)} %v_ref.3), custom_call_target="tpu_custom_call" | custom-call | flops 24999999488 | bytes 84000000 | tf_op jit(solution)/shard_map/attend0/pallas_call | solution.py:428
  57.3 1.5 %collective-permute-start = (f32[2,128,512]{2,1,0:T(8,128)}, f32[2,128,512]{2,1,0:T(8,128)}, u32[]{:S(2)}, u32[]{:S(2)}) collective-permute-start(f32[2,128,512]{2,1,0:T(8,128)} %get-tuple-element.24), channel_id=1, source_target_pairs={{0,2},{2,0},{1,3},{3,1},{4,6},{6,4},{5,7},{7,5}} | collective-permute-start | bytes 1572872 | tf_op jit(solution)/shard_map/ppermute | solution.py:727
  58.8 0.0 collective-permute-done.1.r_ref
  58.8 2.7 %act.1.ao_ref = bf16[3,128,512]{2,1,0:T(8,128)(2,1)} custom-call(f32[8,128,512]{2,1,0:T(8,128)} %get-tuple-element.23.d_ref, f32[1,128,512]{2,1,0:T(8,128)} %get-tuple-element.25.r0_ref, f32[5,128,512]{2,1,0:T(8,128)} %collective-permute-done.1.r_ref), custom_call_target="tpu_custom_call" | custom-call | flops 5000000 | bytes 4000000 | tf_op jit(solution)/shard_map/act/pallas_call | solution.py:490
  61.5 0.6 collective-permute-start.2
  62.1 18.0 %attend10.1 = (bf16[16,4096,256]{2,1,0:T(8,128)(2,1)}, bf16[16,4096,256]{2,1,0:T(8,128)(2,1)}, bf16[16,4096]{1,0:T(8,128)(2,1)}) custom-call(s32[16]{0:T(128)} %len_hbm.3, bf16[2,16,2304]{2,1,0:T(8,128)(2,1)} %get-tuple-element.17.qkv_hbm, bf16[16,4096,256]{2,1,0:T(8,128)(2,1)} %k_ref.3, ...), custom_call_target="tpu_custom_call", output_to_operand_aliasing={{0}: (4, {}), {1}: (5, {})} | custom-call | flops 15000000512 | bytes 50400000 | tf_op jit(solution)/shard_map/attend10/pallas_call | solution.py:428
  80.1 0.0 collective-permute-done.r_ref
  80.1 0.0 collective-permute-done.2.ax_ref
  80.1 18.7 %out_proj.1 = bf16[128,512]{1,0:T(8,128)(2,1)} custom-call(bf16[16,4096]{1,0:T(8,128)(2,1)} %get-tuple-element.19.o1_hbm, bf16[16,4096]{1,0:T(8,128)(2,1)} %get-tuple-element.22.o2_hbm, bf16[128,512]{1,0:T(8,128)(2,1)} %x_hbm.3, f32[8,128,512]{2,1,0:T(8,128)} %get-tuple-element.23.d_ref, f32[2,128,512]{2,1,0:T(8,128)} %collective-permute-done.r_ref, ...), custom_call_target="tpu_custom_call" | custom-call | flops 3000000000 | bytes 26000000 | tf_op jit(solution)/shard_map/out_proj/pallas_call | solution.py:683
  98.8 1.6 %copy.18 = bf16[128,512]{1,0:T(8,128)(2,1)} copy(bf16[128,512]{1,0:T(8,128)(2,1)} %out_proj.1) | data formatting | bytes 262144
Async XLA Ops:
  28.0 30.8 %collective-permute-start.1 = (f32[5,128,512]{2,1,0:T(8,128)}, f32[5,128,512]{2,1,0:T(8,128)}, u32[]{:S(2)}, u32[]{:S(2)}) collective-permute-start(f32[5,128,512]{2,1,0:T(8,128)} %get-tuple-element.26), channel_id=1, source_target_pairs={{0,2},{2,0},{1,3},{3,1},{4,6},{6,4},{5,7},{7,5}} | collective-permute-start | bytes 3932168 | tf_op jit(solution)/shard_map/ppermute | solution.py:724
  57.3 22.8 %collective-permute-start = (f32[2,128,512]{2,1,0:T(8,128)}, f32[2,128,512]{2,1,0:T(8,128)}, u32[]{:S(2)}, u32[]{:S(2)}) collective-permute-start(f32[2,128,512]{2,1,0:T(8,128)} %get-tuple-element.24), channel_id=1, source_target_pairs={{0,2},{2,0},{1,3},{3,1},{4,6},{6,4},{5,7},{7,5}} | collective-permute-start | bytes 1572872 | tf_op jit(solution)/shard_map/ppermute | solution.py:727
  61.5 18.6 %collective-permute-start.2 = (bf16[3,128,512]{2,1,0:T(8,128)(2,1)}, bf16[3,128,512]{2,1,0:T(8,128)(2,1)}, u32[]{:S(2)}, u32[]{:S(2)}) collective-permute-start(bf16[3,128,512]{2,1,0:T(8,128)(2,1)} %act.1.ao_ref), channel_id=1, source_target_pairs={{0,2},{2,0},{1,3},{3,1},{4,6},{6,4},{5,7},{7,5}} | collective-permute-start | bytes 1179656 | tf_op jit(solution)/shard_map/ppermute | solution.py:729

commit v4 on v3

--- a/solution.py
+++ b/solution.py
@@ -9,6 +9,9 @@
 
 MESH = pl.DeviceIdType.MESH
 VMEM_LIMIT = 67043328
+ROWS = 128
+HD = 256
+LOC = 512
 OUT_ROOM = 8000000
 TILE = 512
 SA = 5
@@ -93,7 +96,7 @@
     xf = x_ref[...].astype(f32)
     s1 = jnp.sum(xf, axis=1, keepdims=True)
     s2 = jnp.sum(xf * xf, axis=1, keepdims=True)
-    lane = lax.broadcasted_iota(jnp.int32, (128, 128), 1)
+    lane = lax.broadcasted_iota(jnp.int32, (ROWS, ROWS), 1)
     stat = jnp.where(lane == 0, s1, s2).T
     st[me] = stat[0:8]
 
@@ -110,16 +113,16 @@
         src = 2 * ox + oy
         remote_copy(st.at[me], stx.at[src], sts_sem.at[n], str_sem.at[src], {"x": ox, "yz": oy}).wait()
     tot = jnp.sum(stx[...], axis=0)
-    tot = jnp.concatenate([tot, jnp.zeros((120, 128), f32)], axis=0).T
+    tot = jnp.concatenate([tot, jnp.zeros((120, ROWS), f32)], axis=0).T
     mean = tot[:, 0:1] / d_model
     var = tot[:, 1:2] / d_model - mean * mean
     rstd = lax.rsqrt(var + 1e-6)
-    own_cols = pl.multiple_of(yz * 512, 512)
-    peer_cols = pl.multiple_of((1 - yz) * 512, 512)
-    h[:, pl.ds(own_cols, 512)] = ((xf - mean) * rstd * g_ref[...].astype(f32).reshape(1, 512)).astype(bf16)
+    own_cols = pl.multiple_of(yz * LOC, LOC)
+    peer_cols = pl.multiple_of((1 - yz) * LOC, LOC)
+    h[:, pl.ds(own_cols, LOC)] = ((xf - mean) * rstd * g_ref[...].astype(f32).reshape(1, LOC)).astype(bf16)
     x_send.wait()
     g_send.wait()
-    h[:, pl.ds(peer_cols, 512)] = ((xr[...].astype(f32) - mean) * rstd * gr[...].astype(f32).reshape(1, 512)).astype(bf16)
+    h[:, pl.ds(peer_cols, LOC)] = ((xr[...].astype(f32) - mean) * rstd * gr[...].astype(f32).reshape(1, LOC)).astype(bf16)
 
     for slot in range(W_FIRST, W_AHEAD):
         w_start(slot)
@@ -276,33 +279,33 @@
         in_proj_kernel,
         out_shape=[
             jax.ShapeDtypeStruct((2, 16, NQ * QC), bf16),
-            jax.ShapeDtypeStruct((SA, 128, TILE), f32),
-            jax.ShapeDtypeStruct((NT - 1 - SA, 128, TILE), f32),
-            jax.ShapeDtypeStruct((1, 128, TILE), f32),
-            jax.ShapeDtypeStruct((NT, 128, TILE), f32),
+            jax.ShapeDtypeStruct((SA, ROWS, TILE), f32),
+            jax.ShapeDtypeStruct((NT - 1 - SA, ROWS, TILE), f32),
+            jax.ShapeDtypeStruct((1, ROWS, TILE), f32),
+            jax.ShapeDtypeStruct((NT, ROWS, TILE), f32),
         ],
         in_specs=[anyspec] * 5,
         out_specs=[anyspec] * 5,
         scratch_shapes=[
             pltpu.VMEM((NQ, 1024, QC), bf16),
             pltpu.VMEM((4 * NT, 1024, TILE), bf16),
-            pltpu.VMEM((128, 512), bf16),
-            pltpu.VMEM((512,), bf16),
-            pltpu.VMEM((128, 512), bf16),
-            pltpu.VMEM((512,), bf16),
+            pltpu.VMEM((ROWS, LOC), bf16),
+            pltpu.VMEM((LOC,), bf16),
+            pltpu.VMEM((ROWS, LOC), bf16),
+            pltpu.VMEM((LOC,), bf16),
             pltpu.VMEM((2, 16, NQ * QC), bf16),
-            pltpu.VMEM((8, 8, 128), f32),
-            pltpu.VMEM((8, 8, 128), f32),
-            pltpu.VMEM((128, 1024), bf16),
+            pltpu.VMEM((8, 8, ROWS), f32),
+            pltpu.VMEM((8, 8, ROWS), f32),
+            pltpu.VMEM((ROWS, 1024), bf16),
             pltpu.VMEM((NQ, 4, 32, QC), f32),
             pltpu.VMEM((NQ, 2, 32, QC), f32),
             pltpu.VMEM((NQ, 32, QC), f32),
             pltpu.VMEM((NQ, 32, QC), f32),
             pltpu.VMEM((NQ, 32, QC), bf16),
             pltpu.VMEM((NQ, 16, QC), bf16),
-            pltpu.VMEM((2 * NT, 128, TILE), f32),
-            pltpu.VMEM((2 * NT, 128, TILE), f32),
-            pltpu.VMEM((2 * NT, 128, TILE), f32),
+            pltpu.VMEM((2 * NT, ROWS, TILE), f32),
+            pltpu.VMEM((2 * NT, ROWS, TILE), f32),
+            pltpu.VMEM((2 * NT, ROWS, TILE), f32),
             dma((NQ,)), dma((4 * NT,)), dma, dma, dma, dma, dma((7,)), dma((8,)),
             dma((NQ, 2)), dma((NQ, 2)), dma((NQ,)), dma((NQ,)), dma((NQ,)), dma((NQ,)),
             dma((2 * NT,)), dma((2 * NT,)), dma((2 * NT,)), dma, dma, dma, dma, dma,
@@ -349,29 +352,29 @@
     for r in range(lo + 2, lo + AHEAD):
         k_in(r, r % SLOTS).start()
         v_in(r, r % SLOTS).start()
-    row = lax.broadcasted_iota(jnp.int32, (16, 128), 0)
-    lens = jnp.zeros((16, 128), jnp.int32)
+    row = lax.broadcasted_iota(jnp.int32, (16, ROWS), 0)
+    lens = jnp.zeros((16, ROWS), jnp.int32)
     for r in range(16):
         lens = jnp.where(row == r, len_ref[r], lens)
-    half = lax.broadcasted_iota(jnp.int32, (16, 128), 1).astype(f32)
-    angles = lens.astype(f32) * 10000.0 ** (-half / 128)
+    half = lax.broadcasted_iota(jnp.int32, (16, ROWS), 1).astype(f32)
+    angles = lens.astype(f32) * 10000.0 ** (-half / ROWS)
     cos_t = jnp.cos(angles)
     sin_t = jnp.sin(angles)
     for g in range(17):
-        part, base = (0, g * 256) if g < 9 else (1, (g - 9) * 256)
-        a = qkv_ref[part, :, base:base + 128].astype(f32)
-        b = qkv_ref[part, :, base + 128:base + 256].astype(f32)
+        part, base = (0, g * HD) if g < 9 else (1, (g - 9) * HD)
+        a = qkv_ref[part, :, base:base + ROWS].astype(f32)
+        b = qkv_ref[part, :, base + ROWS:base + HD].astype(f32)
         lower = (a * cos_t - b * sin_t).astype(bf16).astype(f32)
         upper = (b * cos_t + a * sin_t).astype(bf16).astype(f32)
         if g < 16:
-            qs[:, g, 0:128] = lower
-            qs[:, g, 128:256] = upper
+            qs[:, g, 0:ROWS] = lower
+            qs[:, g, ROWS:HD] = upper
         else:
-            kns[:, 0:128] = lower
-            kns[:, 128:256] = upper
+            kns[:, 0:ROWS] = lower
+            kns[:, ROWS:HD] = upper
     vns[...] = qkv_ref[1, :, 2048:2304].astype(f32)
 
-    row16 = lax.broadcasted_iota(jnp.int32, (16, 256), 0)
+    row16 = lax.broadcasted_iota(jnp.int32, (16, HD), 0)
     pos = lax.broadcasted_iota(jnp.int32, (16, t_len), 1)
 
     def body(r, _):
@@ -395,24 +398,24 @@
         k_in(r, s).wait()
         krow = kb[s, pl.ds(base, 16), :]
         kb[s, pl.ds(base, 16), :] = jnp.where(hit, kns[pl.ds(r, 1), :].astype(bf16), krow)
-        q = qs[r].astype(bf16)
-        sc = lax.dot_general(q, kb[s], (((1,), (1,)), ((), ())), preferred_element_type=f32) * (256 ** -0.5)
-        k_out(r, s).start()
         v_in(r, s).wait()
         vrow = vb[s, pl.ds(base, 16), :]
         vb[s, pl.ds(base, 16), :] = jnp.where(hit, vns[pl.ds(r, 1), :].astype(bf16), vrow)
+        q = qs[r].astype(bf16)
+        sc = lax.dot_general(q, kb[s], (((1,), (1,)), ((), ())), preferred_element_type=f32) * (HD ** -0.5)
+        k_out(r, s).start()
+        v_out(r, s).start()
         sc = jnp.where(pos <= p, sc, -1e30)
         m = jnp.max(sc, axis=1, keepdims=True)
         e = jnp.exp(sc - m)
         den = jnp.sum(e, axis=1, keepdims=True)
         pr = (e / den).astype(bf16)
-        v_out(r, s).start()
         osc[r] = jnp.dot(pr, vb[s], preferred_element_type=f32).astype(bf16).astype(f32)
         return 0
 
     lax.fori_loop(lo, hi, body, 0)
     for g in range(16):
-        o_ref[:, 256 * g:256 * (g + 1)] = osc[:, g, :].astype(bf16)
+        o_ref[:, HD * g:HD * (g + 1)] = osc[:, g, :].astype(bf16)
     o_out = local_copy(o_ref, o_hbm, osem)
     o_out.start()
     for r in range(max(lo, hi - SLOTS), hi):
@@ -489,13 +492,13 @@
     dma = pltpu.SemaphoreType.DMA
     return pl.pallas_call(
         act_kernel,
-        out_shape=jax.ShapeDtypeStruct((NA, 128, TILE), bf16),
+        out_shape=jax.ShapeDtypeStruct((NA, ROWS, TILE), bf16),
         in_specs=[anyspec] * 3,
         out_specs=anyspec,
         scratch_shapes=[
-            pltpu.VMEM((2 * NA, 128, TILE), f32),
-            pltpu.VMEM((2 * NA, 128, TILE), f32),
-            pltpu.VMEM((NA, 128, TILE), bf16),
+            pltpu.VMEM((2 * NA, ROWS, TILE), f32),
+            pltpu.VMEM((2 * NA, ROWS, TILE), f32),
+            pltpu.VMEM((NA, ROWS, TILE), bf16),
             dma((2 * NA,)), dma((2 * NA,)), dma((NA,)),
         ],
         compiler_params=pltpu.CompilerParams(vmem_limit_bytes=VMEM_LIMIT),
@@ -540,17 +543,22 @@
 
     order = (x, x_chip, x_core, x_diag)
 
-    def wmo_in(n, t):
+    halves = (pl.ds(pl.multiple_of((1 - yz) * LOC, LOC), LOC), pl.ds(pl.multiple_of(yz * LOC, LOC), LOC))
+    accs = (zs, zk)
+
+    def wmo_in(half, n, t):
         rows = pl.multiple_of(order[n] * 2048 + t * TILE, TILE)
-        return local_copy(wmo_ref.at[pl.ds(rows, TILE), :], wmo.at[4 * n + t], wmosem.at[4 * n + t])
-
-    wao_in = local_copy(wao_ref, wao, waosem)
-
-    def wmo_start(n):
+        k = 4 * n + t
+        return local_copy(wmo_ref.at[pl.ds(rows, TILE), halves[half]], wmo.at[half, k], wmosem.at[half, k])
+
+    def wao_in(half):
+        return local_copy(wao_ref.at[:, halves[half]], wao.at[half], waosem.at[half])
+
+    def wmo_start(half, n):
         for t in range(4):
-            wmo_in(n, t).start()
-
-    wmo_start(0)
+            wmo_in(half, n, t).start()
+
+    wmo_start(0, 0)
     row = lax.broadcasted_iota(jnp.int32, (16, 4096), 0)
     o_ref[...] = jnp.where(row < SPLIT, o1_ref[...].astype(f32), o2_ref[...].astype(f32)).astype(bf16)
     own_half = pl.multiple_of(yz * 2048, 2048)
@@ -586,58 +594,22 @@
     a_chip = remote_copy(ab.at[x, last], ab.at[x, last], e_s, e_r, xpeer)
 
     o_y.start()
+    a_chip.start()
     o_chip[0].start()
-    a_chip.start()
     o_part[0].start()
     a_part[1].start()
     own_in.wait()
     a_part[0].start()
     chip_in.wait()
     a_fwd[0].start()
-    wmo_start(1)
-    wmo_start(2)
-
-    mc = pl.multiple_of((1 - yz) * 512, 512)
-    kc = pl.multiple_of(yz * 512, 512)
-
-    def mlp(n, t, init=False):
-        wmo_in(n, t).wait()
-        a = ab[order[n], t]
-        w = wmo.at[4 * n + t]
-        ps = jnp.dot(a, w[:, pl.ds(mc, 512)], preferred_element_type=f32)
-        zs[...] = ps if init else zs[...] + ps
-        pk = jnp.dot(a, w[:, pl.ds(kc, 512)], preferred_element_type=f32)
-        zk[...] = pk if init else zk[...] + pk
-
-    mlp(0, 0, init=True)
-    mlp(0, 1)
-    mlp(0, 2)
-    mlp(0, 3)
-    o_y.wait()
-    o_chip[1].start()
-    o_part[1].start()
-    wmo_start(3)
-    wao_in.start()
-    mlp(1, 0)
-    mlp(1, 1)
-    o_chip[0].wait()
-    o_fwd[0].start()
-    mlp(1, 2)
-    a_part[0].wait()
-    mlp(2, 0)
-    mlp(2, 1)
-    a_chip.wait()
-    a_fwd[1].start()
-    mlp(1, 3)
-    mlp(2, 2)
-    a_part[1].wait()
-    mlp(2, 3)
-    a_fwd[0].wait()
-    mlp(3, 0)
-    mlp(3, 1)
-    mlp(3, 2)
-    a_fwd[1].wait()
-    mlp(3, 3)
+    wmo_start(0, 1)
+    wmo_start(0, 2)
+
+    def mlp(half, n, t, init=False):
+        wmo_in(half, n, t).wait()
+        acc = accs[half]
+        part = jnp.dot(ab[order[n], t], wmo[half, 4 * n + t], preferred_element_type=f32)
+        acc[...] = part if init else acc[...] + part
 
     chip = x // 2
     own_rows = pl.multiple_of(64 * chip, 64)
@@ -648,26 +620,63 @@
         rows = pl.ds(base, m)
         return remote_copy(zs.at[rows], zr.at[rows], zss.at[c], zrs.at[c], ypeer)
 
-    def attn_rows(base, m):
+    def attn_rows(half, base, m):
         rows = pl.ds(base, m)
         attn = ob[pl.ds(base // 16, m // 16)].reshape(m, 2048)
-        zs[rows] += jnp.dot(attn, wao[:, pl.ds(mc, 512)], preferred_element_type=f32)
-        zk[rows] += jnp.dot(attn, wao[:, pl.ds(kc, 512)], preferred_element_type=f32)
+        accs[half][rows] += jnp.dot(attn, wao[half], preferred_element_type=f32)
 
     blocks = ((own_rows, 64), (chip_rows, 32), (diag_rows, 32))
-    wao_in.wait()
+    for t in range(4):
+        mlp(0, 0, t, init=t == 0)
+    o_y.wait()
+    o_chip[1].start()
+    o_part[1].start()
+    wao_in(0).start()
+    wmo_start(0, 3)
+    wmo_start(1, 0)
+    wmo_start(1, 1)
+    for t in range(NA):
+        mlp(0, 1, t)
+    a_part[0].wait()
+    for t in range(NA):
+        mlp(0, 2, t)
+    a_chip.wait()
+    a_fwd[1].start()
+    mlp(0, 1, NA)
+    a_part[1].wait()
+    mlp(0, 2, NA)
+    o_chip[0].wait()
+    o_fwd[0].start()
+    wao_in(0).wait()
     for k in range(2):
         o_part[k].wait()
-    attn_rows(*blocks[0])
+    attn_rows(0, *blocks[0])
+    a_fwd[0].wait()
+    for t in range(NA):
+        mlp(0, 3, t)
+    a_fwd[1].wait()
+    mlp(0, 3, NA)
+    wmo_start(1, 2)
+    wmo_start(1, 3)
+    wao_in(1).start()
+    mlp(1, 0, 0, init=True)
     z_y(0, *blocks[0]).start()
     o_chip[1].wait()
     o_fwd[1].start()
-    attn_rows(*blocks[1])
+    attn_rows(0, *blocks[1])
+    mlp(1, 0, 1)
     z_y(1, *blocks[1]).start()
     for k in range(2):
         o_fwd[k].wait()
-    attn_rows(*blocks[2])
+    attn_rows(0, *blocks[2])
+    mlp(1, 0, 2)
     z_y(2, *blocks[2]).start()
+    mlp(1, 0, NA)
+    for n in range(1, 4):
+        for t in range(4):
+            mlp(1, n, t)
+    wao_in(1).wait()
+    attn_rows(1, 0, ROWS)
     x_in.wait()
     for c, (base, m) in enumerate(blocks):
         z_y(c, base, m).wait()
@@ -682,24 +691,24 @@
     two = dma((2,))
     return pl.pallas_call(
         out_proj_kernel,
-        out_shape=jax.ShapeDtypeStruct((128, 512), bf16),
+        out_shape=jax.ShapeDtypeStruct((ROWS, LOC), bf16),
         in_specs=[anyspec] * 9,
         out_specs=vspec,
         scratch_shapes=[
             pltpu.VMEM((16, 4096), bf16),
             pltpu.VMEM((16, 4096), bf16),
             pltpu.VMEM((16, 4096), bf16),
-            pltpu.VMEM((128, 512), bf16),
-            pltpu.VMEM((2, 128, TILE), f32),
-            pltpu.VMEM((2, 128, TILE), f32),
-            pltpu.VMEM((2048, 1024), bf16),
-            pltpu.VMEM((16, TILE, 1024), bf16),
-            pltpu.VMEM((4, 4, 128, TILE), bf16),
+            pltpu.VMEM((ROWS, LOC), bf16),
+            pltpu.VMEM((2, ROWS, TILE), f32),
+            pltpu.VMEM((2, ROWS, TILE), f32),
+            pltpu.VMEM((2, 2048, LOC), bf16),
+            pltpu.VMEM((2, 16, TILE, LOC), bf16),
+            pltpu.VMEM((4, 4, ROWS, TILE), bf16),
             pltpu.VMEM((8, 16, 2048), bf16),
-            pltpu.VMEM((128, 512), f32),
-            pltpu.VMEM((128, 512), f32),
-            pltpu.VMEM((128, 512), f32),
-            two, dma, dma, dma, two, dma, dma((16,)),
+            pltpu.VMEM((ROWS, LOC), f32),
+            pltpu.VMEM((ROWS, LOC), f32),
+            pltpu.VMEM((ROWS, LOC), f32),
+            two, dma, dma, dma, two, two, dma((2, 16)),
             two, two, two, two, dma, dma,
             dma, dma, two, two, two, two, two, two, dma((3,)), dma((3,)),
         ],

time: 101 us -> 98.3 us (0.973)
  Pallas kernels: 95.5 us -> 92.9 us
    pallas_call x2, Pallas kernels: 21.4 us -> 19.7 us  [the longest x1 17 us: out_proj(): pl.pallas_call(out_proj_kernel, out_shape=jax.ShapeDtypeStruct((ROWS, LOC...]
  transfers between devices with their start and end apart: 3 -> 3, of which waited for: 0 -> 1; matrix products, arithmetic and copies ran while one was open for 0% -> 0% of each run, Pallas kernels for 49% -> 50%
where the time goes in v4:
time: 98.3 us; the launch traced here: 98.1 us
  Pallas kernels  92.9 us (95%)
  starting transfers between devices  2.64 us (3%)
  local copies, waits for them, and re-layouts  1.57 us (2%)
    pallas_call x2, Pallas kernels, attend(): pl.pallas_call(functools.partial(attend_kernel, lo, hi), out_shape=[jax.S...  45.9 us
    pallas_call x1, Pallas kernels, in_proj(): pl.pallas_call(in_proj_kernel, out_shape=[jax.ShapeDtypeStruct((2, 16, NQ...  27.3 us
    pallas_call x1, Pallas kernels, out_proj(): pl.pallas_call(out_proj_kernel, out_shape=jax.ShapeDtypeStruct((ROWS, LOC...  17 us
    pallas_call x1, Pallas kernels, act(): pl.pallas_call(act_kernel, out_shape=jax.ShapeDtypeStruct((NA, ROWS, TILE...  2.68 us
  transfers between devices with their start and end apart: 3, of which 1 were waited for; matrix products, arithmetic and copies ran while one was open for 0% of the time, Pallas kernels for 50%

profile of v4, /device:TPU:0, one launch (start us, length us, event | category | flops | bytes accessed | tf_op | source)
XLA Modules:
  0.0 98.1 jit_solution(16284320815620663874)
XLA Ops:
  0.6 27.3 %in_proj.1 = (bf16[2,16,2304]{2,1,0:T(8,128)(2,1)}, f32[5,128,512]{2,1,0:T(8,128)}, f32[2,128,512]{2,1,0:T(8,128)}, f32[1,128,512]{2,1,0:T(8,128)}, f32[8,128,512]{2,1,0:T(8,128)}) custom-call(bf16[128,512]{1,0:T(8,128)(2,1)} %x_hbm.3, bf16[512]{0:T(512)(128)(2,1)} %g_hbm.1, bf16[1024,2304]{1,0:T(8,128)(2,1)} %wq_ref.1, bf16[1024,8192]{1,0:T(8,128)(2,1)} %wg_ref.1, ...), custom_call_target="tpu_custom_call" | custom-call | flops 5000000000 | bytes 45000000 | tf_op jit(solution)/shard_map/in_proj/pallas_call | solution.py:278
  28.0 0.6 collective-permute-start.1
  28.5 28.2 %attend0.1 = (bf16[16,4096,256]{2,1,0:T(8,128)(2,1)}, bf16[16,4096,256]{2,1,0:T(8,128)(2,1)}, bf16[16,4096]{1,0:T(8,128)(2,1)}) custom-call(s32[16]{0:T(128)} %len_hbm.3, bf16[2,16,2304]{2,1,0:T(8,128)(2,1)} %get-tuple-element.17.qkv_hbm, bf16[16,4096,256]{2,1,0:T(8,128)(2,1)} %k_ref.3, bf16[16,4096,256]{2,1,0:T(8,128)(2,1)} %v_ref.3), custom_call_target="tpu_custom_call" | custom-call | flops 24999999488 | bytes 84000000 | tf_op jit(solution)/shard_map/attend0/pallas_call | solution.py:431
  56.7 1.5 %collective-permute-start = (f32[2,128,512]{2,1,0:T(8,128)}, f32[2,128,512]{2,1,0:T(8,128)}, u32[]{:S(2)}, u32[]{:S(2)}) collective-permute-start(f32[2,128,512]{2,1,0:T(8,128)} %get-tuple-element.24), channel_id=1, source_target_pairs={{0,2},{2,0},{1,3},{3,1},{4,6},{6,4},{5,7},{7,5}} | collective-permute-start | bytes 1572872 | tf_op jit(solution)/shard_map/ppermute | solution.py:736
  58.2 0.3 collective-permute-done.1.r_ref
  58.5 2.7 %act.1.ao_ref = bf16[3,128,512]{2,1,0:T(8,128)(2,1)} custom-call(f32[8,128,512]{2,1,0:T(8,128)} %get-tuple-element.23.d_ref, f32[1,128,512]{2,1,0:T(8,128)} %get-tuple-element.25.r0_ref, f32[5,128,512]{2,1,0:T(8,128)} %collective-permute-done.1.r_ref), custom_call_target="tpu_custom_call" | custom-call | flops 5000000 | bytes 4000000 | tf_op jit(solution)/shard_map/act/pallas_call | solution.py:493
  61.2 0.6 collective-permute-start.2
  61.8 17.7 %attend10.1 = (bf16[16,4096,256]{2,1,0:T(8,128)(2,1)}, bf16[16,4096,256]{2,1,0:T(8,128)(2,1)}, bf16[16,4096]{1,0:T(8,128)(2,1)}) custom-call(s32[16]{0:T(128)} %len_hbm.3, bf16[2,16,2304]{2,1,0:T(8,128)(2,1)} %get-tuple-element.17.qkv_hbm, bf16[16,4096,256]{2,1,0:T(8,128)(2,1)} %k_ref.3, ...), custom_call_target="tpu_custom_call", output_to_operand_aliasing={{0}: (4, {}), {1}: (5, {})} | custom-call | flops 15000000512 | bytes 50400000 | tf_op jit(solution)/shard_map/attend10/pallas_call | solution.py:431
  79.5 0.0 collective-permute-done.r_ref
  79.5 0.0 collective-permute-done.2.ax_ref
  79.5 17.0 %out_proj.1 = bf16[128,512]{1,0:T(8,128)(2,1)} custom-call(bf16[16,4096]{1,0:T(8,128)(2,1)} %get-tuple-element.19.o1_hbm, bf16[16,4096]{1,0:T(8,128)(2,1)} %get-tuple-element.22.o2_hbm, bf16[128,512]{1,0:T(8,128)(2,1)} %x_hbm.3, f32[8,128,512]{2,1,0:T(8,128)} %get-tuple-element.23.d_ref, f32[2,128,512]{2,1,0:T(8,128)} %collective-permute-done.r_ref, ...), custom_call_target="tpu_custom_call" | custom-call | flops 3000000000 | bytes 26000000 | tf_op jit(solution)/shard_map/out_proj/pallas_call | solution.py:692
  96.5 1.6 %copy.18 = bf16[128,512]{1,0:T(8,128)(2,1)} copy(bf16[128,512]{1,0:T(8,128)(2,1)} %out_proj.1) | data formatting | bytes 262144
Async XLA Ops:
  28.0 30.6 %collective-permute-start.1 = (f32[5,128,512]{2,1,0:T(8,128)}, f32[5,128,512]{2,1,0:T(8,128)}, u32[]{:S(2)}, u32[]{:S(2)}) collective-permute-start(f32[5,128,512]{2,1,0:T(8,128)} %get-tuple-element.26), channel_id=1, source_target_pairs={{0,2},{2,0},{1,3},{3,1},{4,6},{6,4},{5,7},{7,5}} | collective-permute-start | bytes 3932168 | tf_op jit(solution)/shard_map/ppermute | solution.py:733
  56.7 22.8 %collective-permute-start = (f32[2,128,512]{2,1,0:T(8,128)}, f32[2,128,512]{2,1,0:T(8,128)}, u32[]{:S(2)}, u32[]{:S(2)}) collective-permute-start(f32[2,128,512]{2,1,0:T(8,128)} %get-tuple-element.24), channel_id=1, source_target_pairs={{0,2},{2,0},{1,3},{3,1},{4,6},{6,4},{5,7},{7,5}} | collective-permute-start | bytes 1572872 | tf_op jit(solution)/shard_map/ppermute | solution.py:736
  61.2 18.3 %collective-permute-start.2 = (bf16[3,128,512]{2,1,0:T(8,128)(2,1)}, bf16[3,128,512]{2,1,0:T(8,128)(2,1)}, u32[]{:S(2)}, u32[]{:S(2)}) collective-permute-start(bf16[3,128,512]{2,1,0:T(8,128)(2,1)} %act.1.ao_ref), channel_id=1, source_target_pairs={{0,2},{2,0},{1,3},{3,1},{4,6},{6,4},{5,7},{7,5}} | collective-permute-start | bytes 1179656 | tf_op jit(solution)/shard_map/ppermute | solution.py:738

commit v5 on v4

--- a/solution.py
+++ b/solution.py
@@ -12,7 +12,8 @@
 ROWS = 128
 HD = 256
 LOC = 512
-OUT_ROOM = 8000000
+TALL = 2 ** 23
+OUT_ROOM = 11700000
 TILE = 512
 SA = 5
 SPLIT = 10
@@ -34,10 +35,10 @@
     return pltpu.make_async_remote_copy(src, dst, ssem, rsem, device_id=dev, device_id_type=MESH)
 
 
-def in_proj_kernel(x_hbm, g_hbm, wq_ref, wg_ref, wu_ref, qkv_ref, sa_ref, sb_ref, r0_ref, d_ref,
+def in_proj_kernel(x_hbm, g_hbm, wq_ref, wg_ref, wu_ref, qkv_ref, sa_ref, sb_ref, r0_ref, d_ref, xc_ref,
                    wqv, wv, x_ref, g_ref, xr, gr, qout, st, stx, h, qp, qr, qxs, qxr, qf, qyr, sbuf, rbuf, obuf,
                    wqsem, wsem, xs_sem, xr_sem, gs_sem, gr_sem, sts_sem, str_sem,
-                   qds_sem, qdr_sem, qxs_sem, qxr_sem, qys_sem, qyr_sem, ds_sem, dr_sem, out_sem, xin_sem, gin_sem, qo_sem, es_sem, er_sem):
+                   qds_sem, qdr_sem, qxs_sem, qxr_sem, qys_sem, qyr_sem, ds_sem, dr_sem, out_sem, xin_sem, gin_sem, qo_sem, es_sem, er_sem, xc_sem):
     d_model = 4096
     x = lax.axis_index("x")
     yz = lax.axis_index("yz")
@@ -264,11 +265,14 @@
         qout[1 - yz, :, pl.ds(QC * j, QC)] = qyr[j]
     q_out = local_copy(qout, qkv_ref, qo_sem)
     q_out.start()
+    x_out = local_copy(x_ref, xc_ref.at[pl.ds(0, ROWS)], xc_sem)
+    x_out.start()
     for i in range(NT):
         if i:
             s_out(i).wait()
         d_out(i).wait()
     q_out.wait()
+    x_out.wait()
     early.wait()
 
 
@@ -283,9 +287,10 @@
             jax.ShapeDtypeStruct((NT - 1 - SA, ROWS, TILE), f32),
             jax.ShapeDtypeStruct((1, ROWS, TILE), f32),
             jax.ShapeDtypeStruct((NT, ROWS, TILE), f32),
+            jax.ShapeDtypeStruct((TALL // LOC, LOC), bf16),
         ],
         in_specs=[anyspec] * 5,
-        out_specs=[anyspec] * 5,
+        out_specs=[anyspec] * 6,
         scratch_shapes=[
             pltpu.VMEM((NQ, 1024, QC), bf16),
             pltpu.VMEM((4 * NT, 1024, TILE), bf16),
@@ -308,7 +313,7 @@
             pltpu.VMEM((2 * NT, ROWS, TILE), f32),
             dma((NQ,)), dma((4 * NT,)), dma, dma, dma, dma, dma((7,)), dma((8,)),
             dma((NQ, 2)), dma((NQ, 2)), dma((NQ,)), dma((NQ,)), dma((NQ,)), dma((NQ,)),
-            dma((2 * NT,)), dma((2 * NT,)), dma((2 * NT,)), dma, dma, dma, dma, dma,
+            dma((2 * NT,)), dma((2 * NT,)), dma((2 * NT,)), dma, dma, dma, dma, dma, dma,
         ],
         compiler_params=pltpu.CompilerParams(
             collective_id=0, has_side_effects=True, vmem_limit_bytes=VMEM_LIMIT),
@@ -416,7 +421,7 @@
     lax.fori_loop(lo, hi, body, 0)
     for g in range(16):
         o_ref[:, HD * g:HD * (g + 1)] = osc[:, g, :].astype(bf16)
-    o_out = local_copy(o_ref, o_hbm, osem)
+    o_out = local_copy(o_ref, o_hbm.at[pl.ds(0, 16)], osem)
     o_out.start()
     for r in range(max(lo, hi - SLOTS), hi):
         k_out(r, r % SLOTS).wait()
@@ -433,7 +438,7 @@
         out_shape=[
             jax.ShapeDtypeStruct(kc.shape, bf16),
             jax.ShapeDtypeStruct(vc.shape, bf16),
-            jax.ShapeDtypeStruct((n, 4096), bf16),
+            jax.ShapeDtypeStruct((TALL // 4096, 4096), bf16),
         ],
         in_specs=[anyspec] * (4 + len(prev)),
         out_specs=[anyspec] * 3,
@@ -459,7 +464,7 @@
 NA = 3
 
 
-def act_kernel(d_ref, r0_ref, r_ref, a_hbm, db, rb, a_ref, dsem, rsem, asem):
+def act_kernel(d_ref, r0_ref, r_ref, a_hbm, at_hbm, db, rb, a_ref, dsem, rsem, asem, tsem):
     def d_in(i):
         return local_copy(d_ref.at[i], db.at[i], dsem.at[i])
 
@@ -468,6 +473,8 @@
 
     def a_out(t):
         return local_copy(a_ref.at[t], a_hbm.at[t], asem.at[t])
+
+    tall = local_copy(a_ref, at_hbm.at[pl.ds(0, NA)], tsem)
 
     for i in range(2 * NA):
         d_in(i).start()
@@ -483,8 +490,10 @@
         if t:
             a_out(t - 1).start()
     a_out(NA - 1).start()
+    tall.start()
     for t in range(NA):
         a_out(t).wait()
+    tall.wait()
 
 
 def act(d, r0, r):
@@ -492,14 +501,17 @@
     dma = pltpu.SemaphoreType.DMA
     return pl.pallas_call(
         act_kernel,
-        out_shape=jax.ShapeDtypeStruct((NA, ROWS, TILE), bf16),
+        out_shape=[
+            jax.ShapeDtypeStruct((NA, ROWS, TILE), bf16),
+            jax.ShapeDtypeStruct((TALL // (ROWS * TILE), ROWS, TILE), bf16),
+        ],
         in_specs=[anyspec] * 3,
-        out_specs=anyspec,
+        out_specs=[anyspec] * 2,
         scratch_shapes=[
             pltpu.VMEM((2 * NA, ROWS, TILE), f32),
             pltpu.VMEM((2 * NA, ROWS, TILE), f32),
             pltpu.VMEM((NA, ROWS, TILE), bf16),
-            dma((2 * NA,)), dma((2 * NA,)), dma((NA,)),
+            dma((2 * NA,)), dma((2 * NA,)), dma((NA,)), dma,
         ],
         compiler_params=pltpu.CompilerParams(vmem_limit_bytes=VMEM_LIMIT),
         cost_estimate=pl.CostEstimate(flops=5_000_000, bytes_accessed=4_000_000, transcendentals=200_000),
@@ -525,11 +537,12 @@
     for dev in (partner, xpeer, ypeer):
         pl.semaphore_signal(barrier, inc=1, device_id=dev, device_id_type=MESH)
 
-    o_in = [local_copy(o1_hbm, o1_ref, osem.at[0]), local_copy(o2_hbm, o2_ref, osem.at[1])]
+    top = pl.ds(0, 16)
+    o_in = [local_copy(o1_hbm.at[top], o1_ref, osem.at[0]), local_copy(o2_hbm.at[top], o2_ref, osem.at[1])]
     for c in o_in:
         c.start()
     first = pl.ds(0, NA)
-    own_in = local_copy(ao_ref, ab.at[x, first], asem.at[0])
+    own_in = local_copy(ao_ref.at[first], ab.at[x, first], asem.at[0])
     chip_in = local_copy(ax_ref, ab.at[x_chip, first], asem.at[1])
     own_in.start()
     chip_in.start()
@@ -538,7 +551,7 @@
         c.start()
     for c in o_in:
         c.wait()
-    x_in = local_copy(x_hbm, x_ref, xsem)
+    x_in = local_copy(x_hbm.at[pl.ds(0, ROWS)], x_ref, xsem)
     x_in.start()
 
     order = (x, x_chip, x_core, x_diag)
@@ -729,15 +742,15 @@
     swap = [(0, 2), (2, 0), (1, 3), (3, 1)]
 
     def local_layer(x_loc, gain_loc, wqkv_loc, wgate_loc, wup_loc, wao_loc, wmo_loc, kc_loc, vc_loc, len_loc):
-        qkv, sa, sb, r0, d = in_proj(x_loc, gain_loc, wqkv_loc, wgate_loc, wup_loc)
+        qkv, sa, sb, r0, d, x_tall = in_proj(x_loc, gain_loc, wqkv_loc, wgate_loc, wup_loc)
         ra = lax.ppermute(sa, "x", swap)
         k_all, v_all, o1 = attend(0, SPLIT, len_loc, qkv, kc_loc, vc_loc)
         sb, o1 = lax.optimization_barrier((sb, o1))
         rb = lax.ppermute(sb, "x", swap)
-        a_own = act(d, r0, ra)
+        a_own, a_tall = act(d, r0, ra)
         a_chip = lax.ppermute(a_own, "x", swap)
         k_all, v_all, o2 = attend(SPLIT, 16, len_loc, qkv, kc_loc, vc_loc, k_all, v_all)
-        y_loc = out_proj(o1, o2, x_loc, d, rb, a_own, a_chip, wao_loc, wmo_loc)
+        y_loc = out_proj(o1, o2, x_tall, d, rb, a_tall, a_chip, wao_loc, wmo_loc)
         return y_loc, k_all, v_all
 
     in_specs = (row_spec, P(both_axes), in_w_spec, in_w_spec, in_w_spec, out_w_spec, out_w_spec, cache_spec, cache_spec, len_spec)

time: 98.3 us -> 96.9 us (0.986)
  no operation moved by 1% of the time
where the time goes in v5:
time: 96.9 us; the launch traced here: 96.8 us
  Pallas kernels  92.5 us (95%)
  starting transfers between devices  2.64 us (3%)
    pallas_call x2, Pallas kernels, attend(): pl.pallas_call(functools.partial(attend_kernel, lo, hi), out_shape=[jax.S...  45.9 us
    pallas_call x1, Pallas kernels, in_proj(): pl.pallas_call(in_proj_kernel, out_shape=[jax.ShapeDtypeStruct((2, 16, NQ...  27.4 us
    pallas_call x1, Pallas kernels, out_proj(): pl.pallas_call(out_proj_kernel, out_shape=jax.ShapeDtypeStruct((ROWS, LOC...  16.4 us
    pallas_call x1, Pallas kernels, act(): pl.pallas_call(act_kernel, out_shape=[jax.ShapeDtypeStruct((NA, ROWS, TIL...  2.85 us
  transfers between devices with their start and end apart: 3, of which 1 were waited for; matrix products, arithmetic and copies ran while one was open for 0% of the time, Pallas kernels for 50%

profile of v5, /device:TPU:0, one launch (start us, length us, event | category | flops | bytes accessed | tf_op | source)
XLA Modules:
  0.0 96.8 jit_solution(4970080191951446291)
XLA Ops:
  0.6 27.4 %in_proj.1 = (bf16[2,16,2304]{2,1,0:T(8,128)(2,1)}, f32[5,128,512]{2,1,0:T(8,128)}, f32[2,128,512]{2,1,0:T(8,128)}, f32[1,128,512]{2,1,0:T(8,128)}, f32[8,128,512]{2,1,0:T(8,128)}, /*index=5*/bf16[16384,512]{1,0:T(8,128)(2,1)}) custom-call(bf16[128,512]{1,0:T(8,128)(2,1)} %x_hbm.1, bf16[512]{0:T(512)(128)(2,1)} %g_hbm.1, bf16[1024,2304]{1,0:T(8,128)(2,1)} %wq_ref.1, ...), custom_call_target="tpu_custom_call" | custom-call | flops 5000000000 | bytes 45000000 | tf_op jit(solution)/shard_map/in_proj/pallas_call | solution.py:282
  28.0 0.6 collective-permute-start.1
  28.6 28.2 %attend0.1 = (bf16[16,4096,256]{2,1,0:T(8,128)(2,1)}, bf16[16,4096,256]{2,1,0:T(8,128)(2,1)}, bf16[2048,4096]{1,0:T(8,128)(2,1)}) custom-call(s32[16]{0:T(128)} %len_hbm.3, bf16[2,16,2304]{2,1,0:T(8,128)(2,1)} %get-tuple-element.20.qkv_hbm, bf16[16,4096,256]{2,1,0:T(8,128)(2,1)} %k_ref.3, bf16[16,4096,256]{2,1,0:T(8,128)(2,1)} %v_ref.3), custom_call_target="tpu_custom_call" | custom-call | flops 24999999488 | bytes 84000000 | tf_op jit(solution)/shard_map/attend0/pallas_call | solution.py:436
  56.8 1.5 %collective-permute-start = (f32[2,128,512]{2,1,0:T(8,128)}, f32[2,128,512]{2,1,0:T(8,128)}, u32[]{:S(2)}, u32[]{:S(2)}) collective-permute-start(f32[2,128,512]{2,1,0:T(8,128)} %get-tuple-element.28), channel_id=1, source_target_pairs={{0,2},{2,0},{1,3},{3,1},{4,6},{6,4},{5,7},{7,5}} | collective-permute-start | bytes 1572872 | tf_op jit(solution)/shard_map/ppermute | solution.py:749
  58.3 0.3 collective-permute-done.1.r_ref
  58.6 2.8 %act.1 = (bf16[3,128,512]{2,1,0:T(8,128)(2,1)}, bf16[128,128,512]{2,1,0:T(8,128)(2,1)}) custom-call(f32[8,128,512]{2,1,0:T(8,128)} %get-tuple-element.27.d_ref, f32[1,128,512]{2,1,0:T(8,128)} %get-tuple-element.29.r0_ref, f32[5,128,512]{2,1,0:T(8,128)} %collective-permute-done.1.r_ref), custom_call_target="tpu_custom_call" | custom-call | flops 5000000 | bytes 4000000 | tf_op jit(solution)/shard_map/act/pallas_call | solution.py:502
  61.5 0.6 collective-permute-start.2
  62.0 17.7 %attend10.1 = (bf16[16,4096,256]{2,1,0:T(8,128)(2,1)}, bf16[16,4096,256]{2,1,0:T(8,128)(2,1)}, bf16[2048,4096]{1,0:T(8,128)(2,1)}) custom-call(s32[16]{0:T(128)} %len_hbm.3, bf16[2,16,2304]{2,1,0:T(8,128)(2,1)} %get-tuple-element.20.qkv_hbm, bf16[16,4096,256]{2,1,0:T(8,128)(2,1)} %k_ref.3, ...), custom_call_target="tpu_custom_call", output_to_operand_aliasing={{0}: (4, {}), {1}: (5, {})} | custom-call | flops 15000000512 | bytes 50400000 | tf_op jit(solution)/shard_map/attend10/pallas_call | solution.py:436
  79.7 0.0 collective-permute-done.r_ref
  79.7 0.0 collective-permute-done.2.ax_ref
  79.8 16.4 %out_proj.1 = bf16[128,512]{1,0:T(8,128)(2,1)S(1)} custom-call(bf16[2048,4096]{1,0:T(8,128)(2,1)} %get-tuple-element.22.o1_hbm, bf16[2048,4096]{1,0:T(8,128)(2,1)} %get-tuple-element.25.o2_hbm, bf16[16384,512]{1,0:T(8,128)(2,1)} %get-tuple-element.26.x_hbm, f32[8,128,512]{2,1,0:T(8,128)} %get-tuple-element.27.d_ref, ...), custom_call_target="tpu_custom_call" | custom-call | flops 3000000000 | bytes 26000000 | tf_op jit(solution)/shard_map/out_proj/pallas_call | solution.py:705
  96.1 0.7 copy.18
Async XLA Ops:
  28.0 30.6 %collective-permute-start.1 = (f32[5,128,512]{2,1,0:T(8,128)}, f32[5,128,512]{2,1,0:T(8,128)}, u32[]{:S(2)}, u32[]{:S(2)}) collective-permute-start(f32[5,128,512]{2,1,0:T(8,128)} %get-tuple-element.30), channel_id=1, source_target_pairs={{0,2},{2,0},{1,3},{3,1},{4,6},{6,4},{5,7},{7,5}} | collective-permute-start | bytes 3932168 | tf_op jit(solution)/shard_map/ppermute | solution.py:746
  56.8 22.9 %collective-permute-start = (f32[2,128,512]{2,1,0:T(8,128)}, f32[2,128,512]{2,1,0:T(8,128)}, u32[]{:S(2)}, u32[]{:S(2)}) collective-permute-start(f32[2,128,512]{2,1,0:T(8,128)} %get-tuple-element.28), channel_id=1, source_target_pairs={{0,2},{2,0},{1,3},{3,1},{4,6},{6,4},{5,7},{7,5}} | collective-permute-start | bytes 1572872 | tf_op jit(solution)/shard_map/ppermute | solution.py:749
  61.5 18.3 %collective-permute-start.2 = (bf16[3,128,512]{2,1,0:T(8,128)(2,1)}, bf16[3,128,512]{2,1,0:T(8,128)(2,1)}, u32[]{:S(2)}, u32[]{:S(2)}) collective-permute-start(bf16[3,128,512]{2,1,0:T(8,128)(2,1)} %get-tuple-element.32), channel_id=1, source_target_pairs={{0,2},{2,0},{1,3},{3,1},{4,6},{6,4},{5,7},{7,5}} | collective-permute-start | bytes 1179656 | tf_op jit(solution)/shard_map/ppermute | solution.py:751

commit v6 on v5

--- a/solution.py
+++ b/solution.py
@@ -12,6 +12,7 @@
 ROWS = 128
 HD = 256
 LOC = 512
+ACT_LIMIT = 46 * 2 ** 20
 TALL = 2 ** 23
 OUT_ROOM = 11700000
 TILE = 512
@@ -35,10 +36,10 @@
     return pltpu.make_async_remote_copy(src, dst, ssem, rsem, device_id=dev, device_id_type=MESH)
 
 
-def in_proj_kernel(x_hbm, g_hbm, wq_ref, wg_ref, wu_ref, qkv_ref, sa_ref, sb_ref, r0_ref, d_ref, xc_ref,
-                   wqv, wv, x_ref, g_ref, xr, gr, qout, st, stx, h, qp, qr, qxs, qxr, qf, qyr, sbuf, rbuf, obuf,
+def in_proj_kernel(x_hbm, g_hbm, len_hbm, wq_ref, wg_ref, wu_ref, qkv_ref, sa_ref, sb_ref, r0_ref, d_ref, xc_ref, lens_ref,
+                   wqv, wv, x_ref, g_ref, len_s, lens, xr, gr, qout, st, stx, h, qp, qr, qxs, qxr, qf, qyr, sbuf, rbuf, obuf,
                    wqsem, wsem, xs_sem, xr_sem, gs_sem, gr_sem, sts_sem, str_sem,
-                   qds_sem, qdr_sem, qxs_sem, qxr_sem, qys_sem, qyr_sem, ds_sem, dr_sem, out_sem, xin_sem, gin_sem, qo_sem, es_sem, er_sem, xc_sem):
+                   qds_sem, qdr_sem, qxs_sem, qxr_sem, qys_sem, qyr_sem, ds_sem, dr_sem, out_sem, xin_sem, gin_sem, qo_sem, es_sem, er_sem, xc_sem, len_sem, lens_sem):
     d_model = 4096
     x = lax.axis_index("x")
     yz = lax.axis_index("yz")
@@ -63,6 +64,8 @@
     g_in = local_copy(g_hbm, g_ref, gin_sem)
     x_in.start()
     g_in.start()
+    len_in = local_copy(len_hbm, len_s, len_sem)
+    len_in.start()
 
     def wq_copy(j):
         return local_copy(wq_ref.at[:, pl.ds(QC * j, QC)], wqv.at[j], wqsem.at[j])
@@ -171,6 +174,13 @@
 
     early = remote_copy(obuf.at[0], r0_ref.at[0], es_sem, er_sem, xpeer)
 
+    len_in.wait()
+    row = lax.broadcasted_iota(jnp.int32, (16, ROWS), 0)
+    rows = jnp.zeros((16, ROWS), jnp.int32)
+    for r in range(16):
+        rows = jnp.where(row == r, len_s[r], rows)
+    lens[...] = rows
+
     q_compute(0)
     q_compute(1)
     q_pair_start(0)
@@ -263,8 +273,10 @@
     for j in range(NQ):
         q_y(j).wait()
         qout[1 - yz, :, pl.ds(QC * j, QC)] = qyr[j]
-    q_out = local_copy(qout, qkv_ref, qo_sem)
+    q_out = local_copy(qout, qkv_ref.at[pl.ds(0, 2)], qo_sem)
     q_out.start()
+    lens_out = local_copy(lens, lens_ref.at[pl.ds(0, 16)], lens_sem)
+    lens_out.start()
     x_out = local_copy(x_ref, xc_ref.at[pl.ds(0, ROWS)], xc_sem)
     x_out.start()
     for i in range(NT):
@@ -273,29 +285,33 @@
         d_out(i).wait()
     q_out.wait()
     x_out.wait()
+    lens_out.wait()
     early.wait()
 
 
-def in_proj(x_loc, gain, wq, wg, wu):
+def in_proj(x_loc, gain, lens, wq, wg, wu):
     anyspec = pl.BlockSpec(memory_space=pltpu.HBM)
     dma = pltpu.SemaphoreType.DMA
     return pl.pallas_call(
         in_proj_kernel,
         out_shape=[
-            jax.ShapeDtypeStruct((2, 16, NQ * QC), bf16),
+            jax.ShapeDtypeStruct((TALL // (16 * NQ * QC), 16, NQ * QC), bf16),
             jax.ShapeDtypeStruct((SA, ROWS, TILE), f32),
             jax.ShapeDtypeStruct((NT - 1 - SA, ROWS, TILE), f32),
             jax.ShapeDtypeStruct((1, ROWS, TILE), f32),
             jax.ShapeDtypeStruct((NT, ROWS, TILE), f32),
             jax.ShapeDtypeStruct((TALL // LOC, LOC), bf16),
+            jax.ShapeDtypeStruct((TALL // ROWS, ROWS), jnp.int32),
         ],
-        in_specs=[anyspec] * 5,
-        out_specs=[anyspec] * 6,
+        in_specs=[anyspec] * 6,
+        out_specs=[anyspec] * 7,
         scratch_shapes=[
             pltpu.VMEM((NQ, 1024, QC), bf16),
             pltpu.VMEM((4 * NT, 1024, TILE), bf16),
             pltpu.VMEM((ROWS, LOC), bf16),
             pltpu.VMEM((LOC,), bf16),
+            pltpu.SMEM((16,), jnp.int32),
+            pltpu.VMEM((16, ROWS), jnp.int32),
             pltpu.VMEM((ROWS, LOC), bf16),
             pltpu.VMEM((LOC,), bf16),
             pltpu.VMEM((2, 16, NQ * QC), bf16),
@@ -313,13 +329,13 @@
             pltpu.VMEM((2 * NT, ROWS, TILE), f32),
             dma((NQ,)), dma((4 * NT,)), dma, dma, dma, dma, dma((7,)), dma((8,)),
             dma((NQ, 2)), dma((NQ, 2)), dma((NQ,)), dma((NQ,)), dma((NQ,)), dma((NQ,)),
-            dma((2 * NT,)), dma((2 * NT,)), dma((2 * NT,)), dma, dma, dma, dma, dma, dma,
+            dma((2 * NT,)), dma((2 * NT,)), dma((2 * NT,)), dma, dma, dma, dma, dma, dma, dma, dma,
         ],
         compiler_params=pltpu.CompilerParams(
             collective_id=0, has_side_effects=True, vmem_limit_bytes=VMEM_LIMIT),
         cost_estimate=pl.CostEstimate(flops=5_000_000_000, bytes_accessed=45_000_000, transcendentals=0),
         name="in_proj",
-    )(x_loc, gain, wq, wg, wu)
+    )(x_loc, gain, lens, wq, wg, wu)
 
 
 SLOTS = 6
@@ -328,7 +344,7 @@
 def attend_kernel(lo, hi, len_hbm, qkv_hbm, k_ref, v_ref, *refs):
     if lo:
         refs = refs[2:]
-    (ko_ref, vo_ref, o_hbm, o_ref, kb, vb, len_ref, qkv_ref, qs, kns, vns, osc,
+    (ko_ref, vo_ref, o_hbm, o_ref, kb, vb, len_ref, lens, qkv_ref, qs, kns, vns, osc,
      ksem, vsem, kosem, vosem, isem, osem) = refs
     t_len = k_ref.shape[1]
 
@@ -345,24 +361,23 @@
         return local_copy(vb.at[s], vo_ref.at[r], vosem.at[s])
 
     AHEAD = 4
-    len_in = local_copy(len_hbm, len_ref, isem.at[0])
-    qkv_in = local_copy(qkv_hbm, qkv_ref, isem.at[1])
+    len_in = local_copy(len_hbm.at[pl.ds(0, 16)], len_ref, isem.at[0])
+    lens_in = local_copy(len_hbm.at[pl.ds(0, 16)], lens, isem.at[2])
+    lens_in.start()
+    qkv_in = local_copy(qkv_hbm.at[pl.ds(0, 2)], qkv_ref, isem.at[1])
     len_in.start()
     qkv_in.start()
     for r in range(lo, lo + 2):
         k_in(r, r % SLOTS).start()
         v_in(r, r % SLOTS).start()
     len_in.wait()
+    lens_in.wait()
     qkv_in.wait()
     for r in range(lo + 2, lo + AHEAD):
         k_in(r, r % SLOTS).start()
         v_in(r, r % SLOTS).start()
-    row = lax.broadcasted_iota(jnp.int32, (16, ROWS), 0)
-    lens = jnp.zeros((16, ROWS), jnp.int32)
-    for r in range(16):
-        lens = jnp.where(row == r, len_ref[r], lens)
     half = lax.broadcasted_iota(jnp.int32, (16, ROWS), 1).astype(f32)
-    angles = lens.astype(f32) * 10000.0 ** (-half / ROWS)
+    angles = lens[...].astype(f32) * 10000.0 ** (-half / ROWS)
     cos_t = jnp.cos(angles)
     sin_t = jnp.sin(angles)
     for g in range(17):
@@ -397,7 +412,7 @@
             k_in(nxt, s2).start()
             v_in(nxt, s2).start()
 
-        p = len_ref[r]
+        p = len_ref[r, 0]
         base = pl.multiple_of((p // 16) * 16, 16)
         hit = row16 == p - base
         k_in(r, s).wait()
@@ -447,15 +462,16 @@
             pltpu.VMEM((n, 4096), bf16),
             pltpu.VMEM((SLOTS, t_len, hd), bf16),
             pltpu.VMEM((SLOTS, t_len, hd), bf16),
-            pltpu.SMEM((n,), jnp.int32),
+            pltpu.SMEM((n, ROWS), jnp.int32),
+            pltpu.VMEM((n, ROWS), jnp.int32),
             pltpu.VMEM((2, 16, NQ * QC), bf16),
             pltpu.VMEM((n, 16, hd), f32),
             pltpu.VMEM((n, hd), f32),
             pltpu.VMEM((n, hd), f32),
             pltpu.VMEM((n, 16, hd), f32),
-            dma((SLOTS,)), dma((SLOTS,)), dma((SLOTS,)), dma((SLOTS,)), dma((2,)), dma,
+            dma((SLOTS,)), dma((SLOTS,)), dma((SLOTS,)), dma((SLOTS,)), dma((3,)), dma,
         ],
-        compiler_params=pltpu.CompilerParams(vmem_limit_bytes=VMEM_LIMIT),
+        compiler_params=pltpu.CompilerParams(vmem_limit_bytes=VMEM_LIMIT if lo else 44 * 2 ** 20),
         cost_estimate=pl.CostEstimate(flops=2_500_000_000 * (hi - lo), bytes_accessed=8_400_000 * (hi - lo), transcendentals=1_000_000),
         name=f"attend{lo}",
     )(lens, qkv, kc, vc, *prev)
@@ -464,26 +480,15 @@
 NA = 3
 
 
-def act_kernel(d_ref, r0_ref, r_ref, a_hbm, at_hbm, db, rb, a_ref, dsem, rsem, asem, tsem):
-    def d_in(i):
-        return local_copy(d_ref.at[i], db.at[i], dsem.at[i])
-
-    def r_in(i):
-        return local_copy(r_ref.at[i - 1] if i else r0_ref.at[0], rb.at[i], rsem.at[i])
-
+def act_kernel(d_ref, r0_ref, r_ref, a_hbm, at_hbm, a_ref, asem, tsem):
     def a_out(t):
         return local_copy(a_ref.at[t], a_hbm.at[t], asem.at[t])
 
     tall = local_copy(a_ref, at_hbm.at[pl.ds(0, NA)], tsem)
 
-    for i in range(2 * NA):
-        d_in(i).start()
-        r_in(i).start()
-
     def total(i):
-        d_in(i).wait()
-        r_in(i).wait()
-        return (db[i] + rb[i]).astype(bf16).astype(f32)
+        other = r_ref[i - 1] if i else r0_ref[0]
+        return (d_ref[i] + other).astype(bf16).astype(f32)
 
     for t in range(NA):
         a_ref[t] = (jax.nn.silu(total(2 * t)) * total(2 * t + 1)).astype(bf16)
@@ -505,15 +510,13 @@
             jax.ShapeDtypeStruct((NA, ROWS, TILE), bf16),
             jax.ShapeDtypeStruct((TALL // (ROWS * TILE), ROWS, TILE), bf16),
         ],
-        in_specs=[anyspec] * 3,
+        in_specs=[pl.BlockSpec(memory_space=pltpu.VMEM)] * 3,
         out_specs=[anyspec] * 2,
         scratch_shapes=[
-            pltpu.VMEM((2 * NA, ROWS, TILE), f32),
-            pltpu.VMEM((2 * NA, ROWS, TILE), f32),
             pltpu.VMEM((NA, ROWS, TILE), bf16),
-            dma((2 * NA,)), dma((2 * NA,)), dma((NA,)), dma,
+            dma((NA,)), dma,
         ],
-        compiler_params=pltpu.CompilerParams(vmem_limit_bytes=VMEM_LIMIT),
+        compiler_params=pltpu.CompilerParams(vmem_limit_bytes=ACT_LIMIT),
         cost_estimate=pl.CostEstimate(flops=5_000_000, bytes_accessed=4_000_000, transcendentals=200_000),
         name="act",
     )(d, r0, r)
@@ -742,14 +745,14 @@
     swap = [(0, 2), (2, 0), (1, 3), (3, 1)]
 
     def local_layer(x_loc, gain_loc, wqkv_loc, wgate_loc, wup_loc, wao_loc, wmo_loc, kc_loc, vc_loc, len_loc):
-        qkv, sa, sb, r0, d, x_tall = in_proj(x_loc, gain_loc, wqkv_loc, wgate_loc, wup_loc)
+        qkv, sa, sb, r0, d, x_tall, lens = in_proj(x_loc, gain_loc, len_loc, wqkv_loc, wgate_loc, wup_loc)
         ra = lax.ppermute(sa, "x", swap)
-        k_all, v_all, o1 = attend(0, SPLIT, len_loc, qkv, kc_loc, vc_loc)
+        k_all, v_all, o1 = attend(0, SPLIT, lens, qkv, kc_loc, vc_loc)
         sb, o1 = lax.optimization_barrier((sb, o1))
         rb = lax.ppermute(sb, "x", swap)
         a_own, a_tall = act(d, r0, ra)
         a_chip = lax.ppermute(a_own, "x", swap)
-        k_all, v_all, o2 = attend(SPLIT, 16, len_loc, qkv, kc_loc, vc_loc, k_all, v_all)
+        k_all, v_all, o2 = attend(SPLIT, 16, lens, qkv, kc_loc, vc_loc, k_all, v_all)
         y_loc = out_proj(o1, o2, x_tall, d, rb, a_tall, a_chip, wao_loc, wmo_loc)
         return y_loc, k_all, v_all
 

time: 96.9 us -> 96.4 us (level)
  Pallas kernels: 92.5 us -> 91.4 us
    pallas_call x1, Pallas kernels: 2.85 us -> 1.11 us  [act(): pl.pallas_call(act_kernel, out_shape=[jax.ShapeDtypeStruct((NA, ROWS, TIL...]
  transfers between devices with their start and end apart: 3 -> 3, of which waited for: 1 -> 1; matrix products, arithmetic and copies ran while one was open for 0% -> 0% of each run, Pallas kernels for 50% -> 49%
where the time goes in v6:
time: 96.4 us; the launch traced here: 96.3 us
  Pallas kernels  91.4 us (95%)
  starting transfers between devices  2.64 us (3%)
    pallas_call x2, Pallas kernels, attend(): pl.pallas_call(functools.partial(attend_kernel, lo, hi), out_shape=[jax.S...  46.5 us
    pallas_call x1, Pallas kernels, in_proj(): pl.pallas_call(in_proj_kernel, out_shape=[jax.ShapeDtypeStruct((TALL // (...  27.4 us
    pallas_call x1, Pallas kernels, out_proj(): pl.pallas_call(out_proj_kernel, out_shape=jax.ShapeDtypeStruct((ROWS, LOC...  16.3 us
  transfers between devices with their start and end apart: 3, of which 1 were waited for; matrix products, arithmetic and copies ran while one was open for 0% of the time, Pallas kernels for 49%

profile of v6, /device:TPU:0, one launch (start us, length us, event | category | flops | bytes accessed | tf_op | source)
XLA Modules:
  0.0 96.3 jit_solution(9037674521522342988)
XLA Ops:
  0.6 27.4 %in_proj.1 = (bf16[227,16,2304]{2,1,0:T(8,128)(2,1)}, f32[5,128,512]{2,1,0:T(8,128)}, f32[2,128,512]{2,1,0:T(8,128)}, f32[1,128,512]{2,1,0:T(8,128)}, f32[8,128,...) custom-call(bf16[128,512]{1,0:T(8,128)(2,1)} %x_hbm.1, bf16[512]{0:T(512)(128)(2,1)} %g_hbm.1, ...), custom_call_target="tpu_custom_call" | custom-call | flops 5000000000 | bytes 45000000 | tf_op jit(solution)/shard_map/in_proj/pallas_call | solution.py:295
  28.1 0.6 collective-permute-start.1
  28.7 0.0 copy-start
  28.7 0.0 copy-start.1
  28.7 28.8 %attend0.1 = (bf16[16,4096,256]{2,1,0:T(8,128)(2,1)}, bf16[16,4096,256]{2,1,0:T(8,128)(2,1)}, bf16[2048,4096]{1,0:T(8,128)(2,1)}) custom-call(s32[65536,128]{1,0:T(8,128)} %get-tuple-element.21.len_hbm, bf16[227,16,2304]{2,1,0:T(8,128)(2,1)} %get-tuple-element.22.qkv_hbm, bf16[16,4096,256]{2,1,0:T(8,128)(2,1)} %k_ref.3, bf16[16,4096,256]{2,1,0:T(8,128)(2,1)} %v_ref.3), custom_call_target="tpu_custom_call" | custom-call | flops 24999999488 | bytes 84000000 | tf_op jit(solution)/shard_map/attend0/pallas_call | solution.py:451
  57.5 1.5 %collective-permute-start = (f32[2,128,512]{2,1,0:T(8,128)}, f32[2,128,512]{2,1,0:T(8,128)}, u32[]{:S(2)}, u32[]{:S(2)}) collective-permute-start(f32[2,128,512]{2,1,0:T(8,128)} %get-tuple-element.30), channel_id=1, source_target_pairs={{0,2},{2,0},{1,3},{3,1},{4,6},{6,4},{5,7},{7,5}} | collective-permute-start | bytes 1572872 | tf_op jit(solution)/shard_map/ppermute | solution.py:752
  59.0 0.0 collective-permute-done.1.r_ref
  59.0 0.0 copy-done
  59.0 0.0 copy-done.1
  59.0 1.1 %act.1 = (bf16[3,128,512]{2,1,0:T(8,128)(2,1)}, bf16[128,128,512]{2,1,0:T(8,128)(2,1)}) custom-call(f32[8,128,512]{2,1,0:T(8,128)S(1)} %copy-done, f32[1,128,512]{2,1,0:T(8,128)S(1)} %copy-done.1, f32[5,128,512]{2,1,0:T(8,128)S(1)} %collective-permute-done.1.r_ref), custom_call_target="tpu_custom_call" | custom-call | flops 5000000 | bytes 4000000 | tf_op jit(solution)/shard_map/act/pallas_call | solution.py:507
  60.1 0.6 collective-permute-start.2
  60.7 17.7 %attend10.1 = (bf16[16,4096,256]{2,1,0:T(8,128)(2,1)}, bf16[16,4096,256]{2,1,0:T(8,128)(2,1)}, bf16[2048,4096]{1,0:T(8,128)(2,1)}) custom-call(s32[65536,128]{1,0:T(8,128)} %get-tuple-element.21.len_hbm, bf16[227,16,2304]{2,1,0:T(8,128)(2,1)} %get-tuple-element.22.qkv_hbm, ...), custom_call_target="tpu_custom_call", output_to_operand_aliasing={{0}: (4, {}), {1}: (5, {})} | custom-call | flops 15000000512 | bytes 50400000 | tf_op jit(solution)/shard_map/attend10/pallas_call | solution.py:451
  78.4 0.0 collective-permute-done.r_ref
  78.4 0.9 collective-permute-done.2.ax_ref
  79.3 16.3 %out_proj.1 = bf16[128,512]{1,0:T(8,128)(2,1)S(1)} custom-call(bf16[2048,4096]{1,0:T(8,128)(2,1)} %get-tuple-element.24.o1_hbm, bf16[2048,4096]{1,0:T(8,128)(2,1)} %get-tuple-element.27.o2_hbm, bf16[16384,512]{1,0:T(8,128)(2,1)} %get-tuple-element.28.x_hbm, f32[8,128,512]{2,1,0:T(8,128)} %get-tuple-element.29.d_ref, ...), custom_call_target="tpu_custom_call" | custom-call | flops 3000000000 | bytes 26000000 | tf_op jit(solution)/shard_map/out_proj/pallas_call | solution.py:708
  95.7 0.7 copy.18
Async XLA Ops:
  28.1 30.9 %collective-permute-start.1 = (f32[5,128,512]{2,1,0:T(8,128)}, f32[5,128,512]{2,1,0:T(8,128)S(1)}, u32[]{:S(2)}, u32[]{:S(2)}) collective-permute-start(f32[5,128,512]{2,1,0:T(8,128)} %get-tuple-element.32), channel_id=1, source_target_pairs={{0,2},{2,0},{1,3},{3,1},{4,6},{6,4},{5,7},{7,5}} | collective-permute-start | bytes 3932168 | tf_op jit(solution)/shard_map/ppermute | solution.py:749
  28.7 30.3 %copy-start = (f32[8,128,512]{2,1,0:T(8,128)S(1)}, f32[8,128,512]{2,1,0:T(8,128)}, u32[]{:S(2)}) copy-start(f32[8,128,512]{2,1,0:T(8,128)} %get-tuple-element.29.d_ref) | copy-start | bytes 6291460
  28.7 30.3 %copy-start.1 = (f32[1,128,512]{2,1,0:T(8,128)S(1)}, f32[1,128,512]{2,1,0:T(8,128)}, u32[]{:S(2)}) copy-start(f32[1,128,512]{2,1,0:T(8,128)} %get-tuple-element.31.r0_ref) | copy-start | bytes 786436
  57.5 20.9 %collective-permute-start = (f32[2,128,512]{2,1,0:T(8,128)}, f32[2,128,512]{2,1,0:T(8,128)}, u32[]{:S(2)}, u32[]{:S(2)}) collective-permute-start(f32[2,128,512]{2,1,0:T(8,128)} %get-tuple-element.30), channel_id=1, source_target_pairs={{0,2},{2,0},{1,3},{3,1},{4,6},{6,4},{5,7},{7,5}} | collective-permute-start | bytes 1572872 | tf_op jit(solution)/shard_map/ppermute | solution.py:752
  60.1 19.2 %collective-permute-start.2 = (bf16[3,128,512]{2,1,0:T(8,128)(2,1)}, bf16[3,128,512]{2,1,0:T(8,128)(2,1)}, u32[]{:S(2)}, u32[]{:S(2)}) collective-permute-start(bf16[3,128,512]{2,1,0:T(8,128)(2,1)} %get-tuple-element.34), channel_id=1, source_target_pairs={{0,2},{2,0},{1,3},{3,1},{4,6},{6,4},{5,7},{7,5}} | collective-permute-start | bytes 1179656 | tf_op jit(solution)/shard_map/ppermute | solution.py:754

commit v7 on v6

--- a/solution.py
+++ b/solution.py
@@ -12,6 +12,9 @@
 ROWS = 128
 HD = 256
 LOC = 512
+SUB = 16
+HALF = 64
+WIDE = 2048
 ACT_LIMIT = 46 * 2 ** 20
 TALL = 2 ** 23
 OUT_ROOM = 11700000
@@ -77,7 +80,7 @@
         q = quarters[0]
         for n in range(1, 4):
             q = jnp.where(phase == n, quarters[n], q)
-        cols = pl.multiple_of(q * 2048 + (slot % NT) // 2 * TILE, TILE)
+        cols = pl.multiple_of(q * WIDE + (slot % NT) // 2 * TILE, TILE)
 
         def start(w_hbm):
             local_copy(w_hbm.at[:, pl.ds(cols, TILE)], wv.at[slot], wsem.at[slot]).start()
@@ -175,9 +178,9 @@
     early = remote_copy(obuf.at[0], r0_ref.at[0], es_sem, er_sem, xpeer)
 
     len_in.wait()
-    row = lax.broadcasted_iota(jnp.int32, (16, ROWS), 0)
-    rows = jnp.zeros((16, ROWS), jnp.int32)
-    for r in range(16):
+    row = lax.broadcasted_iota(jnp.int32, (SUB, ROWS), 0)
+    rows = jnp.zeros((SUB, ROWS), jnp.int32)
+    for r in range(SUB):
         rows = jnp.where(row == r, len_s[r], rows)
     lens[...] = rows
 
@@ -212,17 +215,17 @@
         elif i:
             s_out(i - 1).start()
 
-    own_rows = pl.multiple_of(yz * 16, 16)
-    peer_rows = pl.multiple_of((1 - yz) * 16, 16)
+    own_rows = pl.multiple_of(yz * SUB, SUB)
+    peer_rows = pl.multiple_of((1 - yz) * SUB, SUB)
 
     def q_y(j):
-        return remote_copy(qf.at[j, pl.ds(peer_rows, 16)], qyr.at[j], qys_sem.at[j], qyr_sem.at[j], ypeer)
+        return remote_copy(qf.at[j, pl.ds(peer_rows, SUB)], qyr.at[j], qys_sem.at[j], qyr_sem.at[j], ypeer)
 
     def q_final(j):
         q_pair(j, 1).wait()
         q_chip(j).wait()
         qf[j] = (qp[j, x] + qr[j, 1] + qxr[j]).astype(bf16)
-        qout[yz, :, pl.ds(QC * j, QC)] = qf[j, pl.ds(own_rows, 16)]
+        qout[yz, :, pl.ds(QC * j, QC)] = qf[j, pl.ds(own_rows, SUB)]
 
     def send_tiles(lo, hi):
         def body(i, _):
@@ -275,7 +278,7 @@
         qout[1 - yz, :, pl.ds(QC * j, QC)] = qyr[j]
     q_out = local_copy(qout, qkv_ref.at[pl.ds(0, 2)], qo_sem)
     q_out.start()
-    lens_out = local_copy(lens, lens_ref.at[pl.ds(0, 16)], lens_sem)
+    lens_out = local_copy(lens, lens_ref.at[pl.ds(0, SUB)], lens_sem)
     lens_out.start()
     x_out = local_copy(x_ref, xc_ref.at[pl.ds(0, ROWS)], xc_sem)
     x_out.start()
@@ -295,7 +298,7 @@
     return pl.pallas_call(
         in_proj_kernel,
         out_shape=[
-            jax.ShapeDtypeStruct((TALL // (16 * NQ * QC), 16, NQ * QC), bf16),
+            jax.ShapeDtypeStruct((TALL // (SUB * NQ * QC), SUB, NQ * QC), bf16),
             jax.ShapeDtypeStruct((SA, ROWS, TILE), f32),
             jax.ShapeDtypeStruct((NT - 1 - SA, ROWS, TILE), f32),
             jax.ShapeDtypeStruct((1, ROWS, TILE), f32),
@@ -310,11 +313,11 @@
             pltpu.VMEM((4 * NT, 1024, TILE), bf16),
             pltpu.VMEM((ROWS, LOC), bf16),
             pltpu.VMEM((LOC,), bf16),
-            pltpu.SMEM((16,), jnp.int32),
-            pltpu.VMEM((16, ROWS), jnp.int32),
+            pltpu.SMEM((SUB,), jnp.int32),
+            pltpu.VMEM((SUB, ROWS), jnp.int32),
             pltpu.VMEM((ROWS, LOC), bf16),
             pltpu.VMEM((LOC,), bf16),
-            pltpu.VMEM((2, 16, NQ * QC), bf16),
+            pltpu.VMEM((2, SUB, NQ * QC), bf16),
             pltpu.VMEM((8, 8, ROWS), f32),
             pltpu.VMEM((8, 8, ROWS), f32),
             pltpu.VMEM((ROWS, 1024), bf16),
@@ -323,7 +326,7 @@
             pltpu.VMEM((NQ, 32, QC), f32),
             pltpu.VMEM((NQ, 32, QC), f32),
             pltpu.VMEM((NQ, 32, QC), bf16),
-            pltpu.VMEM((NQ, 16, QC), bf16),
+            pltpu.VMEM((NQ, SUB, QC), bf16),
             pltpu.VMEM((2 * NT, ROWS, TILE), f32),
             pltpu.VMEM((2 * NT, ROWS, TILE), f32),
             pltpu.VMEM((2 * NT, ROWS, TILE), f32),
@@ -361,8 +364,8 @@
         return local_copy(vb.at[s], vo_ref.at[r], vosem.at[s])
 
     AHEAD = 4
-    len_in = local_copy(len_hbm.at[pl.ds(0, 16)], len_ref, isem.at[0])
-    lens_in = local_copy(len_hbm.at[pl.ds(0, 16)], lens, isem.at[2])
+    len_in = local_copy(len_hbm.at[pl.ds(0, SUB)], len_ref, isem.at[0])
+    lens_in = local_copy(len_hbm.at[pl.ds(0, SUB)], lens, isem.at[2])
     lens_in.start()
     qkv_in = local_copy(qkv_hbm.at[pl.ds(0, 2)], qkv_ref, isem.at[1])
     len_in.start()
@@ -376,7 +379,7 @@
     for r in range(lo + 2, lo + AHEAD):
         k_in(r, r % SLOTS).start()
         v_in(r, r % SLOTS).start()
-    half = lax.broadcasted_iota(jnp.int32, (16, ROWS), 1).astype(f32)
+    half = lax.broadcasted_iota(jnp.int32, (SUB, ROWS), 1).astype(f32)
     angles = lens[...].astype(f32) * 10000.0 ** (-half / ROWS)
     cos_t = jnp.cos(angles)
     sin_t = jnp.sin(angles)
@@ -386,16 +389,16 @@
         b = qkv_ref[part, :, base + ROWS:base + HD].astype(f32)
         lower = (a * cos_t - b * sin_t).astype(bf16).astype(f32)
         upper = (b * cos_t + a * sin_t).astype(bf16).astype(f32)
-        if g < 16:
+        if g < SUB:
             qs[:, g, 0:ROWS] = lower
             qs[:, g, ROWS:HD] = upper
         else:
             kns[:, 0:ROWS] = lower
             kns[:, ROWS:HD] = upper
-    vns[...] = qkv_ref[1, :, 2048:2304].astype(f32)
-
-    row16 = lax.broadcasted_iota(jnp.int32, (16, HD), 0)
-    pos = lax.broadcasted_iota(jnp.int32, (16, t_len), 1)
+    vns[...] = qkv_ref[1, :, WIDE:2304].astype(f32)
+
+    row16 = lax.broadcasted_iota(jnp.int32, (SUB, HD), 0)
+    pos = lax.broadcasted_iota(jnp.int32, (SUB, t_len), 1)
 
     def body(r, _):
         s = lax.rem(r, SLOTS)
@@ -413,14 +416,14 @@
             v_in(nxt, s2).start()
 
         p = len_ref[r, 0]
-        base = pl.multiple_of((p // 16) * 16, 16)
+        base = pl.multiple_of((p // SUB) * SUB, SUB)
         hit = row16 == p - base
         k_in(r, s).wait()
-        krow = kb[s, pl.ds(base, 16), :]
-        kb[s, pl.ds(base, 16), :] = jnp.where(hit, kns[pl.ds(r, 1), :].astype(bf16), krow)
+        krow = kb[s, pl.ds(base, SUB), :]
+        kb[s, pl.ds(base, SUB), :] = jnp.where(hit, kns[pl.ds(r, 1), :].astype(bf16), krow)
         v_in(r, s).wait()
-        vrow = vb[s, pl.ds(base, 16), :]
-        vb[s, pl.ds(base, 16), :] = jnp.where(hit, vns[pl.ds(r, 1), :].astype(bf16), vrow)
+        vrow = vb[s, pl.ds(base, SUB), :]
+        vb[s, pl.ds(base, SUB), :] = jnp.where(hit, vns[pl.ds(r, 1), :].astype(bf16), vrow)
         q = qs[r].astype(bf16)
         sc = lax.dot_general(q, kb[s], (((1,), (1,)), ((), ())), preferred_element_type=f32) * (HD ** -0.5)
         k_out(r, s).start()
@@ -434,9 +437,9 @@
         return 0
 
     lax.fori_loop(lo, hi, body, 0)
-    for g in range(16):
+    for g in range(SUB):
         o_ref[:, HD * g:HD * (g + 1)] = osc[:, g, :].astype(bf16)
-    o_out = local_copy(o_ref, o_hbm.at[pl.ds(0, 16)], osem)
+    o_out = local_copy(o_ref, o_hbm.at[pl.ds(0, SUB)], osem)
     o_out.start()
     for r in range(max(lo, hi - SLOTS), hi):
         k_out(r, r % SLOTS).wait()
@@ -464,11 +467,11 @@
             pltpu.VMEM((SLOTS, t_len, hd), bf16),
             pltpu.SMEM((n, ROWS), jnp.int32),
             pltpu.VMEM((n, ROWS), jnp.int32),
-            pltpu.VMEM((2, 16, NQ * QC), bf16),
-            pltpu.VMEM((n, 16, hd), f32),
+            pltpu.VMEM((2, SUB, NQ * QC), bf16),
+            pltpu.VMEM((n, SUB, hd), f32),
             pltpu.VMEM((n, hd), f32),
             pltpu.VMEM((n, hd), f32),
-            pltpu.VMEM((n, 16, hd), f32),
+            pltpu.VMEM((n, SUB, hd), f32),
             dma((SLOTS,)), dma((SLOTS,)), dma((SLOTS,)), dma((SLOTS,)), dma((3,)), dma,
         ],
         compiler_params=pltpu.CompilerParams(vmem_limit_bytes=VMEM_LIMIT if lo else 44 * 2 ** 20),
@@ -540,7 +543,7 @@
     for dev in (partner, xpeer, ypeer):
         pl.semaphore_signal(barrier, inc=1, device_id=dev, device_id_type=MESH)
 
-    top = pl.ds(0, 16)
+    top = pl.ds(0, SUB)
     o_in = [local_copy(o1_hbm.at[top], o1_ref, osem.at[0]), local_copy(o2_hbm.at[top], o2_ref, osem.at[1])]
     for c in o_in:
         c.start()
@@ -563,7 +566,7 @@
     accs = (zs, zk)
 
     def wmo_in(half, n, t):
-        rows = pl.multiple_of(order[n] * 2048 + t * TILE, TILE)
+        rows = pl.multiple_of(order[n] * WIDE + t * TILE, TILE)
         k = 4 * n + t
         return local_copy(wmo_ref.at[pl.ds(rows, TILE), halves[half]], wmo.at[half, k], wmosem.at[half, k])
 
@@ -575,13 +578,13 @@
             wmo_in(half, n, t).start()
 
     wmo_start(0, 0)
-    row = lax.broadcasted_iota(jnp.int32, (16, 4096), 0)
+    row = lax.broadcasted_iota(jnp.int32, (SUB, 4096), 0)
     o_ref[...] = jnp.where(row < SPLIT, o1_ref[...].astype(f32), o2_ref[...].astype(f32)).astype(bf16)
-    own_half = pl.multiple_of(yz * 2048, 2048)
-    peer_half = pl.multiple_of((1 - yz) * 2048, 2048)
+    own_half = pl.multiple_of(yz * WIDE, WIDE)
+    peer_half = pl.multiple_of((1 - yz) * WIDE, WIDE)
     mine = 2 * x + yz
     theirs = 2 * x + 1 - yz
-    ob[mine] = o_ref[:, pl.ds(own_half, 2048)]
+    ob[mine] = o_ref[:, pl.ds(own_half, WIDE)]
 
     for c in loads:
         c.wait()
@@ -590,7 +593,7 @@
     ab[x, NA] = (jax.nn.silu(gate) * up).astype(bf16)
     pl.semaphore_wait(barrier, 3)
 
-    o_y = remote_copy(o_ref.at[:, pl.ds(peer_half, 2048)], ob.at[mine], o0s, o0r, ypeer)
+    o_y = remote_copy(o_ref.at[:, pl.ds(peer_half, WIDE)], ob.at[mine], o0s, o0r, ypeer)
 
     def o_hop(k, ss, rs, dev, owner):
         block = ob.at[2 * owner + (yz if k == 0 else 1 - yz)]
@@ -604,13 +607,23 @@
         block = ab.at[owner, tiles]
         return remote_copy(block, block, ss.at[k], rs.at[k], dev)
 
+    chip = x // 2
+    own_rows = pl.multiple_of(HALF * chip, HALF)
+    peer_rows = pl.multiple_of(HALF - HALF * chip, HALF)
+
+    def last_hop(owner, base, ss, rs, k, dev):
+        block = ab.at[owner, NA, pl.ds(base, HALF)]
+        return remote_copy(block, block, ss.at[k], rs.at[k], dev)
+
     last = pl.ds(NA, 1)
     a_part = [a_hop(x, first, pss, psr, 0, partner), a_hop(x, last, pss, psr, 1, partner)]
-    a_fwd = [a_hop(x_chip, first, fss, fsr, 0, partner), a_hop(x_chip, last, fss, fsr, 1, partner)]
-    a_chip = remote_copy(ab.at[x, last], ab.at[x, last], e_s, e_r, xpeer)
+    a_fwd = [a_hop(x_chip, first, fss, fsr, 0, partner)]
+    a_chip = [last_hop(x, peer_rows, e_s, e_r, 0, xpeer), last_hop(x, own_rows, e_s, e_r, 1, xpeer)]
+    a_fwd += [last_hop(x_chip, own_rows, fss, fsr, 1, partner), last_hop(x_chip, peer_rows, fss, fsr, 2, partner)]
 
     o_y.start()
-    a_chip.start()
+    for c in a_chip:
+        c.start()
     o_chip[0].start()
     o_part[0].start()
     a_part[1].start()
@@ -620,6 +633,8 @@
     a_fwd[0].start()
     wmo_start(0, 1)
     wmo_start(0, 2)
+    wao_in(0).start()
+    wmo_start(0, 3)
 
     def mlp(half, n, t, init=False):
         wmo_in(half, n, t).wait()
@@ -627,8 +642,6 @@
         part = jnp.dot(ab[order[n], t], wmo[half, 4 * n + t], preferred_element_type=f32)
         acc[...] = part if init else acc[...] + part
 
-    chip = x // 2
-    own_rows = pl.multiple_of(64 * chip, 64)
     chip_rows = pl.multiple_of(32 * x_chip, 32)
     diag_rows = pl.multiple_of(32 * x_diag, 32)
 
@@ -638,17 +651,19 @@
 
     def attn_rows(half, base, m):
         rows = pl.ds(base, m)
-        attn = ob[pl.ds(base // 16, m // 16)].reshape(m, 2048)
+        attn = ob[pl.ds(base // SUB, m // SUB)].reshape(m, WIDE)
         accs[half][rows] += jnp.dot(attn, wao[half], preferred_element_type=f32)
 
-    blocks = ((own_rows, 64), (chip_rows, 32), (diag_rows, 32))
+    def mlp_rows(n, base):
+        rows = pl.ds(base, HALF)
+        zs[rows] += jnp.dot(ab[order[n], NA, rows], wmo[0, 4 * n + NA], preferred_element_type=f32)
+
+    blocks = ((own_rows, HALF), (chip_rows, 32), (diag_rows, 32))
     for t in range(4):
         mlp(0, 0, t, init=t == 0)
     o_y.wait()
     o_chip[1].start()
     o_part[1].start()
-    wao_in(0).start()
-    wmo_start(0, 3)
     wmo_start(1, 0)
     wmo_start(1, 1)
     for t in range(NA):
@@ -656,13 +671,12 @@
     a_part[0].wait()
     for t in range(NA):
         mlp(0, 2, t)
-    a_chip.wait()
+    a_chip[0].wait()
     a_fwd[1].start()
-    mlp(0, 1, NA)
     a_part[1].wait()
     mlp(0, 2, NA)
-    o_chip[0].wait()
-    o_fwd[0].start()
+    wmo_in(0, 1, NA).wait()
+    mlp_rows(1, own_rows)
     wao_in(0).wait()
     for k in range(2):
         o_part[k].wait()
@@ -670,13 +684,21 @@
     a_fwd[0].wait()
     for t in range(NA):
         mlp(0, 3, t)
+    wmo_in(0, 3, NA).wait()
     a_fwd[1].wait()
-    mlp(0, 3, NA)
+    mlp_rows(3, own_rows)
     wmo_start(1, 2)
     wmo_start(1, 3)
     wao_in(1).start()
+    a_chip[1].wait()
+    a_fwd[2].start()
+    mlp_rows(1, peer_rows)
+    z_y(0, *blocks[0]).start()
+    o_chip[0].wait()
+    o_fwd[0].start()
     mlp(1, 0, 0, init=True)
-    z_y(0, *blocks[0]).start()
+    a_fwd[2].wait()
+    mlp_rows(3, peer_rows)
     o_chip[1].wait()
     o_fwd[1].start()
     attn_rows(0, *blocks[1])
@@ -711,21 +733,21 @@
         in_specs=[anyspec] * 9,
         out_specs=vspec,
         scratch_shapes=[
-            pltpu.VMEM((16, 4096), bf16),
-            pltpu.VMEM((16, 4096), bf16),
-            pltpu.VMEM((16, 4096), bf16),
+            pltpu.VMEM((SUB, 4096), bf16),
+            pltpu.VMEM((SUB, 4096), bf16),
+            pltpu.VMEM((SUB, 4096), bf16),
             pltpu.VMEM((ROWS, LOC), bf16),
             pltpu.VMEM((2, ROWS, TILE), f32),
             pltpu.VMEM((2, ROWS, TILE), f32),
-            pltpu.VMEM((2, 2048, LOC), bf16),
-            pltpu.VMEM((2, 16, TILE, LOC), bf16),
+            pltpu.VMEM((2, WIDE, LOC), bf16),
+            pltpu.VMEM((2, SUB, TILE, LOC), bf16),
             pltpu.VMEM((4, 4, ROWS, TILE), bf16),
-            pltpu.VMEM((8, 16, 2048), bf16),
+            pltpu.VMEM((8, SUB, WIDE), bf16),
             pltpu.VMEM((ROWS, LOC), f32),
             pltpu.VMEM((ROWS, LOC), f32),
             pltpu.VMEM((ROWS, LOC), f32),
-            two, dma, dma, dma, two, two, dma((2, 16)),
-            two, two, two, two, dma, dma,
+            two, dma, dma, dma, two, two, dma((2, SUB)),
+            two, two, dma((3,)), dma((3,)), two, two,
             dma, dma, two, two, two, two, two, two, dma((3,)), dma((3,)),
         ],
         compiler_params=pltpu.CompilerParams(
@@ -752,7 +774,7 @@
         rb = lax.ppermute(sb, "x", swap)
         a_own, a_tall = act(d, r0, ra)
         a_chip = lax.ppermute(a_own, "x", swap)
-        k_all, v_all, o2 = attend(SPLIT, 16, lens, qkv, kc_loc, vc_loc, k_all, v_all)
+        k_all, v_all, o2 = attend(SPLIT, SUB, lens, qkv, kc_loc, vc_loc, k_all, v_all)
         y_loc = out_proj(o1, o2, x_tall, d, rb, a_tall, a_chip, wao_loc, wmo_loc)
         return y_loc, k_all, v_all
 

time: 96.4 us -> 95.8 us (level)
  transfers between devices with their start and end apart: 3 -> 3, of which waited for: 1 -> 1; matrix products, arithmetic and copies ran while one was open for 0% -> 0% of each run, Pallas kernels for 49% -> 50%
where the time goes in v7:
time: 95.8 us; the launch traced here: 95.7 us
  Pallas kernels  90.8 us (95%)
  starting transfers between devices  2.64 us (3%)
    pallas_call x2, Pallas kernels, attend(): pl.pallas_call(functools.partial(attend_kernel, lo, hi), out_shape=[jax.S...  46.5 us
    pallas_call x1, Pallas kernels, in_proj(): pl.pallas_call(in_proj_kernel, out_shape=[jax.ShapeDtypeStruct((TALL // (...  27.4 us
    pallas_call x1, Pallas kernels, out_proj(): pl.pallas_call(out_proj_kernel, out_shape=jax.ShapeDtypeStruct((ROWS, LOC...  15.7 us
  transfers between devices with their start and end apart: 3, of which 1 were waited for; matrix products, arithmetic and copies ran while one was open for 0% of the time, Pallas kernels for 50%

profile of v7, /device:TPU:0, one launch (start us, length us, event | category | flops | bytes accessed | tf_op | source)
XLA Modules:
  0.0 95.7 jit_solution(9975919536077062174)
XLA Ops:
  0.6 27.4 %in_proj.1 = (bf16[227,16,2304]{2,1,0:T(8,128)(2,1)}, f32[5,128,512]{2,1,0:T(8,128)}, f32[2,128,512]{2,1,0:T(8,128)}, f32[1,128,512]{2,1,0:T(8,128)}, f32[8,128,...) custom-call(bf16[128,512]{1,0:T(8,128)(2,1)} %x_hbm.1, bf16[512]{0:T(512)(128)(2,1)} %g_hbm.1, ...), custom_call_target="tpu_custom_call" | custom-call | flops 5000000000 | bytes 45000000 | tf_op jit(solution)/shard_map/in_proj/pallas_call | solution.py:298
  28.1 0.6 collective-permute-start.1
  28.7 0.0 copy-start
  28.7 0.0 copy-start.1
  28.7 28.8 %attend0.1 = (bf16[16,4096,256]{2,1,0:T(8,128)(2,1)}, bf16[16,4096,256]{2,1,0:T(8,128)(2,1)}, bf16[2048,4096]{1,0:T(8,128)(2,1)}) custom-call(s32[65536,128]{1,0:T(8,128)} %get-tuple-element.21.len_hbm, bf16[227,16,2304]{2,1,0:T(8,128)(2,1)} %get-tuple-element.22.qkv_hbm, bf16[16,4096,256]{2,1,0:T(8,128)(2,1)} %k_ref.3, bf16[16,4096,256]{2,1,0:T(8,128)(2,1)} %v_ref.3), custom_call_target="tpu_custom_call" | custom-call | flops 24999999488 | bytes 84000000 | tf_op jit(solution)/shard_map/attend0/pallas_call | solution.py:454
  57.5 1.5 %collective-permute-start = (f32[2,128,512]{2,1,0:T(8,128)}, f32[2,128,512]{2,1,0:T(8,128)}, u32[]{:S(2)}, u32[]{:S(2)}) collective-permute-start(f32[2,128,512]{2,1,0:T(8,128)} %get-tuple-element.30), channel_id=1, source_target_pairs={{0,2},{2,0},{1,3},{3,1},{4,6},{6,4},{5,7},{7,5}} | collective-permute-start | bytes 1572872 | tf_op jit(solution)/shard_map/ppermute | solution.py:774
  59.0 0.0 collective-permute-done.1.r_ref
  59.0 0.0 copy-done
  59.0 0.0 copy-done.1
  59.0 1.1 %act.1 = (bf16[3,128,512]{2,1,0:T(8,128)(2,1)}, bf16[128,128,512]{2,1,0:T(8,128)(2,1)}) custom-call(f32[8,128,512]{2,1,0:T(8,128)S(1)} %copy-done, f32[1,128,512]{2,1,0:T(8,128)S(1)} %copy-done.1, f32[5,128,512]{2,1,0:T(8,128)S(1)} %collective-permute-done.1.r_ref), custom_call_target="tpu_custom_call" | custom-call | flops 5000000 | bytes 4000000 | tf_op jit(solution)/shard_map/act/pallas_call | solution.py:510
  60.1 0.6 collective-permute-start.2
  60.7 17.7 %attend10.1 = (bf16[16,4096,256]{2,1,0:T(8,128)(2,1)}, bf16[16,4096,256]{2,1,0:T(8,128)(2,1)}, bf16[2048,4096]{1,0:T(8,128)(2,1)}) custom-call(s32[65536,128]{1,0:T(8,128)} %get-tuple-element.21.len_hbm, bf16[227,16,2304]{2,1,0:T(8,128)(2,1)} %get-tuple-element.22.qkv_hbm, ...), custom_call_target="tpu_custom_call", output_to_operand_aliasing={{0}: (4, {}), {1}: (5, {})} | custom-call | flops 15000000512 | bytes 50400000 | tf_op jit(solution)/shard_map/attend10/pallas_call | solution.py:454
  78.4 0.0 collective-permute-done.r_ref
  78.4 0.9 collective-permute-done.2.ax_ref
  79.3 15.7 %out_proj.1 = bf16[128,512]{1,0:T(8,128)(2,1)S(1)} custom-call(bf16[2048,4096]{1,0:T(8,128)(2,1)} %get-tuple-element.24.o1_hbm, bf16[2048,4096]{1,0:T(8,128)(2,1)} %get-tuple-element.27.o2_hbm, bf16[16384,512]{1,0:T(8,128)(2,1)} %get-tuple-element.28.x_hbm, f32[8,128,512]{2,1,0:T(8,128)} %get-tuple-element.29.d_ref, ...), custom_call_target="tpu_custom_call" | custom-call | flops 3000000000 | bytes 26000000 | tf_op jit(solution)/shard_map/out_proj/pallas_call | solution.py:730
  95.0 0.7 copy.18
Async XLA Ops:
  28.1 30.9 %collective-permute-start.1 = (f32[5,128,512]{2,1,0:T(8,128)}, f32[5,128,512]{2,1,0:T(8,128)S(1)}, u32[]{:S(2)}, u32[]{:S(2)}) collective-permute-start(f32[5,128,512]{2,1,0:T(8,128)} %get-tuple-element.32), channel_id=1, source_target_pairs={{0,2},{2,0},{1,3},{3,1},{4,6},{6,4},{5,7},{7,5}} | collective-permute-start | bytes 3932168 | tf_op jit(solution)/shard_map/ppermute | solution.py:771
  28.7 30.3 %copy-start = (f32[8,128,512]{2,1,0:T(8,128)S(1)}, f32[8,128,512]{2,1,0:T(8,128)}, u32[]{:S(2)}) copy-start(f32[8,128,512]{2,1,0:T(8,128)} %get-tuple-element.29.d_ref) | copy-start | bytes 6291460
  28.7 30.3 %copy-start.1 = (f32[1,128,512]{2,1,0:T(8,128)S(1)}, f32[1,128,512]{2,1,0:T(8,128)}, u32[]{:S(2)}) copy-start(f32[1,128,512]{2,1,0:T(8,128)} %get-tuple-element.31.r0_ref) | copy-start | bytes 786436
  57.5 20.9 %collective-permute-start = (f32[2,128,512]{2,1,0:T(8,128)}, f32[2,128,512]{2,1,0:T(8,128)}, u32[]{:S(2)}, u32[]{:S(2)}) collective-permute-start(f32[2,128,512]{2,1,0:T(8,128)} %get-tuple-element.30), channel_id=1, source_target_pairs={{0,2},{2,0},{1,3},{3,1},{4,6},{6,4},{5,7},{7,5}} | collective-permute-start | bytes 1572872 | tf_op jit(solution)/shard_map/ppermute | solution.py:774
  60.1 19.2 %collective-permute-start.2 = (bf16[3,128,512]{2,1,0:T(8,128)(2,1)}, bf16[3,128,512]{2,1,0:T(8,128)(2,1)}, u32[]{:S(2)}, u32[]{:S(2)}) collective-permute-start(bf16[3,128,512]{2,1,0:T(8,128)(2,1)} %get-tuple-element.34), channel_id=1, source_target_pairs={{0,2},{2,0},{1,3},{3,1},{4,6},{6,4},{5,7},{7,5}} | collective-permute-start | bytes 1179656 | tf_op jit(solution)/shard_map/ppermute | solution.py:776

commit v8 on v7

--- a/solution.py
+++ b/solution.py
@@ -22,8 +22,8 @@
 SA = 5
 SPLIT = 10
 NT = 8
-QC = 768
-NQ = 3
+QC = 384
+NQ = 6
 W_FIRST = 8
 W_AHEAD = 12
 
@@ -184,18 +184,18 @@
         rows = jnp.where(row == r, len_s[r], rows)
     lens[...] = rows
 
-    q_compute(0)
-    q_compute(1)
-    q_pair_start(0)
-    q_compute(2)
-    q_pair_start(1)
+    for j in range(NQ):
+        q_compute(j)
+        if j:
+            q_pair_start(j - 1)
+    q_sum(0)
 
     after = {
-        0: lambda: q_pair_start(2),
-        1: lambda: q_sum(0),
-        2: lambda: (q_chip(0).start(), q_sum(1)),
-        3: lambda: (q_chip(1).start(), q_sum(2)),
-        4: lambda: q_chip(2).start(),
+        0: lambda: (q_pair_start(NQ - 1), q_chip(0).start(), q_sum(1)),
+        1: lambda: (q_chip(1).start(), q_sum(2), q_sum(3)),
+        2: lambda: (q_chip(2).start(), q_chip(3).start(), q_sum(4)),
+        3: lambda: (q_chip(4).start(), q_sum(5)),
+        4: lambda: q_chip(5).start(),
     }
     for i in range(NT):
         sbuf[i] = tile(i)
@@ -260,18 +260,21 @@
         lax.fori_loop(lo, hi, body, 0)
 
     send_tiles(0, 3)
-    q_final(0)
+    for j in range(3):
+        q_final(j)
     send_tiles(3, 4)
-    q_y(0).start()
+    for j in range(3):
+        q_y(j).start()
     send_tiles(4, 8)
+    q_final(3)
+    q_final(4)
     keep_tiles(0, 2)
-    q_final(1)
+    q_y(3).start()
+    q_y(4).start()
+    q_final(5)
     keep_tiles(2, 3)
-    q_y(1).start()
-    keep_tiles(3, 7)
-    q_final(2)
-    keep_tiles(7, 8)
-    q_y(2).start()
+    q_y(5).start()
+    keep_tiles(3, 8)
     d_out(NT - 1).start()
     for j in range(NQ):
         q_y(j).wait()

time: 95.8 us -> 95 us (level)
  Pallas kernels: 90.8 us -> 89.6 us
    pallas_call x1, Pallas kernels: 27.4 us -> 26.3 us  [in_proj(): pl.pallas_call(in_proj_kernel, out_shape=[jax.ShapeDtypeStruct((TALL // (...]
where the time goes in v8:
time: 95 us; the launch traced here: 94.9 us
  Pallas kernels  89.6 us (94%)
  starting transfers between devices  3.32 us (3%)
    pallas_call x2, Pallas kernels, attend(): pl.pallas_call(functools.partial(attend_kernel, lo, hi), out_shape=[jax.S...  46.5 us
    pallas_call x1, Pallas kernels, in_proj(): pl.pallas_call(in_proj_kernel, out_shape=[jax.ShapeDtypeStruct((TALL // (...  26.3 us
    pallas_call x1, Pallas kernels, out_proj(): pl.pallas_call(out_proj_kernel, out_shape=jax.ShapeDtypeStruct((ROWS, LOC...  15.7 us
  transfers between devices with their start and end apart: 3, of which 1 were waited for; matrix products, arithmetic and copies ran while one was open for 0% of the time, Pallas kernels for 50%

profile of v8, /device:TPU:0, one launch (start us, length us, event | category | flops | bytes accessed | tf_op | source)
XLA Modules:
  0.0 94.9 jit_solution(4553156756972011079)
XLA Ops:
  0.6 26.3 %in_proj.1 = (bf16[227,16,2304]{2,1,0:T(8,128)(2,1)}, f32[5,128,512]{2,1,0:T(8,128)}, f32[2,128,512]{2,1,0:T(8,128)}, f32[1,128,512]{2,1,0:T(8,128)}, f32[8,128,...) custom-call(bf16[128,512]{1,0:T(8,128)(2,1)} %x_hbm.1, bf16[512]{0:T(512)(128)(2,1)} %g_hbm.1, ...), custom_call_target="tpu_custom_call" | custom-call | flops 5000000000 | bytes 45000000 | tf_op jit(solution)/shard_map/in_proj/pallas_call | solution.py:301
  26.9 1.3 %collective-permute-start.1 = (f32[5,128,512]{2,1,0:T(8,128)}, f32[5,128,512]{2,1,0:T(8,128)S(1)}, u32[]{:S(2)}, u32[]{:S(2)}) collective-permute-start(f32[5,128,512]{2,1,0:T(8,128)} %get-tuple-element.32), channel_id=1, source_target_pairs={{0,2},{2,0},{1,3},{3,1},{4,6},{6,4},{5,7},{7,5}} | collective-permute-start | bytes 3932168 | tf_op jit(solution)/shard_map/ppermute | solution.py:774
  28.2 0.0 copy-start
  28.2 0.0 copy-start.1
  28.2 28.8 %attend0.1 = (bf16[16,4096,256]{2,1,0:T(8,128)(2,1)}, bf16[16,4096,256]{2,1,0:T(8,128)(2,1)}, bf16[2048,4096]{1,0:T(8,128)(2,1)}) custom-call(s32[65536,128]{1,0:T(8,128)} %get-tuple-element.21.len_hbm, bf16[227,16,2304]{2,1,0:T(8,128)(2,1)} %get-tuple-element.22.qkv_hbm, bf16[16,4096,256]{2,1,0:T(8,128)(2,1)} %k_ref.3, bf16[16,4096,256]{2,1,0:T(8,128)(2,1)} %v_ref.3), custom_call_target="tpu_custom_call" | custom-call | flops 24999999488 | bytes 84000000 | tf_op jit(solution)/shard_map/attend0/pallas_call | solution.py:457
  57.0 0.8 collective-permute-start
  57.8 0.0 collective-permute-done.1.r_ref
  57.8 0.0 copy-done
  57.8 0.0 copy-done.1
  57.8 1.1 %act.1 = (bf16[3,128,512]{2,1,0:T(8,128)(2,1)}, bf16[128,128,512]{2,1,0:T(8,128)(2,1)}) custom-call(f32[8,128,512]{2,1,0:T(8,128)S(1)} %copy-done, f32[1,128,512]{2,1,0:T(8,128)S(1)} %copy-done.1, f32[5,128,512]{2,1,0:T(8,128)S(1)} %collective-permute-done.1.r_ref), custom_call_target="tpu_custom_call" | custom-call | flops 5000000 | bytes 4000000 | tf_op jit(solution)/shard_map/act/pallas_call | solution.py:513
  59.0 1.3 %collective-permute-start.2 = (bf16[3,128,512]{2,1,0:T(8,128)(2,1)}, bf16[3,128,512]{2,1,0:T(8,128)(2,1)}, u32[]{:S(2)}, u32[]{:S(2)}) collective-permute-start(bf16[3,128,512]{2,1,0:T(8,128)(2,1)} %get-tuple-element.34), channel_id=1, source_target_pairs={{0,2},{2,0},{1,3},{3,1},{4,6},{6,4},{5,7},{7,5}} | collective-permute-start | bytes 1179656 | tf_op jit(solution)/shard_map/ppermute | solution.py:779
  60.2 17.7 %attend10.1 = (bf16[16,4096,256]{2,1,0:T(8,128)(2,1)}, bf16[16,4096,256]{2,1,0:T(8,128)(2,1)}, bf16[2048,4096]{1,0:T(8,128)(2,1)}) custom-call(s32[65536,128]{1,0:T(8,128)} %get-tuple-element.21.len_hbm, bf16[227,16,2304]{2,1,0:T(8,128)(2,1)} %get-tuple-element.22.qkv_hbm, ...), custom_call_target="tpu_custom_call", output_to_operand_aliasing={{0}: (4, {}), {1}: (5, {})} | custom-call | flops 15000000512 | bytes 50400000 | tf_op jit(solution)/shard_map/attend10/pallas_call | solution.py:457
  77.9 0.0 collective-permute-done.r_ref
  78.0 0.6 collective-permute-done.2.ax_ref
  78.6 15.7 %out_proj.1 = bf16[128,512]{1,0:T(8,128)(2,1)S(1)} custom-call(bf16[2048,4096]{1,0:T(8,128)(2,1)} %get-tuple-element.24.o1_hbm, bf16[2048,4096]{1,0:T(8,128)(2,1)} %get-tuple-element.27.o2_hbm, bf16[16384,512]{1,0:T(8,128)(2,1)} %get-tuple-element.28.x_hbm, f32[8,128,512]{2,1,0:T(8,128)} %get-tuple-element.29.d_ref, ...), custom_call_target="tpu_custom_call" | custom-call | flops 3000000000 | bytes 26000000 | tf_op jit(solution)/shard_map/out_proj/pallas_call | solution.py:733
  94.2 0.7 copy.18
Async XLA Ops:
  26.9 30.9 %collective-permute-start.1 = (f32[5,128,512]{2,1,0:T(8,128)}, f32[5,128,512]{2,1,0:T(8,128)S(1)}, u32[]{:S(2)}, u32[]{:S(2)}) collective-permute-start(f32[5,128,512]{2,1,0:T(8,128)} %get-tuple-element.32), channel_id=1, source_target_pairs={{0,2},{2,0},{1,3},{3,1},{4,6},{6,4},{5,7},{7,5}} | collective-permute-start | bytes 3932168 | tf_op jit(solution)/shard_map/ppermute | solution.py:774
  28.2 29.6 %copy-start = (f32[8,128,512]{2,1,0:T(8,128)S(1)}, f32[8,128,512]{2,1,0:T(8,128)}, u32[]{:S(2)}) copy-start(f32[8,128,512]{2,1,0:T(8,128)} %get-tuple-element.29.d_ref) | copy-start | bytes 6291460
  28.2 29.6 %copy-start.1 = (f32[1,128,512]{2,1,0:T(8,128)S(1)}, f32[1,128,512]{2,1,0:T(8,128)}, u32[]{:S(2)}) copy-start(f32[1,128,512]{2,1,0:T(8,128)} %get-tuple-element.31.r0_ref) | copy-start | bytes 786436
  57.0 20.9 %collective-permute-start = (f32[2,128,512]{2,1,0:T(8,128)}, f32[2,128,512]{2,1,0:T(8,128)}, u32[]{:S(2)}, u32[]{:S(2)}) collective-permute-start(f32[2,128,512]{2,1,0:T(8,128)} %get-tuple-element.30), channel_id=1, source_target_pairs={{0,2},{2,0},{1,3},{3,1},{4,6},{6,4},{5,7},{7,5}} | collective-permute-start | bytes 1572872 | tf_op jit(solution)/shard_map/ppermute | solution.py:777
  59.0 19.6 %collective-permute-start.2 = (bf16[3,128,512]{2,1,0:T(8,128)(2,1)}, bf16[3,128,512]{2,1,0:T(8,128)(2,1)}, u32[]{:S(2)}, u32[]{:S(2)}) collective-permute-start(bf16[3,128,512]{2,1,0:T(8,128)(2,1)} %get-tuple-element.34), channel_id=1, source_target_pairs={{0,2},{2,0},{1,3},{3,1},{4,6},{6,4},{5,7},{7,5}} | collective-permute-start | bytes 1179656 | tf_op jit(solution)/shard_map/ppermute | solution.py:779

commit v9 on v8

--- a/solution.py
+++ b/solution.py
@@ -553,14 +553,14 @@
     first = pl.ds(0, NA)
     own_in = local_copy(ao_ref.at[first], ab.at[x, first], asem.at[0])
     chip_in = local_copy(ax_ref, ab.at[x_chip, first], asem.at[1])
-    own_in.start()
-    chip_in.start()
     loads = [local_copy(d_ref.at[pl.ds(2 * NA, 2)], db, dsem), local_copy(r_ref, rb, rsem)]
     for c in loads:
         c.start()
     for c in o_in:
         c.wait()
     x_in = local_copy(x_hbm.at[pl.ds(0, ROWS)], x_ref, xsem)
+    own_in.start()
+    chip_in.start()
     x_in.start()
 
     order = (x, x_chip, x_core, x_diag)
@@ -580,7 +580,6 @@
         for t in range(4):
             wmo_in(half, n, t).start()
 
-    wmo_start(0, 0)
     row = lax.broadcasted_iota(jnp.int32, (SUB, 4096), 0)
     o_ref[...] = jnp.where(row < SPLIT, o1_ref[...].astype(f32), o2_ref[...].astype(f32)).astype(bf16)
     own_half = pl.multiple_of(yz * WIDE, WIDE)
@@ -591,6 +590,7 @@
 
     for c in loads:
         c.wait()
+    wmo_start(0, 0)
     gate = (db[0] + rb[0]).astype(bf16).astype(f32)
     up = (db[1] + rb[1]).astype(bf16).astype(f32)
     ab[x, NA] = (jax.nn.silu(gate) * up).astype(bf16)

time: 95 us -> 94.9 us (level)
  no operation moved by 1% of the time
where the time goes in v9:
time: 94.9 us; the launch traced here: 94.7 us
  Pallas kernels  89.5 us (94%)
  starting transfers between devices  3.32 us (3%)
    pallas_call x2, Pallas kernels, attend(): pl.pallas_call(functools.partial(attend_kernel, lo, hi), out_shape=[jax.S...  46.5 us
    pallas_call x1, Pallas kernels, in_proj(): pl.pallas_call(in_proj_kernel, out_shape=[jax.ShapeDtypeStruct((TALL // (...  26.3 us
    pallas_call x1, Pallas kernels, out_proj(): pl.pallas_call(out_proj_kernel, out_shape=jax.ShapeDtypeStruct((ROWS, LOC...  15.5 us
  transfers between devices with their start and end apart: 3, of which 1 were waited for; matrix products, arithmetic and copies ran while one was open for 0% of the time, Pallas kernels for 50%

profile of v9, /device:TPU:0, one launch (start us, length us, event | category | flops | bytes accessed | tf_op | source)
XLA Modules:
  0.0 94.7 jit_solution(17677025206637328251)
XLA Ops:
  0.6 26.3 %in_proj.1 = (bf16[227,16,2304]{2,1,0:T(8,128)(2,1)}, f32[5,128,512]{2,1,0:T(8,128)}, f32[2,128,512]{2,1,0:T(8,128)}, f32[1,128,512]{2,1,0:T(8,128)}, f32[8,128,...) custom-call(bf16[128,512]{1,0:T(8,128)(2,1)} %x_hbm.1, bf16[512]{0:T(512)(128)(2,1)} %g_hbm.1, ...), custom_call_target="tpu_custom_call" | custom-call | flops 5000000000 | bytes 45000000 | tf_op jit(solution)/shard_map/in_proj/pallas_call | solution.py:301
  26.9 1.3 %collective-permute-start.1 = (f32[5,128,512]{2,1,0:T(8,128)}, f32[5,128,512]{2,1,0:T(8,128)S(1)}, u32[]{:S(2)}, u32[]{:S(2)}) collective-permute-start(f32[5,128,512]{2,1,0:T(8,128)} %get-tuple-element.32), channel_id=1, source_target_pairs={{0,2},{2,0},{1,3},{3,1},{4,6},{6,4},{5,7},{7,5}} | collective-permute-start | bytes 3932168 | tf_op jit(solution)/shard_map/ppermute | solution.py:774
  28.2 0.0 copy-start
  28.2 0.0 copy-start.1
  28.2 28.8 %attend0.1 = (bf16[16,4096,256]{2,1,0:T(8,128)(2,1)}, bf16[16,4096,256]{2,1,0:T(8,128)(2,1)}, bf16[2048,4096]{1,0:T(8,128)(2,1)}) custom-call(s32[65536,128]{1,0:T(8,128)} %get-tuple-element.21.len_hbm, bf16[227,16,2304]{2,1,0:T(8,128)(2,1)} %get-tuple-element.22.qkv_hbm, bf16[16,4096,256]{2,1,0:T(8,128)(2,1)} %k_ref.3, bf16[16,4096,256]{2,1,0:T(8,128)(2,1)} %v_ref.3), custom_call_target="tpu_custom_call" | custom-call | flops 24999999488 | bytes 84000000 | tf_op jit(solution)/shard_map/attend0/pallas_call | solution.py:457
  57.0 0.8 collective-permute-start
  57.8 0.0 collective-permute-done.1.r_ref
  57.8 0.0 copy-done
  57.8 0.0 copy-done.1
  57.8 1.1 %act.1 = (bf16[3,128,512]{2,1,0:T(8,128)(2,1)}, bf16[128,128,512]{2,1,0:T(8,128)(2,1)}) custom-call(f32[8,128,512]{2,1,0:T(8,128)S(1)} %copy-done, f32[1,128,512]{2,1,0:T(8,128)S(1)} %copy-done.1, f32[5,128,512]{2,1,0:T(8,128)S(1)} %collective-permute-done.1.r_ref), custom_call_target="tpu_custom_call" | custom-call | flops 5000000 | bytes 4000000 | tf_op jit(solution)/shard_map/act/pallas_call | solution.py:513
  59.0 1.3 %collective-permute-start.2 = (bf16[3,128,512]{2,1,0:T(8,128)(2,1)}, bf16[3,128,512]{2,1,0:T(8,128)(2,1)}, u32[]{:S(2)}, u32[]{:S(2)}) collective-permute-start(bf16[3,128,512]{2,1,0:T(8,128)(2,1)} %get-tuple-element.34), channel_id=1, source_target_pairs={{0,2},{2,0},{1,3},{3,1},{4,6},{6,4},{5,7},{7,5}} | collective-permute-start | bytes 1179656 | tf_op jit(solution)/shard_map/ppermute | solution.py:779
  60.2 17.7 %attend10.1 = (bf16[16,4096,256]{2,1,0:T(8,128)(2,1)}, bf16[16,4096,256]{2,1,0:T(8,128)(2,1)}, bf16[2048,4096]{1,0:T(8,128)(2,1)}) custom-call(s32[65536,128]{1,0:T(8,128)} %get-tuple-element.21.len_hbm, bf16[227,16,2304]{2,1,0:T(8,128)(2,1)} %get-tuple-element.22.qkv_hbm, ...), custom_call_target="tpu_custom_call", output_to_operand_aliasing={{0}: (4, {}), {1}: (5, {})} | custom-call | flops 15000000512 | bytes 50400000 | tf_op jit(solution)/shard_map/attend10/pallas_call | solution.py:457
  77.9 0.0 collective-permute-done.r_ref
  78.0 0.6 collective-permute-done.2.ax_ref
  78.6 15.5 %out_proj.1 = bf16[128,512]{1,0:T(8,128)(2,1)S(1)} custom-call(bf16[2048,4096]{1,0:T(8,128)(2,1)} %get-tuple-element.24.o1_hbm, bf16[2048,4096]{1,0:T(8,128)(2,1)} %get-tuple-element.27.o2_hbm, bf16[16384,512]{1,0:T(8,128)(2,1)} %get-tuple-element.28.x_hbm, f32[8,128,512]{2,1,0:T(8,128)} %get-tuple-element.29.d_ref, ...), custom_call_target="tpu_custom_call" | custom-call | flops 3000000000 | bytes 26000000 | tf_op jit(solution)/shard_map/out_proj/pallas_call | solution.py:733
  94.1 0.7 copy.18
Async XLA Ops:
  26.9 30.9 %collective-permute-start.1 = (f32[5,128,512]{2,1,0:T(8,128)}, f32[5,128,512]{2,1,0:T(8,128)S(1)}, u32[]{:S(2)}, u32[]{:S(2)}) collective-permute-start(f32[5,128,512]{2,1,0:T(8,128)} %get-tuple-element.32), channel_id=1, source_target_pairs={{0,2},{2,0},{1,3},{3,1},{4,6},{6,4},{5,7},{7,5}} | collective-permute-start | bytes 3932168 | tf_op jit(solution)/shard_map/ppermute | solution.py:774
  28.2 29.6 %copy-start = (f32[8,128,512]{2,1,0:T(8,128)S(1)}, f32[8,128,512]{2,1,0:T(8,128)}, u32[]{:S(2)}) copy-start(f32[8,128,512]{2,1,0:T(8,128)} %get-tuple-element.29.d_ref) | copy-start | bytes 6291460
  28.2 29.6 %copy-start.1 = (f32[1,128,512]{2,1,0:T(8,128)S(1)}, f32[1,128,512]{2,1,0:T(8,128)}, u32[]{:S(2)}) copy-start(f32[1,128,512]{2,1,0:T(8,128)} %get-tuple-element.31.r0_ref) | copy-start | bytes 786436
  57.0 20.9 %collective-permute-start = (f32[2,128,512]{2,1,0:T(8,128)}, f32[2,128,512]{2,1,0:T(8,128)}, u32[]{:S(2)}, u32[]{:S(2)}) collective-permute-start(f32[2,128,512]{2,1,0:T(8,128)} %get-tuple-element.30), channel_id=1, source_target_pairs={{0,2},{2,0},{1,3},{3,1},{4,6},{6,4},{5,7},{7,5}} | collective-permute-start | bytes 1572872 | tf_op jit(solution)/shard_map/ppermute | solution.py:777
  59.0 19.6 %collective-permute-start.2 = (bf16[3,128,512]{2,1,0:T(8,128)(2,1)}, bf16[3,128,512]{2,1,0:T(8,128)(2,1)}, u32[]{:S(2)}, u32[]{:S(2)}) collective-permute-start(bf16[3,128,512]{2,1,0:T(8,128)(2,1)} %get-tuple-element.34), channel_id=1, source_target_pairs={{0,2},{2,0},{1,3},{3,1},{4,6},{6,4},{5,7},{7,5}} | collective-permute-start | bytes 1179656 | tf_op jit(solution)/shard_map/ppermute | solution.py:779
